TPU v7x, 32 devices: a whole 2x2x4 slice. The times are simulated.
32 devices in a mesh: blk: 32 (over z, y, x, core).
Axes of the slice: x: 2, y: 2, z: 4, core: 2. Of those that a mesh axis runs over, the one named last changes fastest.
Arguments:
- fields: float32 [256, 4, 16, 256], P('blk'), may hold values from -1 to 2, as said below
- guidance: float32 [256, 4, 16, 256], P('blk'), may hold values from -6 to 6
- levels: int32 [256], P('blk'), may hold values from -1 to 2, as said below
- send_faces: int32 [32, 32, 6], P('blk'), may hold values from -1 to 7, as said below
- ghost_peer: int32 [256, 6, 4], P('blk'), may hold values from -1 to 31, as said below
- ghost_code: int32 [256, 6, 4], P('blk'), may hold values from 0 to 24, as said below
- child_send: int32 [32, 32], P('blk'), may hold values from -1 to 7, as said below
- parent_peer: int32 [256, 8], P('blk'), may hold values from -1 to 31, as said below
Outputs:
- final_fields: float32 [256, 4, 16, 256], P('blk')
- gradient: float32 [256, 4, 16, 256], P('blk')
Inputs may be any that keep to these rules, and one draw needn't show every extreme that they name: `fields`: channel 0 is a density between 0.5 and 2; channels 1 to 3 are that density times velocities of magnitude at most 0.5. `levels`: on each device the occupied slots come first and the rest are -1; a device has 8, 4, 2 or 1 occupied slots, device 0 all of them and device 1 an eighth. `send_faces`: entry [p, d, j] is an occupied local slot of device p, or -1 where p sends no face of type j to d; device (d + 1) mod 32 sends every face type to device d. `ghost_peer`: rows of empty slots are -1. For each occupied slot and face the entries in use come first: one, or four for a face next to finer blocks; each names a device p with send_faces[p, d, f xor 1] >= 0 for the slot's device d and face f; unused entries are -1. `ghost_code`: 0 for a single same-level entry and for unused entries; a and b in 1, 2 for a single entry from a coarser block; the four pairs of 3, 4 over the four entries of a face next to finer blocks. `child_send`: entry [c, d] is an occupied slot of device c that is not a covered parent, exactly where device d names c in parent_peer, else -1. `parent_peer`: A covered parent's row holds eight devices, and all devices named on one device are distinct; other rows are -1. Covered parents are the last occupied slots of a device, at most 4 of them and at most half of its occupied slots.
All inputs are finite; a program needn't handle non-finite values.
Results may differ from a plain program's by a relative error of at most 0.0003.
Values sent between devices are 32-bit elements; how exact they have to be, the bound alone decides.
No kernel may reach another device: no remote copies, remote signals or barrier semaphores. Data moves between devices by JAX's collectives and lax.ppermute only.
A program may use at most 128 MiB of HBM per device.

v0:
```python
import jax
import jax.numpy as jnp
from jax import lax
from jax.sharding import PartitionSpec as P

sound_speed = 1.0
base_ratio = 0.04
speed_floor = 0.01
highest = lax.Precision.HIGHEST


def make_tables(extent):
    half_size = extent // 2
    row_ids = jnp.arange(extent)[:, None]
    col_ids = jnp.arange(half_size)[None, :]
    placing = [(row_ids == offset * half_size + col_ids).astype(jnp.float32) for offset in range(2)]
    widen = (row_ids // 2 == col_ids).astype(jnp.float32)
    shrink = 0.5 * widen.T
    reduce_table = jnp.kron(shrink, shrink).T
    place_tables = jnp.stack(
        [jnp.kron(placing[first], placing[second]) for first in range(2) for second in range(2)]
    )
    widen_table = jnp.kron(widen, widen)
    return (reduce_table, place_tables, widen_table, shrink)


def rusanov(behind, beyond, normal_direction):

    def physical(values):
        velocity = values[1 + normal_direction] / values[0]
        momentum_flux = values[1:] * velocity
        momentum_flux = momentum_flux.at[normal_direction].add(
            sound_speed * sound_speed * values[0]
        )
        return (jnp.concatenate([values[1 + normal_direction][None], momentum_flux]), velocity)

    flux_behind, speed_behind = physical(behind)
    flux_beyond, speed_beyond = physical(beyond)
    wave_speed = sound_speed + jnp.sqrt(
        0.5 * (speed_behind * speed_behind + speed_beyond * speed_beyond) + speed_floor
    )
    return 0.5 * (flux_behind + flux_beyond) - 0.5 * wave_speed * (beyond - behind)


def face_layers(volume):
    extent = volume.shape[1]
    square = volume.shape[2]
    return jnp.stack(
        [
            volume[:, 0],
            volume[:, extent - 1],
            volume[:, :, 0:extent].reshape(4, square),
            volume[:, :, square - extent :].reshape(4, square),
            volume[:, :, 0::extent].reshape(4, square),
            volume[:, :, extent - 1 :: extent].reshape(4, square),
        ]
    )


def boundary_fluxes(layers, ghosts):
    stacked = []
    for surface in range(6):
        if surface % 2 == 0:
            stacked.append(rusanov(ghosts[surface], layers[surface], surface // 2))
        else:
            stacked.append(rusanov(layers[surface], ghosts[surface], surface // 2))
    return jnp.stack(stacked)


def interior_change(volume, step_ratio):
    extent = volume.shape[1]
    square = volume.shape[2]
    summed = jnp.zeros_like(volume)
    flux_x = rusanov(volume[:, : extent - 1], volume[:, 1:], 0)
    padded = jnp.pad(flux_x, ((0, 0), (1, 1), (0, 0)))
    summed = summed + (padded[:, 1 : extent + 1] - padded[:, 0:extent])
    flux_y = rusanov(volume[:, :, : square - extent], volume[:, :, extent:], 1)
    padded = jnp.pad(flux_y, ((0, 0), (0, 0), (extent, extent)))
    summed = summed + (padded[:, :, extent : square + extent] - padded[:, :, 0:square])
    flux_z = rusanov(volume[:, :, : square - 1], volume[:, :, 1:], 2)
    inside = (jnp.arange(square - 1) % extent != extent - 1)[None, None, :]
    flux_z = jnp.where(inside, flux_z, 0.0)
    padded = jnp.pad(flux_z, ((0, 0), (0, 0), (1, 1)))
    summed = summed + (padded[:, :, 1 : square + 1] - padded[:, :, 0:square])
    return -step_ratio * summed


def boundary_change(corrected, step_ratio, extent):
    square = extent * extent
    change = jnp.zeros((4, extent, square), corrected.dtype)
    change = change.at[:, 0].add(step_ratio * corrected[0])
    change = change.at[:, extent - 1].add(-step_ratio * corrected[1])
    change = change.at[:, :, 0:extent].add((step_ratio * corrected[2]).reshape(4, extent, extent))
    change = change.at[:, :, square - extent :].add(
        (-step_ratio * corrected[3]).reshape(4, extent, extent)
    )
    change = change.at[:, :, 0::extent].add((step_ratio * corrected[4]).reshape(4, extent, extent))
    change = change.at[:, :, extent - 1 :: extent].add(
        (-step_ratio * corrected[5]).reshape(4, extent, extent)
    )
    return change


def boundary_adjoint(cotangent, step_ratio):
    signs = jnp.array([1.0, -1.0, 1.0, -1.0, 1.0, -1.0], cotangent.dtype)[:, None, None]
    return face_layers(cotangent) * (step_ratio * signs)


def average_all(volumes, tables):
    reduce_table, place_tables, widen_table, shrink = tables
    slot_count, _, extent, square = volumes.shape
    half_size = extent // 2
    across = jnp.dot(volumes.reshape(-1, square), reduce_table, precision=highest).reshape(
        slot_count, 4, extent, half_size * half_size
    )
    coarse = jnp.einsum("ki,scim->sckm", shrink, across, precision=highest)
    return coarse.reshape(slot_count, 4, half_size * half_size * half_size)


def place_all(pieces, tables):
    reduce_table, place_tables, widen_table, shrink = tables
    slot_count = pieces.shape[0]
    square = place_tables.shape[1]
    quarter = place_tables.shape[2]
    half_size = pieces.shape[-1] // quarter
    extent = 2 * half_size
    shaped = pieces.reshape(slot_count, 2, 2, 2, 4, half_size, quarter)
    pairs = place_tables.reshape(2, 2, square, quarter)
    placed = jnp.einsum("soabcxm,abnm->socxn", shaped, pairs, precision=highest)
    return placed.transpose(0, 2, 1, 3, 4).reshape(slot_count, 4, extent, square)


def pack_faces(layers, send_row):
    flattened = layers.reshape(layers.shape[0] * 6, -1)
    row_ids = jnp.maximum(send_row, 0) * 6 + jnp.arange(6, dtype=jnp.int32)[None, :]
    present = (send_row >= 0).astype(flattened.dtype)[:, :, None]
    return flattened[row_ids] * present


def place_quarters(quarters, sources, op_codes, tables):
    place_tables = tables[1]
    active = sources >= 0
    code_list = jnp.array([18, 19, 23, 24], jnp.int32)
    weights = (active[..., None] & (op_codes[..., None] == code_list)).astype(quarters.dtype)
    grouped = jnp.einsum("sfej,sfecm->sfjcm", weights, quarters, precision=highest)
    return jnp.einsum("sfjcm,jnm->sfcn", grouped, place_tables, precision=highest)


def remap_faces(picked, sources, op_codes, tables):
    reduce_table, place_tables, widen_table, shrink = tables
    slot_count = picked.shape[0]
    square = picked.shape[-1]
    quarter = reduce_table.shape[1]
    active = sources >= 0
    same = (active & (op_codes == 0)).astype(picked.dtype)[:, :, :, None, None]
    result = jnp.sum(picked * same, axis=2)
    quarters = jnp.dot(picked.reshape(-1, square), reduce_table, precision=highest).reshape(
        slot_count, 6, 4, 4, quarter
    )
    result = result + place_quarters(quarters, sources, op_codes, tables)
    first = picked[:, :, 0]
    selector = place_tables.transpose(1, 0, 2).reshape(square, 4 * quarter)
    chosen = jnp.dot(first.reshape(-1, square), selector, precision=highest).reshape(
        slot_count, 6, 4, 4, quarter
    )
    coarse_list = jnp.array([6, 7, 11, 12], jnp.int32)
    weights = (active[:, :, 0, None] & (op_codes[:, :, 0, None] == coarse_list)).astype(
        picked.dtype
    )
    coarse_part = jnp.sum(chosen * weights[:, :, None, :, None], axis=3)
    widened = jnp.dot(coarse_part.reshape(-1, quarter), widen_table.T, precision=highest).reshape(
        slot_count, 6, 4, square
    )
    return result + widened


def assemble(received, sources, op_codes, tables):
    square = tables[0].shape[0]
    opposite = (jnp.arange(6, dtype=jnp.int32) ^ 1)[None, :, None]
    row_ids = jnp.maximum(sources, 0) * 6 + opposite
    picked = received.reshape(-1, 4, square)[row_ids]
    return remap_faces(picked, sources, op_codes, tables)


def on_device(
    fields, guidance, levels, send_faces, ghost_peer, ghost_code, child_send, parent_peer
):
    slot_count = fields.shape[0]
    extent = fields.shape[2]
    square = fields.shape[3]
    half_size = extent // 2
    quarter = half_size * half_size
    eighth = quarter * half_size
    peer_count = send_faces.shape[1]
    tables = make_tables(extent)
    send_row = send_faces[0]
    child_row = child_send[0]
    occupied = levels >= 0
    occupied_mask = occupied[:, None, None, None]
    live_count = jnp.sum(occupied.astype(jnp.int32))
    live_mask = occupied.astype(fields.dtype)[:, None, None, None]
    degree = levels.astype(fields.dtype)
    step_ratio = base_ratio * (1.0 + degree + 0.5 * degree * (degree - 1.0))
    covered = (parent_peer[:, 0] >= 0)[:, None, None, None]
    refined = (ghost_peer[:, :, 1] >= 0)[:, :, None, None]
    parent_rows = jnp.maximum(parent_peer, 0)
    child_rows = jnp.maximum(child_row, 0)
    child_present = (child_row >= 0).astype(fields.dtype)[:, None, None]

    def change_all(corrected):
        return jax.vmap(lambda edge_fluxes, factor: boundary_change(edge_fluxes, factor, extent))(
            corrected, step_ratio
        )

    def gather_layers(layers):
        received = lax.all_to_all(
            pack_faces(layers, send_row), "blk", split_axis=0, concat_axis=0, tiled=True
        )
        return jnp.where(occupied_mask, assemble(received, ghost_peer, ghost_code, tables), layers)

    def correct(fluxes):
        incoming_data = lax.all_to_all(
            pack_faces(fluxes, send_row), "blk", split_axis=0, concat_axis=0, tiled=True
        )
        gathered = assemble(incoming_data, ghost_peer, ghost_code, tables)
        return jnp.where(refined, gathered, fluxes)

    def interior_sweep(initial):

        def interior_process_block(number, result):
            volume = lax.dynamic_index_in_dim(initial, number, 0, keepdims=False)
            factor = lax.dynamic_index_in_dim(step_ratio, number, 0, keepdims=False)
            return lax.dynamic_update_index_in_dim(
                result, volume + interior_change(volume, factor), number, 0
            )

        return lax.fori_loop(0, live_count, interior_process_block, initial)

    def restrict(updated):
        coarse = average_all(updated, tables)
        incoming_data = lax.all_to_all(
            coarse[child_rows] * child_present, "blk", split_axis=0, concat_axis=0, tiled=True
        )
        pieces = incoming_data[parent_rows]
        return jnp.where(covered, place_all(pieces, tables), updated)

    def forward_step(initial):
        partial_sum = interior_sweep(initial)
        layers = jax.vmap(face_layers)(initial)
        ghosts = gather_layers(layers)
        corrected = correct(jax.vmap(boundary_fluxes)(layers, ghosts))
        updated = partial_sum + change_all(corrected) * live_mask
        return (restrict(updated), ghosts)

    def backward_step(initial, ghosts, cotangent):
        zero_pieces = jnp.zeros((slot_count, 8, 4, eighth), fields.dtype)
        pull_place = jax.vjp(lambda pieces: place_all(pieces, tables), zero_pieces)[1]
        octants = pull_place(cotangent)[0]
        owners = jnp.where(parent_peer >= 0, parent_peer, peer_count).reshape(-1)
        outgoing = jax.ops.segment_sum(
            octants.reshape(slot_count * 8, 4, eighth), owners, num_segments=peer_count + 1
        )[:peer_count]
        returned = lax.all_to_all(outgoing, "blk", split_axis=0, concat_axis=0, tiled=True)
        targets = jnp.where(child_row >= 0, child_row, slot_count)
        coarse_cot = jax.ops.segment_sum(returned, targets, num_segments=slot_count + 1)[
            :slot_count
        ]
        pull_average = jax.vjp(lambda volume_set: average_all(volume_set, tables), initial)[1]
        upward = jnp.where(covered, 0.0, cotangent) + pull_average(coarse_cot)[0]

        def backward_process_block(number, result):
            volume = lax.dynamic_index_in_dim(initial, number, 0, keepdims=False)
            factor = lax.dynamic_index_in_dim(step_ratio, number, 0, keepdims=False)
            weight = lax.dynamic_index_in_dim(upward, number, 0, keepdims=False)
            pulled = jax.vjp(lambda inner_volume: interior_change(inner_volume, factor), volume)[1](
                weight
            )[0]
            return lax.dynamic_update_index_in_dim(result, weight + pulled, number, 0)

        through = lax.fori_loop(0, live_count, backward_process_block, upward)
        corrected_cot = jax.vmap(boundary_adjoint)(upward, step_ratio) * live_mask
        layers = jax.vmap(face_layers)(initial)
        zero_packets = jnp.zeros((peer_count, 6, 4 * square), fields.dtype)
        pull_ghost = jax.vjp(
            lambda packets: assemble(packets, ghost_peer, ghost_code, tables), zero_packets
        )[1]
        pull_pack = jax.vjp(lambda face_data: pack_faces(face_data, send_row), layers)[1]
        kept_cot = jnp.where(refined, 0.0, corrected_cot)
        sent_back = jnp.where(refined, corrected_cot, 0.0)
        returned_flux = lax.all_to_all(
            pull_ghost(sent_back)[0], "blk", split_axis=0, concat_axis=0, tiled=True
        )
        flux_cot = kept_cot + pull_pack(returned_flux)[0]
        pull_bound = jax.vjp(jax.vmap(boundary_fluxes), layers, ghosts)[1]
        layer_cot, ghost_cot = pull_bound(flux_cot)
        ghost_cot = jnp.where(occupied_mask, ghost_cot, 0.0)
        ghost_back = lax.all_to_all(
            pull_ghost(ghost_cot)[0], "blk", split_axis=0, concat_axis=0, tiled=True
        )
        layer_cot = layer_cot + pull_pack(ghost_back)[0]
        pull_faces = jax.vjp(jax.vmap(face_layers), initial)[1]
        return through + pull_faces(layer_cot)[0]

    middle, ghosts_first = forward_step(fields)
    final_state, ghosts_second = forward_step(middle)
    inner_cot = backward_step(middle, ghosts_second, guidance)
    gradient = backward_step(fields, ghosts_first, inner_cot)
    return (final_state, gradient)


def solution(mesh):
    placed = (
        P("blk", None, None, None),
        P("blk", None, None, None),
        P("blk"),
        P("blk", None, None),
        P("blk", None, None),
        P("blk", None, None),
        P("blk", None),
        P("blk", None),
    )
    return jax.shard_map(
        on_device,
        mesh=mesh,
        in_specs=placed,
        out_specs=(P("blk", None, None, None), P("blk", None, None, None)),
        check_vma=False,
    )
```

profile of v0, /device:TPU:0, one launch (start us, length us, event | category | flops | bytes accessed | tf_op | source)
XLA Modules:
  0.0 709.2 jit_solution(17276552218853683882)
XLA Ops:
  4.2 3.2 scatter_fusion.4
  8.1 7.4 %all-to-all-start.6 = ((f32[32,4,512]{2,1,0:T(4,128)}), f32[32,4,512]{2,1,0:T(4,128)}, u32[]{:S(2)}, u32[]{:S(2)}) async-start(f32[32,4,512]{2,1,0:T(4,128)} %slice.3005), calls=%async_computation.6 | async-start | bytes 524288 | tf_op jit(solution)/shard_map/all_to_all | solution.py:263
  25.3 22.5 %while.98 = (s32[]{:T(128)}, f32[8,4,16,256]{3,2,1,0:T(8,128)S(1)}, s32[]{:T(128)}, f32[8,4,16,256]{3,2,1,0:T(8,128)S(1)}, f32[8]{0:T(128)S(1)}, /*index=5*/s32[]{:T(128)}, s32[]{:T(128)}, s32[]{:T(128)}) while((s32[]{:T(128)}, f32[8,4,16,256]{3,2,1,0:T(8,128)S(1)}, s32[]{:T(128)}, f32[8,4,16,256]{3,2,1,0:T(8,128)S(1)}, f32[8]{0:T(128)S(1)}, ...), condition=%wide.region_2.3_spmd, body=%wide.region_1.2_spmd.sunk | while | flops 685519 | bytes 2928725 | solution.py:237
  52.1 2.4 broadcast_multiply_fusion.13
  54.5 6.1 all-to-all-start
  60.6 3.3 scatter_fusion.5
  65.4 2.3 slice.2716
  67.7 2.4 slice.2717
  77.2 14.9 %scatter_fusion.6 = f32[192,4,256]{2,1,0:T(4,128)S(1)} fusion(f32[192,4,256]{2,1,0:T(4,128)S(1)} %broadcast.3112.clone, s32[192]{0:T(256)S(1)} %reshape.4233, f32[192,4,256]{2,1,0:T(4,128)} %bitcast.1671), kind=kCustom, calls=%fused_computation.18 | custom fusion | flops 196608 | bytes 2360064 | tf_op jit(solution)/shard_map/transpose(jvp())/scatter-add | solution.py:181
  93.6 6.3 all-to-all-start.7
  99.9 2.5 reshape.4156
  114.6 11.5 %all-to-all-done.7 = f32[32,6,1024]{2,1,0:T(8,128)} async-done(((f32[32,6,1024]{2,1,0:T(8,128)}), f32[32,6,1024]{2,1,0:T(8,128)}, u32[]{:S(2)}, u32[]{:S(2)}) %all-to-all-start.7) | async-done | bytes 786464 | tf_op jit(solution)/shard_map/all_to_all | solution.py:290
  126.1 3.1 broadcast_multiply_fusion.9
  129.2 3.8 all-to-all-start.1
  136.8 2.8 scatter_custom_fusion.7
  142.4 16.7 %all-to-all-done.1 = f32[32,6,1024]{2,1,0:T(8,128)} async-done(((f32[32,6,1024]{2,1,0:T(8,128)}), f32[32,6,1024]{2,1,0:T(8,128)}, u32[]{:S(2)}, u32[]{:S(2)}) %all-to-all-start.1) | async-done | bytes 786464 | tf_op jit(solution)/shard_map/all_to_all | solution.py:222
  159.1 2.5 reshape.4159
  174.4 10.2 %scatter-add.291 = f32[8,4,16,256]{3,0,1,2:T(8,128)S(1)} dynamic-update-slice(f32[8,4,16,256]{3,0,1,2:T(8,128)S(1)} %scatter-add.288, f32[8,4,16,16]{3,0,1,2:T(8,128)} %get-tuple-element.1578, s32[]{:T(128)} %constant.1638.clone.1, s32[]{:T(128)} %constant.1638.clone.1, s32[]{:T(128)} %constant.1638.clone.1, s32[]{:T(128)} %constant.1653.clone.1) | dynamic-update-slice | bytes 65540 | tf_op jit(solution)/shard_map/vmap()/scatter-add | solution.py:94
  184.6 2.8 copy.221
  188.0 2.4 scatter_fusion
  190.5 2.4 scatter_fusion.1
  192.9 3.0 copy.225
  200.2 3.8 all-to-all-start.2
  205.8 8.7 %all-to-all-done.2 = f32[32,4,512]{2,1,0:T(4,128)S(1)} async-done(((f32[32,4,512]{2,1,0:T(4,128)}), f32[32,4,512]{2,1,0:T(4,128)S(1)}, u32[]{:S(2)}, u32[]{:S(2)}) %all-to-all-start.2) | async-done | bytes 262176 | tf_op jit(solution)/shard_map/all_to_all | solution.py:241
  220.4 6.0 slice.2638
  226.4 2.4 slice.2639
  244.0 2.3 broadcast_multiply_fusion.11
  246.3 3.4 all-to-all-start.3
  249.7 46.3 %while.100 = (s32[]{:T(128)}, f32[8,4,16,256]{3,0,1,2:T(8,128)}, s32[]{:T(128)}, f32[8,4,16,256]{3,0,1,2:T(8,128)S(1)}, f32[8,4,16,256]{3,2,1,0:T(8,128)S(1)}, /...) while((s32[]{:T(128)}, f32[8,4,16,256]{3,0,1,2:T(8,128)}, s32[]{:T(128)}, ...), condition=%wide.region_29.30_spmd, body=%wide.region_19.29_spmd.sunk | while | flops 1689743 | bytes 6185057 | solution.py:280
  253.1 2.3 dynamic_update_slice.34
  258.8 2.3 dynamic_update_slice.34
  264.5 2.3 dynamic_update_slice.34
  296.7 2.5 reshape.4169
  325.0 14.9 %scatter_fusion.7 = f32[192,4,256]{2,1,0:T(4,128)S(1)} fusion(f32[192,4,256]{2,1,0:T(4,128)S(1)} %broadcast.3112.clone.2, s32[192]{0:T(256)S(1)} %reshape.4233, f32[192,4,256]{2,1,0:T(4,128)} %bitcast.1672), kind=kCustom, calls=%fused_computation.20 | custom fusion | flops 196608 | bytes 2360064 | tf_op jit(solution)/shard_map/transpose(jvp())/scatter-add | solution.py:181
  341.4 5.9 all-to-all-start.8
  347.3 30.8 %while.99 = (s32[]{:T(128)}, f32[8,4,16,256]{3,0,1,2:T(8,128)S(1)}, s32[]{:T(128)}, f32[8,4,16,256]{3,2,1,0:T(8,128)S(1)}, f32[8]{0:T(128)S(1)}, /*index=5*/s32[]{:T(128)}, s32[]{:T(128)}, s32[]{:T(128)}) while((s32[]{:T(128)}, f32[8,4,16,256]{3,0,1,2:T(8,128)S(1)}, s32[]{:T(128)}, f32[8,4,16,256]{3,2,1,0:T(8,128)S(1)}, f32[8]{0:T(128)S(1)}, ...), condition=%wide.region_10.11_spmd, body=%wide.region_9.10_spmd.sunk | while | flops 685519 | bytes 3182425 | solution.py:237
  382.5 2.8 scatter_custom_fusion.9
  387.9 22.7 %pad.1113 = f32[8,4,16,256]{3,0,1,2:T(8,128)} pad(f32[8,4,16,16]{3,0,1,2:T(8,128)S(1)} %copy.284, f32[]{:T(128)} %constant.1647.clone.1), padding=0_0_0x0_0_0x0_0_0x15_0_15 | pad | bytes 557060 | tf_op jit(solution)/shard_map/transpose(jvp(vmap()))/pad | solution.py:55
  410.5 22.6 %pad.1114 = f32[8,4,16,256]{3,0,1,2:T(8,128)} pad(f32[8,4,16,16]{3,0,1,2:T(8,128)S(1)} %copy.285, f32[]{:T(128)} %constant.1647.clone.1), padding=0_0_0x0_0_0x0_0_0x0_15_15 | pad | bytes 557060 | tf_op jit(solution)/shard_map/transpose(jvp(vmap()))/pad | solution.py:54
  437.3 2.4 reshape.4522
  439.7 6.0 scatter_fusion.8
  446.4 5.7 all-to-all-start.9
  459.8 2.9 all-to-all-done.9
  469.6 2.4 slice.2725
  483.4 14.9 %scatter_fusion.10 = f32[192,4,256]{2,1,0:T(4,128)S(1)} fusion(f32[192,4,256]{2,1,0:T(4,128)S(1)} %broadcast.3112.clone.1, s32[192]{0:T(256)S(1)} %reshape.4233, f32[192,4,256]{2,1,0:T(4,128)} %bitcast.1673), kind=kCustom, calls=%fused_computation.24 | custom fusion | flops 196608 | bytes 2360064 | tf_op jit(solution)/shard_map/transpose(jvp())/scatter-add | solution.py:181
  499.8 3.5 all-to-all-start.10
  512.5 17.0 %all-to-all-done.10 = f32[32,6,1024]{2,1,0:T(8,128)} async-done(((f32[32,6,1024]{2,1,0:T(8,128)}), f32[32,6,1024]{2,1,0:T(8,128)}, u32[]{:S(2)}, u32[]{:S(2)}) %all-to-all-start.10) | async-done | bytes 786464 | tf_op jit(solution)/shard_map/all_to_all | solution.py:290
  529.5 2.3 broadcast_multiply_fusion.7
  534.1 2.9 scatter_custom_fusion.13
  559.0 14.9 %scatter_fusion.11 = f32[192,4,256]{2,1,0:T(4,128)S(1)} fusion(f32[192,4,256]{2,1,0:T(4,128)S(1)} %broadcast.3112, s32[192]{0:T(256)S(1)} %reshape.4233, f32[192,4,256]{2,1,0:T(4,128)} %bitcast.1670), kind=kCustom, calls=%fused_computation.26 | custom fusion | flops 196608 | bytes 2360064 | tf_op jit(solution)/shard_map/transpose(jvp())/scatter-add | solution.py:181
  575.4 3.7 all-to-all-start.11
  586.9 18.3 %all-to-all-done.11 = f32[32,6,1024]{2,1,0:T(8,128)} async-done(((f32[32,6,1024]{2,1,0:T(8,128)}), f32[32,6,1024]{2,1,0:T(8,128)}, u32[]{:S(2)}, u32[]{:S(2)}) %all-to-all-start.11) | async-done | bytes 786464 | tf_op jit(solution)/shard_map/all_to_all | solution.py:297
  605.3 3.1 broadcast_multiply_fusion.6
  608.4 3.7 all-to-all-start.4
  612.2 34.3 %while.101 = (s32[]{:T(128)}, f32[8,4,16,256]{3,0,1,2:T(8,128)S(1)}, s32[]{:T(128)}, f32[8,4,16,256]{3,0,1,2:T(8,128)S(1)}, f32[8,4,16,256]{3,2,1,0:T(8,128)S(1)...) while((s32[]{:T(128)}, f32[8,4,16,256]{3,0,1,2:T(8,128)S(1)}, s32[]{:T(128)}, ...), condition=%wide.region_64.65_spmd, body=%wide.region_54.64_spmd.sunk | while | flops 1689743 | bytes 6185057 | solution.py:280
  648.1 2.5 scatter_custom_fusion.15
  659.9 9.4 %scatter-add.327 = f32[8,4,16,256]{3,0,1,2:T(8,128)S(1)} dynamic-update-slice(f32[8,4,16,256]{3,0,1,2:T(8,128)S(1)} %scatter-add.324, f32[8,4,16,16]{3,0,1,2:T(8,128)S(1)} %get-tuple-element.1570, s32[]{:T(128)} %constant.1638.clone.1, s32[]{:T(128)} %constant.1638.clone.1, s32[]{:T(128)} %constant.1638.clone.1, s32[]{:T(128)} %constant.1653.clone.1) | dynamic-update-slice | bytes 65540 | tf_op jit(solution)/shard_map/vmap()/scatter-add | solution.py:94
  669.2 2.8 copy.252
  672.7 2.4 scatter_fusion.2
  675.1 2.4 scatter_fusion.3
  677.6 3.0 copy.256
  683.6 6.0 all-to-all-start.5
  691.9 5.4 pad.1181
  697.4 5.4 pad.1182
  (1664 shorter events, 295.2 us)
Async XLA Ops:
  8.1 46.4 %all-to-all-start.6 = ((f32[32,4,512]{2,1,0:T(4,128)}), f32[32,4,512]{2,1,0:T(4,128)}, u32[]{:S(2)}, u32[]{:S(2)}) async-start(f32[32,4,512]{2,1,0:T(4,128)} %slice.3005), calls=%async_computation.6 | async-start | bytes 524288 | tf_op jit(solution)/shard_map/all_to_all | solution.py:263
  19.4 44.6 %copy-start.157 = (s32[16]{0:T(128)}, s32[16]{0:T(128)S(1)}, u32[]{:S(2)}) copy-start(s32[16]{0:T(128)S(1)} %and_select_fusion.4) | copy-start | bytes 196
  20.5 43.9 %copy-start.15 = (f32[64,256,1,1]{1,0,2,3:T(8,128)}, f32[64,256,1,1]{1,0,2,3:T(8,128)S(1)}, u32[]{:S(2)}) copy-start(f32[64,256,1,1]{1,0,2,3:T(8,128)S(1)} %reshape.4489) | copy-start | bytes 196612
  20.6 43.8 %copy-start.168 = (pred[8]{0:T(512)(128)(4,1)}, pred[8]{0:T(512)(128)(4,1)S(1)}, u32[]{:S(2)}) copy-start(pred[8]{0:T(512)(128)(4,1)S(1)} %fusion.480) | copy-start | bytes 28
  21.2 50.9 %copy-start.161 = (f32[8]{0:T(128)}, f32[8]{0:T(128)S(1)}, u32[]{:S(2)}) copy-start(f32[8]{0:T(128)S(1)} %get-tuple-element.1575) | copy-start | bytes 100
  24.6 23.2 %copy-start.185 = (s32[192]{0:T(256)}, s32[192]{0:T(256)S(1)}, u32[]{:S(2)}) copy-start(s32[192]{0:T(256)S(1)} %reshape.4225) | copy-start | bytes 2308
  24.6 36.0 %copy-start.193 = (s32[32]{0:T(128)}, s32[32]{0:T(128)S(1)}, u32[]{:S(2)}) copy-start(s32[32]{0:T(128)S(1)} %get-tuple-element.1573) | copy-start | bytes 388
  25.3 23.3 %copy-start.195 = (s32[4]{0:T(128)S(1)}, s32[4]{0:T(128)}, u32[]{:S(2)}) copy-start(s32[4]{0:T(128)} %constant.1656.clone) | copy-start | bytes 52
  25.3 23.4 %copy-start.196 = (s32[4]{0:T(128)S(1)}, s32[4]{0:T(128)}, u32[]{:S(2)}) copy-start(s32[4]{0:T(128)} %constant.1657.clone) | copy-start | bytes 52
  48.7 57.5 %copy-start.11 = (pred[8,6,4,4]{3,2,1,0:T(4,128)(4,1)}, pred[8,6,4,4]{3,2,1,0:T(4,128)(4,1)S(1)}, u32[]{:S(2)}) copy-start(pred[8,6,4,4]{3,2,1,0:T(4,128)(4,1)S(1)} %compare_and_fusion) | copy-start | bytes 2308
  48.8 58.0 %copy-start.22 = (f32[8,6,4]{0,2,1:T(4,128)}, f32[8,6,4]{0,2,1:T(4,128)S(1)}, u32[]{:S(2)}) copy-start(f32[8,6,4]{0,2,1:T(4,128)S(1)} %and_convert_fusion.1) | copy-start | bytes 2308
  51.1 54.7 %copy-start.18 = (f32[8,6,4]{0,1,2:T(8,128)}, f32[8,6,4]{0,1,2:T(8,128)S(1)}, u32[]{:S(2)}) copy-start(f32[8,6,4]{0,1,2:T(8,128)S(1)} %copy.201) | copy-start | bytes 2308
  52.1 59.8 %copy-start.38 = (f32[8,4,256]{2,0,1:T(8,128)}, f32[8,4,256]{2,0,1:T(8,128)S(1)}, u32[]{:S(2)}) copy-start(f32[8,4,256]{2,0,1:T(8,128)S(1)} %get-tuple-element.1432) | copy-start | bytes 98308
  52.1 59.8 %copy-start.40 = (f32[8,4,256]{2,0,1:T(8,128)}, f32[8,4,256]{2,0,1:T(8,128)S(1)}, u32[]{:S(2)}) copy-start(f32[8,4,256]{2,0,1:T(8,128)S(1)} %get-tuple-element.1431) | copy-start | bytes 98308
  52.1 59.8 %copy-start.42 = (f32[8,4,256]{2,0,1:T(8,128)}, f32[8,4,256]{2,0,1:T(8,128)S(1)}, u32[]{:S(2)}) copy-start(f32[8,4,256]{2,0,1:T(8,128)S(1)} %get-tuple-element.1430) | copy-start | bytes 98308
  54.5 39.1 %all-to-all-start = ((f32[32,6,1024]{2,1,0:T(8,128)}), f32[32,6,1024]{2,1,0:T(8,128)}, u32[]{:S(2)}, u32[]{:S(2)}) async-start(f32[32,6,1024]{2,1,0:T(8,128)} %broadcast_multiply_fusion.13), calls=%async_computation | async-start | bytes 2097152 | tf_op jit(solution)/shard_map/all_to_all | solution.py:216
  93.6 32.5 %all-to-all-start.7 = ((f32[32,6,1024]{2,1,0:T(8,128)}), f32[32,6,1024]{2,1,0:T(8,128)}, u32[]{:S(2)}, u32[]{:S(2)}) async-start(f32[32,6,1024]{2,1,0:T(8,128)} %reshape.4182), calls=%async_computation.7 | async-start | bytes 2097152 | tf_op jit(solution)/shard_map/all_to_all | solution.py:290
  114.6 25.2 %copy-start.28 = (f32[6,8,4,256]{3,1,2,0:T(8,128)S(1)}, f32[6,8,4,256]{3,1,2,0:T(8,128)}, u32[]{:S(2)}) copy-start(f32[6,8,4,256]{3,1,2,0:T(8,128)} %copy-done.27) | copy-start | bytes 589828
  114.6 25.2 %copy-start.140 = (pred[8,6]{0,1:T(8,128)(4,1)S(1)}, pred[8,6]{0,1:T(8,128)(4,1)}, u32[]{:S(2)}) copy-start(pred[8,6]{0,1:T(8,128)(4,1)} %copy-done.139) | copy-start | bytes 148
  114.6 25.2 %copy-start.162 = (f32[8]{0:T(128)S(1)}, f32[8]{0:T(128)}, u32[]{:S(2)}) copy-start(f32[8]{0:T(128)} %copy-done.161) | copy-start | bytes 100
  129.2 29.9 %all-to-all-start.1 = ((f32[32,6,1024]{2,1,0:T(8,128)}), f32[32,6,1024]{2,1,0:T(8,128)}, u32[]{:S(2)}, u32[]{:S(2)}) async-start(f32[32,6,1024]{2,1,0:T(8,128)} %get-tuple-element.1550), calls=%async_computation.1 | async-start | bytes 2097152 | tf_op jit(solution)/shard_map/all_to_all | solution.py:222
  132.9 30.9 %copy-start.19 = (f32[8,6,4]{0,1,2:T(8,128)S(1)}, f32[8,6,4]{0,1,2:T(8,128)}, u32[]{:S(2)}) copy-start(f32[8,6,4]{0,1,2:T(8,128)} %copy-done.18) | copy-start | bytes 2308
  136.8 28.6 %copy-start.23 = (f32[8,6,4]{0,2,1:T(4,128)S(1)}, f32[8,6,4]{0,2,1:T(4,128)}, u32[]{:S(2)}) copy-start(f32[8,6,4]{0,2,1:T(4,128)} %copy-done.22) | copy-start | bytes 2308
  139.6 26.4 %copy-start.12 = (pred[8,6,4,4]{3,2,1,0:T(4,128)(4,1)S(1)}, pred[8,6,4,4]{3,2,1,0:T(4,128)(4,1)}, u32[]{:S(2)}) copy-start(pred[8,6,4,4]{3,2,1,0:T(4,128)(4,1)} %copy-done.11) | copy-start | bytes 2308
  140.5 24.9 %copy-start.75 = (f32[8,4,256]{2,0,1:T(8,128)}, f32[8,4,256]{2,0,1:T(8,128)S(1)}, u32[]{:S(2)}) copy-start(f32[8,4,256]{2,0,1:T(8,128)S(1)} %get-tuple-element.1407) | copy-start | bytes 98308
  140.5 24.9 %copy-start.77 = (f32[8,4,256]{2,0,1:T(8,128)}, f32[8,4,256]{2,0,1:T(8,128)S(1)}, u32[]{:S(2)}) copy-start(f32[8,4,256]{2,0,1:T(8,128)S(1)} %get-tuple-element.1406) | copy-start | bytes 98308
  140.5 24.9 %copy-start.79 = (f32[8,4,256]{2,0,1:T(8,128)}, f32[8,4,256]{2,0,1:T(8,128)S(1)}, u32[]{:S(2)}) copy-start(f32[8,4,256]{2,0,1:T(8,128)S(1)} %get-tuple-element.1405) | copy-start | bytes 98308
  142.4 24.8 %copy-start.32 = (f32[6,8,4,256]{3,1,2,0:T(8,128)S(1)}, f32[6,8,4,256]{3,1,2,0:T(8,128)}, u32[]{:S(2)}) copy-start(f32[6,8,4,256]{3,1,2,0:T(8,128)} %copy-done.31) | copy-start | bytes 589828
  200.2 14.4 %all-to-all-start.2 = ((f32[32,4,512]{2,1,0:T(4,128)}), f32[32,4,512]{2,1,0:T(4,128)S(1)}, u32[]{:S(2)}, u32[]{:S(2)}) async-start(f32[32,4,512]{2,1,0:T(4,128)} %broadcast_multiply_fusion.21), calls=%async_computation.2 | async-start | bytes 524288 | tf_op jit(solution)/shard_map/all_to_all | solution.py:241
  246.3 50.4 %all-to-all-start.3 = ((f32[32,6,1024]{2,1,0:T(8,128)}), f32[32,6,1024]{2,1,0:T(8,128)}, u32[]{:S(2)}, u32[]{:S(2)}) async-start(f32[32,6,1024]{2,1,0:T(8,128)} %broadcast_multiply_fusion.11), calls=%async_computation.3 | async-start | bytes 2097152 | tf_op jit(solution)/shard_map/all_to_all | solution.py:216
  249.7 51.8 %copy-start.20 = (f32[8,6,4]{0,1,2:T(8,128)S(1)}, f32[8,6,4]{0,1,2:T(8,128)}, u32[]{:S(2)}) copy-start(f32[8,6,4]{0,1,2:T(8,128)} %copy-done.18) | copy-start | bytes 2308
  341.4 38.8 %all-to-all-start.8 = ((f32[32,6,1024]{2,1,0:T(8,128)}), f32[32,6,1024]{2,1,0:T(8,128)}, u32[]{:S(2)}, u32[]{:S(2)}) async-start(f32[32,6,1024]{2,1,0:T(8,128)} %reshape.4196), calls=%async_computation.8 | async-start | bytes 2097152 | tf_op jit(solution)/shard_map/all_to_all | solution.py:297
  347.3 30.9 %copy-start.107 = (f32[8,3,256]{2,0,1:T(8,128)S(1)}, f32[8,3,256]{2,0,1:T(8,128)}, u32[]{:S(2)}) copy-start(f32[8,3,256]{2,0,1:T(8,128)} %get-tuple-element.1556) | copy-start | bytes 73732
  347.3 30.9 %copy-start.106 = (f32[8,3,256]{2,0,1:T(8,128)S(1)}, f32[8,3,256]{2,0,1:T(8,128)}, u32[]{:S(2)}) copy-start(f32[8,3,256]{2,0,1:T(8,128)} %get-tuple-element.1557) | copy-start | bytes 73732
  347.3 32.8 %copy-start.36 = (f32[1,32,6]{2,1,0:T(8,128)S(1)}, f32[1,32,6]{2,1,0:T(8,128)}, u32[]{:S(2)}) copy-start(f32[1,32,6]{2,1,0:T(8,128)} %copy-done.33) | copy-start | bytes 2308
  382.5 50.7 %copy-start.8 = (f32[8,4,16,256]{3,0,1,2:T(8,128)S(1)}, f32[8,4,16,256]{3,0,1,2:T(8,128)}, u32[]{:S(2)}) copy-start(f32[8,4,16,256]{3,0,1,2:T(8,128)} %get-tuple-element.932) | copy-start | bytes 1572868
  434.8 27.9 %copy-start.194 = (s32[32]{0:T(128)S(1)}, s32[32]{0:T(128)}, u32[]{:S(2)}) copy-start(s32[32]{0:T(128)} %copy-done.193) | copy-start | bytes 388
  436.1 28.7 %copy-start.159 = (s32[16]{0:T(128)S(1)}, s32[16]{0:T(128)}, u32[]{:S(2)}) copy-start(s32[16]{0:T(128)} %copy-done.157) | copy-start | bytes 196
  436.1 29.1 %copy-start.17 = (f32[64,256,1,1]{1,0,2,3:T(8,128)S(1)}, f32[64,256,1,1]{1,0,2,3:T(8,128)}, u32[]{:S(2)}) copy-start(f32[64,256,1,1]{1,0,2,3:T(8,128)} %copy-done.15) | copy-start | bytes 196612
  436.1 29.1 %copy-start.170 = (pred[8]{0:T(512)(128)(4,1)S(1)}, pred[8]{0:T(512)(128)(4,1)}, u32[]{:S(2)}) copy-start(pred[8]{0:T(512)(128)(4,1)} %copy-done.168) | copy-start | bytes 28
  446.4 16.3 %all-to-all-start.9 = ((f32[32,4,512]{2,1,0:T(4,128)}), f32[32,4,512]{2,1,0:T(4,128)S(1)}, u32[]{:S(2)}, u32[]{:S(2)}) async-start(f32[32,4,512]{2,1,0:T(4,128)} %slice.3011), calls=%async_computation.9 | async-start | bytes 524288 | tf_op jit(solution)/shard_map/all_to_all | solution.py:263
  499.7 37.4 %copy-start.26 = (f32[6,8,4,256]{3,1,2,0:T(8,128)S(1)}, f32[6,8,4,256]{3,1,2,0:T(8,128)}, u32[]{:S(2)}) copy-start(f32[6,8,4,256]{3,1,2,0:T(8,128)} %constant_dynamic-update-slice_fusion.34) | copy-start | bytes 589828
  499.7 38.3 %copy-start.2 = (f32[8,6,4,256]{3,0,2,1:T(8,128)S(1)}, f32[8,6,4,256]{3,0,2,1:T(8,128)}, u32[]{:S(2)}) copy-start(f32[8,6,4,256]{3,0,2,1:T(8,128)} %copy-done.1) | copy-start | bytes 589828
  499.7 38.3 %copy-start.49 = (f32[8,4,256]{2,0,1:T(8,128)S(1)}, f32[8,4,256]{2,0,1:T(8,128)}, u32[]{:S(2)}) copy-start(f32[8,4,256]{2,0,1:T(8,128)} %get-tuple-element.1427) | copy-start | bytes 98308
  499.7 39.1 %copy-start.47 = (f32[8,4,256]{2,0,1:T(8,128)S(1)}, f32[8,4,256]{2,0,1:T(8,128)}, u32[]{:S(2)}) copy-start(f32[8,4,256]{2,0,1:T(8,128)} %get-tuple-element.1428) | copy-start | bytes 98308
  499.7 40.0 %copy-start.45 = (f32[8,4,256]{2,0,1:T(8,128)S(1)}, f32[8,4,256]{2,0,1:T(8,128)}, u32[]{:S(2)}) copy-start(f32[8,4,256]{2,0,1:T(8,128)} %get-tuple-element.1429) | copy-start | bytes 98308
  499.7 40.7 %copy-start.43 = (f32[8,4,256]{2,0,1:T(8,128)S(1)}, f32[8,4,256]{2,0,1:T(8,128)}, u32[]{:S(2)}) copy-start(f32[8,4,256]{2,0,1:T(8,128)} %copy-done.42) | copy-start | bytes 98308
  499.7 41.5 %copy-start.41 = (f32[8,4,256]{2,0,1:T(8,128)S(1)}, f32[8,4,256]{2,0,1:T(8,128)}, u32[]{:S(2)}) copy-start(f32[8,4,256]{2,0,1:T(8,128)} %copy-done.40) | copy-start | bytes 98308
  499.7 41.5 %copy-start.86 = (f32[8,1,256]{2,0,1:T(8,128)S(1)}, f32[8,1,256]{2,0,1:T(8,128)}, u32[]{:S(2)}) copy-start(f32[8,1,256]{2,0,1:T(8,128)} %copy-done.85) | copy-start | bytes 24580
  499.7 42.3 %copy-start.39 = (f32[8,4,256]{2,0,1:T(8,128)S(1)}, f32[8,4,256]{2,0,1:T(8,128)}, u32[]{:S(2)}) copy-start(f32[8,4,256]{2,0,1:T(8,128)} %copy-done.38) | copy-start | bytes 98308
  499.7 42.3 %copy-start.51 = (f32[8,4,256]{2,0,1:T(8,128)S(1)}, f32[8,4,256]{2,0,1:T(8,128)}, u32[]{:S(2)}) copy-start(f32[8,4,256]{2,0,1:T(8,128)} %copy-done.50) | copy-start | bytes 98308
  499.8 42.3 %copy-start.82 = (f32[8,1,256]{2,0,1:T(8,128)S(1)}, f32[8,1,256]{2,0,1:T(8,128)}, u32[]{:S(2)}) copy-start(f32[8,1,256]{2,0,1:T(8,128)} %copy-done.81) | copy-start | bytes 24580
  499.8 42.3 %copy-start.84 = (f32[8,1,256]{2,0,1:T(8,128)S(1)}, f32[8,1,256]{2,0,1:T(8,128)}, u32[]{:S(2)}) copy-start(f32[8,1,256]{2,0,1:T(8,128)} %copy-done.83) | copy-start | bytes 24580
  499.8 29.7 %all-to-all-start.10 = ((f32[32,6,1024]{2,1,0:T(8,128)}), f32[32,6,1024]{2,1,0:T(8,128)}, u32[]{:S(2)}, u32[]{:S(2)}) async-start(f32[32,6,1024]{2,1,0:T(8,128)} %reshape.4205), calls=%async_computation.10 | async-start | bytes 2097152 | tf_op jit(solution)/shard_map/all_to_all | solution.py:290
  531.8 23.9 %copy-start.14 = (pred[8,6,4,4]{3,2,1,0:T(4,128)(4,1)S(1)}, pred[8,6,4,4]{3,2,1,0:T(4,128)(4,1)}, u32[]{:S(2)}) copy-start(pred[8,6,4,4]{3,2,1,0:T(4,128)(4,1)} %copy-done.11) | copy-start | bytes 2308
  575.4 29.9 %all-to-all-start.11 = ((f32[32,6,1024]{2,1,0:T(8,128)}), f32[32,6,1024]{2,1,0:T(8,128)}, u32[]{:S(2)}, u32[]{:S(2)}) async-start(f32[32,6,1024]{2,1,0:T(8,128)} %reshape.4219), calls=%async_computation.11 | async-start | bytes 2097152 | tf_op jit(solution)/shard_map/all_to_all | solution.py:297
  585.7 26.4 %copy-start.176 = (f32[8]{0:T(128)S(1)}, f32[8]{0:T(128)}, u32[]{:S(2)}) copy-start(f32[8]{0:T(128)} %copy-done.175) | copy-start | bytes 100
  608.4 43.2 %all-to-all-start.4 = ((f32[32,6,1024]{2,1,0:T(8,128)}), f32[32,6,1024]{2,1,0:T(8,128)}, u32[]{:S(2)}, u32[]{:S(2)}) async-start(f32[32,6,1024]{2,1,0:T(8,128)} %get-tuple-element.1542), calls=%async_computation.4 | async-start | bytes 2097152 | tf_op jit(solution)/shard_map/all_to_all | solution.py:222
  612.1 38.6 %copy-start.108 = (f32[8,1,4,256]{3,0,2,1:T(8,128)S(1)}, f32[8,1,4,256]{3,0,2,1:T(8,128)}, u32[]{:S(2)}) copy-start(f32[8,1,4,256]{3,0,2,1:T(8,128)} %get-tuple-element.1355) | copy-start | bytes 98308
  612.1 38.6 %copy-start.109 = (f32[8,1,4,256]{3,0,2,1:T(8,128)S(1)}, f32[8,1,4,256]{3,0,2,1:T(8,128)}, u32[]{:S(2)}) copy-start(f32[8,1,4,256]{3,0,2,1:T(8,128)} %get-tuple-element.1357) | copy-start | bytes 98308
  612.1 38.6 %copy-start.110 = (f32[8,1,4,256]{3,0,2,1:T(8,128)S(1)}, f32[8,1,4,256]{3,0,2,1:T(8,128)}, u32[]{:S(2)}) copy-start(f32[8,1,4,256]{3,0,2,1:T(8,128)} %get-tuple-element.1359) | copy-start | bytes 98308
  612.2 38.6 %copy-start.111 = (f32[8,1,4,256]{3,0,2,1:T(8,128)S(1)}, f32[8,1,4,256]{3,0,2,1:T(8,128)}, u32[]{:S(2)}) copy-start(f32[8,1,4,256]{3,0,2,1:T(8,128)} %get-tuple-element.1361) | copy-start | bytes 98308
  612.2 38.6 %copy-start.112 = (f32[8,1,4,256]{3,0,2,1:T(8,128)S(1)}, f32[8,1,4,256]{3,0,2,1:T(8,128)}, u32[]{:S(2)}) copy-start(f32[8,1,4,256]{3,0,2,1:T(8,128)} %get-tuple-element.1363) | copy-start | bytes 98308
  683.6 21.6 %all-to-all-start.5 = ((f32[32,4,512]{2,1,0:T(4,128)}), f32[32,4,512]{2,1,0:T(4,128)S(1)}, u32[]{:S(2)}, u32[]{:S(2)}) async-start(f32[32,4,512]{2,1,0:T(4,128)} %broadcast_multiply_fusion.20), calls=%async_computation.5 | async-start | bytes 524288 | tf_op jit(solution)/shard_map/all_to_all | solution.py:241
  (149 other events, 1602.0 us)
where the time goes:
time: 723 us; the launch traced here: 709 us
  local copies, waits for them, and re-layouts  272 us (38%)
  other arithmetic  216 us (30%)
  waiting for transfers between devices  75.2 us (10%)
  starting transfers between devices  59.4 us (8%)
  loops' own time  48 us (7%)
  matrix products  33.1 us (5%)
    scatter-add x4, other arithmetic, assemble(): picked = received.reshape(-1, 4, square)[row_ids]  59.7 us
    all_to_all x2, waiting for transfers between devices, backward_step(): lax.all_to_all(pull_ghost(sent_back)[0], 'blk', split_axis=0, concat_axis...  28.5 us
    pad x2, local copies, waits for them, and re-layouts, face_layers(): volume[:, :, extent - 1::extent].reshape(4, square)  28.1 us
    pad x2, local copies, waits for them, and re-layouts, face_layers(): volume[:, :, 0::extent].reshape(4, square)  28 us
    dynamic_update_slice x32, local copies, waits for them, and re-layouts, backward_process_block(): return lax.dynamic_update_index_in_dim(result, weight + pulled, number, 0)  26.5 us
    another operation x2, loops' own time, backward_step(): through = lax.fori_loop(0, live_count, backward_process_block, upward)  25.5 us
    scatter-add x4, local copies, waits for them, and re-layouts, boundary_change(): change.at[:, :, square - extent:]  25.1 us
    another operation x2, loops' own time, interior_sweep(): return lax.fori_loop(0, live_count, interior_process_block, initial)  22.5 us
  transfers between devices with their start and end apart: 12, of which 6 were waited for; matrix products, arithmetic and copies ran while one was open for 29% of the time, Pallas kernels for 0%

commit v1 on v0

v1 whole, which is shorter than its diff:
```python
import jax
import jax.numpy as jnp
import numpy as np
from jax import lax
from jax.experimental import pallas as pl
from jax.experimental.pallas import tpu as pltpu
from jax.sharding import PartitionSpec as P

sound_speed = 1.0
base_ratio = 0.04
speed_floor = 0.01
f32 = jnp.float32
bf16 = jnp.bfloat16


def half_map(extent):
    half = extent // 2
    square = extent * extent
    table = np.zeros((2, extent, extent, half, 2, half), np.float32)
    for group in range(2):
        for i in range(extent):
            for j in range(extent):
                table[group, i, j, i // 2, group, j // 2] = 0.25
    return table.reshape(2 * square, square // 2)


def dot2(values, table):
    high = values.astype(bf16)
    low = (values - high.astype(f32)).astype(bf16)
    return jnp.dot(high, table, preferred_element_type=f32) + jnp.dot(
        low, table, preferred_element_type=f32
    )


def roll(values, shift):
    lanes = values.shape[1]
    shift = shift % lanes
    return values if shift == 0 else pltpu.roll(values, shift, 1)


def flux_of(behind, beyond, normal, inv_behind, inv_beyond):
    v = behind[1 + normal] * inv_behind
    w = beyond[1 + normal] * inv_beyond
    c = sound_speed + jnp.sqrt(0.5 * (v * v + w * w) + speed_floor)
    result = [0.5 * ((behind[1 + normal] + beyond[1 + normal]) - c * (beyond[0] - behind[0]))]
    for k in range(1, 4):
        total = behind[k] * v + beyond[k] * w
        if k == 1 + normal:
            total = total + (sound_speed * sound_speed) * (behind[0] + beyond[0])
        result.append(0.5 * (total - c * (beyond[k] - behind[k])))
    return result


def flux_pull(behind, beyond, normal, inv_behind, inv_beyond, cot):
    v = behind[1 + normal] * inv_behind
    w = beyond[1 + normal] * inv_beyond
    inside = 0.5 * (v * v + w * w) + speed_floor
    root = jnp.sqrt(inside)
    c = sound_speed + root
    half_cot = [0.5 * part for part in cot]
    jump = half_cot[0] * (beyond[0] - behind[0])
    v_cot = half_cot[1] * behind[1]
    w_cot = half_cot[1] * beyond[1]
    for k in range(1, 4):
        jump = jump + half_cot[k] * (beyond[k] - behind[k])
        if k > 1:
            v_cot = v_cot + half_cot[k] * behind[k]
            w_cot = w_cot + half_cot[k] * beyond[k]
    scale = jump * (-0.5) / root
    v_cot = (v_cot + scale * v) * inv_behind
    w_cot = (w_cot + scale * w) * inv_beyond
    plus = v + c
    minus = w - c
    behind_cot = []
    beyond_cot = []
    pressure = (sound_speed * sound_speed) * half_cot[1 + normal]
    for k in range(4):
        if k == 0:
            behind_cot.append(c * half_cot[0] + pressure - v_cot * v)
            beyond_cot.append(pressure - c * half_cot[0] - w_cot * w)
        else:
            left = half_cot[k] * plus
            right = half_cot[k] * minus
            if k == 1 + normal:
                left = left + half_cot[0] + v_cot
                right = right + half_cot[0] + w_cot
            behind_cot.append(left)
            beyond_cot.append(right)
    return behind_cot, beyond_cot


class Plan:
    def __init__(self, slots, extent, peers):
        self.S = slots
        self.E = extent
        self.P = peers
        self.H = extent // 2
        self.COL = extent * extent // 2
        self.slab = (2, extent * 4 * slots, self.COL)
        self.ff = (2, 6 * 4 * slots, self.COL)
        self.fb = (2, 3 * slots * 8, self.COL)
        self.native = (slots * 4 * extent, 2 * self.COL)
        self.coarse = (slots * 16, self.COL)

    def lane(self, rows):
        return lax.broadcasted_iota(jnp.int32, (rows, self.COL), 1)

    def low(self, rows):
        return (self.lane(rows) & (self.E - 1)) < self.H

    def per_slot(self, scalar_of):
        sub = lax.broadcasted_iota(jnp.int32, (self.S, self.COL), 0)
        value = jnp.zeros((self.S, self.COL), jnp.int32)
        for s in range(self.S):
            value = jnp.where(sub == s, scalar_of(s), value)
        return value

    def ratio(self, levels):
        level = self.per_slot(lambda s: levels[s])
        degree = level.astype(f32)
        ratio = base_ratio * (1.0 + degree + 0.5 * degree * (degree - 1.0))
        return jnp.where(level >= 0, ratio, 0.0)

    def slab_at(self, ref):
        return lambda q, x, c: ref[q, (x * 4 + c) * self.S : (x * 4 + c + 1) * self.S, :]

    def native_at(self, planes):
        step = 4 * self.E
        return lambda q, x, c: planes[q][pl.ds(c * self.E + x, self.S, stride=step), :]

    def ff_at(self, ref):
        return lambda q, f, c: ref[q, (f * 4 + c) * self.S : (f * 4 + c + 1) * self.S, :]

    def fb_rows(self, f, c, swapped=False):
        side = f % 2
        half = 1 - side if swapped else side
        return pl.ds((f // 2) * self.S * 8 + half * 4 + c, self.S, stride=8)

    def extract(self, get, c):
        E, H, COL = self.E, self.H, self.COL
        lane = self.lane(self.S)
        group = lax.shift_right_logical(lane, E.bit_length() - 1)
        within = lane & (E - 1)
        faces = [[get(q, 0, c) for q in range(2)], [get(q, E - 1, c) for q in range(2)]]
        low_y, high_y, low_z, high_z = [], [], [], []
        for q in range(2):
            first, last, near, far = None, None, None, None
            for k in range(H):
                a = roll(get(0, q * H + k, c), E * k)
                b = roll(get(1, q * H + k, c), E * k - (COL - E))
                first = a if first is None else jnp.where(group == k, a, first)
                last = b if last is None else jnp.where(group == k, b, last)
            for x in range(E):
                source = get(q, x, c)
                a = roll(source, x)
                b = roll(source, x - (E - 1))
                near = a if near is None else jnp.where(within == x, a, near)
                far = b if far is None else jnp.where(within == x, b, far)
            low_y.append(first)
            high_y.append(last)
            low_z.append(near)
            high_z.append(far)
        return faces + [low_y, high_y, low_z, high_z]

    def spread(self, face, q, x, c):
        E, H, COL = self.E, self.H, self.COL
        lane = self.lane(self.S)
        within = lane & (E - 1)
        k = x % H
        y_face = face(x // H, 2 + q, c)
        if q == 0:
            total = jnp.where(lane < E, roll(y_face, -E * k), 0.0)
        else:
            total = jnp.where(lane >= COL - E, roll(y_face, (COL - E) - E * k), 0.0)
        near = roll(face(q, 4, c), -x)
        far = roll(face(q, 5, c), E - 1 - x)
        total = total + jnp.where(within == 0, near, jnp.where(within == E - 1, far, 0.0))
        if x == 0:
            total = total + face(q, 0, c)
        if x == E - 1:
            total = total + face(q, 1, c)
        return total

    def pack_faces(self, fb, send, out):
        sub = lax.broadcasted_iota(jnp.int32, (8, self.COL), 0)

        def one(peer, carry):
            for axis in range(3):
                slots = [jnp.maximum(send[peer * 6 + axis * 2 + side], 0) for side in range(2)]
                for q in range(2):
                    lo, hi = [
                        fb[q, pl.ds(pl.multiple_of((axis * self.S + slot) * 8, 8), 8), :]
                        for slot in slots
                    ]
                    row = axis * 16 + q * 8
                    out[peer, row : row + 8, :] = jnp.where(sub < 4, lo, hi)
            return carry

        lax.fori_loop(0, self.P, one, 0)

    def take_faces(self, packets, send, sums):
        def one(peer, carry):
            for f in range(6):
                slot = jnp.maximum(send[peer * 6 + f], 0)
                rows = pl.ds(pl.multiple_of(slot * 8, 8), 8)
                for q in range(2):
                    at = (f // 2) * 16 + q * 8
                    sums[f][q, rows, :] += packets[peer, at : at + 8, :]
            return carry

        for f in range(6):
            sums[f][...] = jnp.zeros(sums[f].shape, f32)
        lax.fori_loop(0, self.P, one, 0)

    def pack_averages(self, face, rb, send, out, row0, half):
        S, COL = self.S, self.COL
        rows = []
        for axis in range(3):
            for c in range(4):
                rows.append(
                    jnp.concatenate(
                        [face(q, 2 * axis + side, c) for side in range(2) for q in range(2)], axis=1
                    )
                )
        small = dot2(jnp.concatenate(rows, axis=0), half[...])
        for k in range(12):
            rb[pl.ds(k, S, stride=16), :] = small[k * S : (k + 1) * S]
        zero = jnp.zeros((S, COL), f32)
        for k in range(12, 16):
            rb[pl.ds(k, S, stride=16), :] = zero
        sub = lax.broadcasted_iota(jnp.int32, (8, COL), 0)
        low = self.low(8)

        def one(peer, carry):
            def part(f, at):
                slot = jnp.maximum(send[peer * 6 + f], 0)
                return rb[pl.ds(pl.multiple_of(slot * 16 + at, 8), 8), :]

            first = jnp.where(low, part(0, 0), part(1, 0))
            second = jnp.where(low, part(2, 0), part(3, 0))
            out[peer, row0 : row0 + 8, :] = jnp.where(sub < 4, first, second)
            out[peer, row0 + 8 : row0 + 16, :] = jnp.where(low, part(4, 8), part(5, 8))
            return carry

        lax.fori_loop(0, self.P, one, 0)

    def pack_quarters(self, fb, table, out, row0):
        E, H = self.E, self.H
        low = self.low(4)

        def clear(peer, carry):
            out[peer, row0 : row0 + 16, :] = jnp.zeros((16, self.COL), f32)
            return carry

        lax.fori_loop(0, self.P, clear, 0)
        for s in range(self.S):
            for f in range(6):
                base = (s * 6 + f) * 8

                def send_quarters(s=s, f=f, base=base):
                    axis, side = f // 2, f % 2
                    keep = low if side == 1 else jnp.logical_not(low)
                    row = (axis * self.S + s) * 8 + side * 4
                    at = row0 + axis * 4
                    for h in range(2):
                        values = fb[h, row : row + 4, :]
                        for g in range(2):
                            moved = roll(values, H * ((1 - side) - g))
                            peer = table[base + h * 2 + g]
                            out[peer, at : at + 4, :] += jnp.where(keep, moved, 0.0)

                pl.when(table[base + 4] == 2)(send_quarters)

    def take_quarters(self, packets, row0, send, sums, face_out, half_back):
        S, COL = self.S, self.COL

        def one(peer, carry):
            block = packets[peer, row0 : row0 + 16, :]
            for f in range(6):
                slot = jnp.maximum(send[peer * 6 + f], 0)
                rows = pl.ds(pl.multiple_of(slot * 16, 8), 16)
                sums[f][rows, :] += block
            return carry

        for f in range(6):
            sums[f][...] = jnp.zeros(sums[f].shape, f32)
        lax.fori_loop(0, self.P, one, 0)
        for f in range(6):
            axis, side = f // 2, f % 2
            rows = jnp.concatenate(
                [sums[f][pl.ds(axis * 4 + c, S, stride=16), :] for c in range(4)], axis=0
            )
            wide = dot2(rows, half_back[:, side * 2 * COL : (side + 1) * 2 * COL])
            for c in range(4):
                face_out(f, c, [wide[c * S : (c + 1) * S, q * COL : (q + 1) * COL] for q in range(2)])

    def ghosts(self, packets, table, planes, near, kinds, gb, half, half_back):
        S, COL, H = self.S, self.COL, self.H
        for s in range(S):
            for f in range(6):
                base = (s * 6 + f) * 8
                axis, half_row = f // 2, (1 - f % 2) * 4
                row = (axis * S + s) * 8 + half_row
                first = None
                for k in range(4):
                    peer = table[base + k]
                    got = []
                    for q in range(2):
                        at = axis * 16 + q * 8 + half_row
                        values = packets[peer, at : at + 4, :]
                        planes[k * 2 + q, row : row + 4, :] = values
                        got.append(values)
                    if k == 0:
                        first = got
                source = jnp.where(table[base + 5] == 1, first[1], first[0])
                source = jnp.where(table[base + 6] == 1, roll(source, -H), source)
                near[row : row + 4, :] = source
                kinds[row : row + 4, :] = jnp.full((4, COL), table[base + 4], jnp.int32)
        for axis in range(3):
            rows = slice(axis * S * 8, (axis + 1) * S * 8)
            kind = kinds[rows, :]
            coarse = 4.0 * dot2(near[rows, :], half_back[:, : 2 * COL])
            for h in range(2):
                parts = [planes[(h * 2 + g) * 2 + q, rows, :] for g in range(2) for q in range(2)]
                fine = dot2(jnp.concatenate(parts, axis=1), half[...])
                value = jnp.where(kind == 1, coarse[:, h * COL : (h + 1) * COL], planes[h, rows, :])
                gb[h, rows, :] = jnp.where(kind == 2, fine, value)

    def pack_ghost_cot(self, gb, table, wide, near, out, half, half_back):
        S, COL, H = self.S, self.COL, self.H
        low = self.low(4)

        def clear(peer, carry):
            out[peer, 0:48, :] = jnp.zeros((48, COL), f32)
            return carry

        lax.fori_loop(0, self.P, clear, 0)
        rows_all = 3 * S * 8
        for h in range(2):
            for g in range(2):
                spread = dot2(gb[h, :, :], half_back[:, g * 2 * COL : (g + 1) * 2 * COL])
                for q in range(2):
                    wide[(h * 2 + g) * 2 + q, :, :] = spread[:, q * COL : (q + 1) * COL]
        both = jnp.concatenate([gb[0, :, :], gb[1, :, :]], axis=1)
        near[...] = 4.0 * dot2(both, half[0 : 2 * COL, :])
        del rows_all
        for s in range(S):
            for f in range(6):
                base = (s * 6 + f) * 8
                axis, half_row = f // 2, (1 - f % 2) * 4
                row = (axis * S + s) * 8 + half_row
                kind = table[base + 4]

                def same(base=base, axis=axis, half_row=half_row, row=row):
                    peer = table[base]
                    for q in range(2):
                        at = axis * 16 + q * 8 + half_row
                        out[peer, at : at + 4, :] += gb[q, row : row + 4, :]

                def coarse(base=base, axis=axis, half_row=half_row, row=row):
                    peer = table[base]
                    values = near[row : row + 4, :]
                    values = jnp.where(table[base + 6] == 1, roll(values, H), values)
                    for q in range(2):
                        at = axis * 16 + q * 8 + half_row
                        out[peer, at : at + 4, :] += jnp.where(table[base + 5] == q, values, 0.0)

                def fine(base=base, axis=axis, half_row=half_row, row=row):
                    for k in range(4):
                        peer = table[base + k]
                        for q in range(2):
                            at = axis * 16 + q * 8 + half_row
                            out[peer, at : at + 4, :] += wide[k * 2 + q, row : row + 4, :]

                pl.when(kind == 0)(same)
                pl.when(kind == 1)(coarse)
                pl.when(kind == 2)(fine)

    def corrected(self, b_fb, packets, row0, table, out):
        H = self.H
        low = self.low(4)
        out[...] = b_fb[...]
        for s in range(self.S):
            for f in range(6):
                base = (s * 6 + f) * 8

                def replace(s=s, f=f, base=base):
                    axis, side = f // 2, f % 2
                    row = (axis * self.S + s) * 8 + side * 4
                    at = row0 + axis * 4
                    for h in range(2):
                        got = []
                        for g in range(2):
                            values = packets[table[base + h * 2 + g], at : at + 4, :]
                            got.append(roll(values, H * (g - (1 - side))))
                        out[h, row : row + 4, :] = jnp.where(low, got[0], got[1])

                pl.when(table[base + 4] == 2)(replace)

    def pack_octants(self, load, parents, out, row0):
        H = self.H
        low = self.low(4)
        for s in range(self.S):

            def send(s=s):
                for ox in range(2):
                    for oy in range(2):
                        peers = [parents[s * 8 + ox * 4 + oy * 2 + oz] for oz in range(2)]
                        for pair in range(H // 2):
                            x = ox * H + pair * 2
                            first, second = load(s, x, oy), load(s, x + 1, oy)
                            at = row0 + pair * 4
                            out[peers[0], at : at + 4, :] = jnp.where(low, first, roll(second, H))
                            out[peers[1], at : at + 4, :] = jnp.where(low, roll(first, -H), second)

            pl.when(parents[s * 8] >= 0)(send)

    def place_octants(self, packets, row0, parents, store):
        H = self.H
        low = self.low(4)
        for s in range(self.S):

            def place(s=s):
                for ox in range(2):
                    for oy in range(2):
                        peers = [parents[s * 8 + ox * 4 + oy * 2 + oz] for oz in range(2)]
                        for pair in range(H // 2):
                            x = ox * H + pair * 2
                            at = row0 + pair * 4
                            first = packets[peers[0], at : at + 4, :]
                            second = packets[peers[1], at : at + 4, :]
                            store(s, x, oy, jnp.where(low, first, roll(second, H)))
                            store(s, x + 1, oy, jnp.where(low, roll(first, -H), second))

            pl.when(parents[s * 8] >= 0)(place)

    def slab_rows(self, s, x):
        return pl.ds(x * 4 * self.S + s, 4, stride=self.S)

    def native_rows(self, s, x):
        return pl.ds(s * 4 * self.E + x, 4, stride=self.E)

    def pack_children(self, get, cb, children, out, row0, half):
        S = self.S
        rows = []
        for pair in range(self.E // 4):
            for c in range(4):
                x = 4 * pair
                rows.append(
                    jnp.concatenate(
                        [get(q, x + 2 * a, c) + get(q, x + 2 * a + 1, c) for a in range(2) for q in range(2)],
                        axis=1,
                    )
                )
        small = 0.5 * dot2(jnp.concatenate(rows, axis=0), half[...])
        for k in range(16):
            cb[pl.ds(k, S, stride=16), :] = small[k * S : (k + 1) * S]

        def one(peer, carry):
            slot = jnp.maximum(children[peer], 0)
            out[peer, row0 : row0 + 16, :] = cb[pl.ds(pl.multiple_of(slot * 16, 8), 16), :]
            return carry

        lax.fori_loop(0, self.P, one, 0)

    def upward(self, packets, row0, cc, children, parents, get, put, half_back):
        S, COL = self.S, self.COL
        cc[...] = jnp.zeros(cc.shape, f32)

        def one(peer, carry):
            child = children[peer]
            slot = jnp.where(child < 0, S, child)
            rows = pl.ds(pl.multiple_of(slot * 16, 8), 16)
            cc[rows, :] += jnp.where(child < 0, 0.0, packets[peer, row0 : row0 + 16, :])
            return carry

        lax.fori_loop(0, self.P, one, 0)
        rows = jnp.concatenate([cc[pl.ds(k, S, stride=16), :] for k in range(16)], axis=0)
        wide = 0.5 * dot2(rows, half_back[...])
        covered = self.per_slot(lambda s: parents[s * 8]) >= 0
        for x in range(self.E):
            for c in range(4):
                row = ((x // 4) * 4 + c) * S
                for q in range(2):
                    lane0 = ((x // 2) % 2 * 2 + q) * COL
                    added = wide[row : row + S, lane0 : lane0 + COL]
                    put(q, x, c, jnp.where(covered, 0.0, get(q, x, c)) + added)

    def shifted(self, planes, amount):
        COL = self.COL
        lane = self.lane(self.S)
        moved = [roll(values, amount) for values in planes]
        if amount > 0:
            return [jnp.where(lane < amount, moved[1 - q], moved[q]) for q in range(2)]
        return [jnp.where(lane >= COL + amount, moved[1 - q], moved[q]) for q in range(2)]

    def interior(self, get, levels, forward_put, cot_get=None, cot_put=None):
        S, E, COL = self.S, self.E, self.COL
        ratio = self.ratio(levels)
        lane = self.lane(S)
        y_inside = [lane >= 0, lane < COL - E]
        z_inside = (lane & (E - 1)) != E - 1
        zero = jnp.zeros((S, COL), f32)

        def row_of(x, c):
            return pl.ds(pl.multiple_of((x * 4 + c) * S, S), S)

        def one(x, carry):
            after = jnp.minimum(x + 1, E - 1)
            x_inside = x < E - 1
            here = [[get(q, row_of(x, c)) for c in range(4)] for q in range(2)]
            inverse = [1.0 / here[q][0] for q in range(2)]
            ahead = [[get(q, row_of(after, c)) for c in range(4)] for q in range(2)]
            ahead_inv = [1.0 / ahead[q][0] for q in range(2)]
            flux_carry, cot_carry = carry
            new_flux, new_cot = [], []
            change = [[None] * 4 for _ in range(2)]
            if cot_get is not None:
                weight = [[get_c(q, row_of(x, c)) for c in range(4)] for q in range(2)]
                scaled = [[ratio * weight[q][c] for c in range(4)] for q in range(2)]
                ahead_scaled = [
                    [ratio * get_c(q, row_of(after, c)) for c in range(4)] for q in range(2)
                ]
                back = [[weight[q][c] for c in range(4)] for q in range(2)]
            for q in range(2):
                if forward_put is not None:
                    flux = flux_of(here[q], ahead[q], 0, inverse[q], ahead_inv[q])
                    flux = [jnp.where(x_inside, part, 0.0) for part in flux]
                    change[q] = [flux[c] - flux_carry[q * 4 + c] for c in range(4)]
                    new_flux += flux
                if cot_get is not None:
                    cot = [
                        jnp.where(x_inside, ahead_scaled[q][c] - scaled[q][c], 0.0) for c in range(4)
                    ]
                    left, right = flux_pull(here[q], ahead[q], 0, inverse[q], ahead_inv[q], cot)
                    back[q] = [back[q][c] + left[c] + cot_carry[q * 4 + c] for c in range(4)]
                    new_cot += right
            for normal, step, inside in ((1, E, y_inside), (2, 1, [z_inside, z_inside])):
                turned = [self.shifted([here[q][c] for q in range(2)], -step) for c in range(4)]
                turned_inv = self.shifted(inverse, -step)
                beyond = [[turned[c][q] for c in range(4)] for q in range(2)]
                if forward_put is not None:
                    flux = []
                    for q in range(2):
                        got = flux_of(here[q], beyond[q], normal, inverse[q], turned_inv[q])
                        flux.append([jnp.where(inside[q], part, 0.0) for part in got])
                    for c in range(4):
                        behind = self.shifted([flux[q][c] for q in range(2)], step)
                        for q in range(2):
                            change[q][c] = change[q][c] + (flux[q][c] - behind[q])
                if cot_get is not None:
                    turned_w = [self.shifted([scaled[q][c] for q in range(2)], -step) for c in range(4)]
                    rights = []
                    for q in range(2):
                        cot = [
                            jnp.where(inside[q], turned_w[c][q] - scaled[q][c], 0.0) for c in range(4)
                        ]
                        left, right = flux_pull(here[q], beyond[q], normal, inverse[q], turned_inv[q], cot)
                        back[q] = [back[q][c] + left[c] for c in range(4)]
                        rights.append(right)
                    for c in range(4):
                        moved = self.shifted([rights[q][c] for q in range(2)], step)
                        for q in range(2):
                            back[q][c] = back[q][c] + moved[q]
            for q in range(2):
                for c in range(4):
                    if forward_put is not None:
                        forward_put(q, row_of(x, c), here[q][c] - ratio * change[q][c])
                    if cot_get is not None:
                        cot_put(q, row_of(x, c), back[q][c])
            return (new_flux, new_cot)

        get_c = cot_get
        start = (
            [zero] * 8 if forward_put is not None else [],
            [zero] * 8 if cot_get is not None else [],
        )
        lax.fori_loop(0, E, one, start)


def run(body, name, scalars, arrays, outs, scratch):
    specs = [pl.BlockSpec(memory_space=pltpu.SMEM) for _ in scalars]
    operands = list(scalars)
    for item in arrays:
        if isinstance(item, tuple):
            block = (item[0].shape[0], item[0].shape[1] // 2)
            for q in range(2):
                specs.append(pl.BlockSpec(block, lambda i, q=q: (0, q)))
                operands.append(item[0])
        else:
            zeros = (0,) * item.ndim
            specs.append(pl.BlockSpec(item.shape, lambda i, zeros=zeros: zeros))
            operands.append(item)
    out_specs = []
    for shape, native in outs:
        if native:
            out_specs.append(pl.BlockSpec(memory_space=pl.ANY))
        else:
            zeros = (0,) * len(shape)
            out_specs.append(pl.BlockSpec(shape, lambda i, zeros=zeros: zeros))
    return pl.pallas_call(
        body,
        name=name,
        grid=(1,),
        in_specs=specs,
        out_specs=out_specs,
        out_shape=[jax.ShapeDtypeStruct(shape, f32) for shape, native in outs],
        scratch_shapes=scratch,
        compiler_params=pltpu.CompilerParams(vmem_limit_bytes=48 * 1024 * 1024),
    )(*operands)


def write_native(planes, out, sems):
    copies = []
    lanes = planes[0].shape[1]
    for q in range(2):
        copies.append(
            pltpu.make_async_copy(planes[q], out.at[:, pl.ds(q * lanes, lanes)], sems.at[q])
        )
        copies[-1].start()
    for copy in copies:
        copy.wait()


def boundary_fluxes(plan, layers, ghost, emit):
    for f in range(6):
        result = []
        for q in range(2):
            inner = [layers(q, f, c) for c in range(4)]
            outer = [ghost(q, f, c) for c in range(4)]
            inner_inv, outer_inv = 1.0 / inner[0], 1.0 / outer[0]
            if f % 2 == 0:
                result.append(flux_of(outer, inner, f // 2, outer_inv, inner_inv))
            else:
                result.append(flux_of(inner, outer, f // 2, inner_inv, outer_inv))
        for c in range(4):
            emit(f, c, [result[q][c] for q in range(2)])


def boundary_pull(plan, layers, ghost, cot, emit):
    for f in range(6):
        result = []
        for q in range(2):
            inner = [layers(q, f, c) for c in range(4)]
            outer = [ghost(q, f, c) for c in range(4)]
            weight = [cot(q, f, c) for c in range(4)]
            inner_inv, outer_inv = 1.0 / inner[0], 1.0 / outer[0]
            if f % 2 == 0:
                out_cot, in_cot = flux_pull(outer, inner, f // 2, outer_inv, inner_inv, weight)
            else:
                in_cot, out_cot = flux_pull(inner, outer, f // 2, inner_inv, outer_inv, weight)
            result.append((in_cot, out_cot))
        for c in range(4):
            emit(f, c, [result[q][0][c] for q in range(2)], [result[q][1][c] for q in range(2)])


def on_device(fields, guidance, levels, send_faces, ghost_peer, ghost_code, child_send, parent_peer):
    slots, _, extent, square = fields.shape
    peers = send_faces.shape[1]
    plan = Plan(slots, extent, peers)
    S, E, COL = slots, extent, plan.COL
    half_np = half_map(extent)
    half = jnp.asarray(half_np, bf16)
    half_back = jnp.asarray(np.ascontiguousarray(half_np.T), bf16)

    first_map, second_map = ghost_code // 5, ghost_code % 5
    turned = (jnp.arange(6) >= 4)[None, :, None]
    major = jnp.where(turned, second_map, first_map)
    minor = jnp.where(turned, first_map, second_map)
    refined = ghost_peer[:, :, 1] >= 0
    quarter = (major - 3) * 2 + (minor - 3)
    chosen = jnp.maximum(ghost_peer, 0)
    columns = [
        jnp.where(refined, jnp.sum(jnp.where(quarter == k, chosen, 0), axis=2), chosen[:, :, 0])
        for k in range(4)
    ]
    coarser = ghost_code[:, :, 0] > 0
    kind = jnp.where(
        ghost_peer[:, :, 0] < 0, 3, jnp.where(refined, 2, jnp.where(coarser, 1, 0))
    )
    single = jnp.logical_and(coarser, jnp.logical_not(refined))
    columns += [
        kind,
        jnp.where(single, major[:, :, 0] - 1, 0),
        jnp.where(single, minor[:, :, 0] - 1, 0),
        jnp.zeros_like(kind),
    ]
    table = jnp.stack(columns, axis=-1).astype(jnp.int32).reshape(-1)
    send = send_faces.reshape(-1)
    children = child_send.reshape(-1)
    parents = parent_peer.reshape(-1)
    native_fields = fields.reshape(plan.native)
    native_guidance = guidance.reshape(plan.native)

    def exchange(packets):
        return lax.all_to_all(packets, "blk", split_axis=0, concat_axis=0, tiled=True)

    def vm(*shape):
        return pltpu.VMEM(shape, f32)

    def occupied_of(levels_ref):
        return plan.per_slot(lambda s: levels_ref[s]) >= 0

    fb_scratch = vm(*plan.fb)
    signs = [1.0, -1.0, 1.0, -1.0, 1.0, -1.0]

    def layers_of(get, fb, ff):
        for c in range(4):
            faces = plan.extract(get, c)
            for f in range(6):
                for q in range(2):
                    if fb is not None:
                        fb[q, plan.fb_rows(f, c), :] = faces[f][q]
                    if ff is not None:
                        ff[q, (f * 4 + c) * S : (f * 4 + c + 1) * S, :] = faces[f][q]

    def corrected_cot_of(get, levels_ref, fb):
        ratio = plan.ratio(levels_ref)
        for c in range(4):
            faces = plan.extract(get, c)
            for f in range(6):
                for q in range(2):
                    fb[q, plan.fb_rows(f, c), :] = (signs[f] * ratio) * faces[f][q]

    def finished(partial, corr, levels_ref, put):
        ratio = plan.ratio(levels_ref)
        occupied = ratio > 0.0
        get = plan.slab_at(partial)

        def face(q, f, c):
            value = corr[q, plan.fb_rows(f, c), :]
            return jnp.where(occupied, (signs[f] * ratio) * value, 0.0)

        for x in range(E):
            for c in range(4):
                for q in range(2):
                    put(q, x, c, get(q, x, c) + plan.spread(face, q, x, c))

    def ghost_reader(gb, layers, levels_ref):
        occupied = occupied_of(levels_ref)
        return lambda q, f, c: jnp.where(
            occupied, gb[q, plan.fb_rows(f, c, True), :], layers(q, f, c)
        )

    def slab_put(ref):
        def put(q, x, c, value):
            ref[q, (x * 4 + c) * S : (x * 4 + c + 1) * S, :] = value

        return put

    def dyn_get(ref):
        return lambda q, rows: ref[q, rows, :]

    def dyn_put(ref):
        def put(q, rows, value):
            ref[q, rows, :] = value

        return put

    ghost_scratch = [
        vm(8, 3 * S * 8, COL),
        vm(3 * S * 8, COL),
        pltpu.VMEM((3 * S * 8, COL), jnp.int32),
    ]

    def first_pack(send_s, parents_s, f0, f1, g0, g1, volume, layers, packets, fb):
        get = plan.native_at([f0, f1])
        for x in range(E):
            for c in range(4):
                for q in range(2):
                    volume[q, (x * 4 + c) * S : (x * 4 + c + 1) * S, :] = get(q, x, c)
        layers_of(plan.slab_at(volume), fb, layers)
        plan.pack_faces(fb, send_s, packets)
        planes = [g0, g1]
        plan.pack_octants(lambda s, x, q: planes[q][plan.native_rows(s, x), :], parents_s, packets, 48)

    volume1, layers1, packets = run(
        first_pack,
        "first_pack",
        [send, parents],
        [(native_fields,), (native_guidance,)],
        [(plan.slab, False), (plan.ff, False), ((peers, 64, COL), False)],
        [fb_scratch],
    )
    received1 = exchange(packets)

    def interior_first(levels_s, volume, partial):
        plan.interior(dyn_get(volume), levels_s, dyn_put(partial))

    (partial1,) = run(interior_first, "interior_first", [levels], [volume1], [(plan.slab, False)], [])

    def first_flux(levels_s, send_s, table_s, children_s, parents_s, g0, g1, layers, recv, half_r,
                   back_r, gb, b_fb, up, cot_fb, packets, planes, near, kinds, ff, rb, cc):
        plan.ghosts(recv, table_s, planes, near, kinds, gb, half_r, back_r)
        layer = plan.ff_at(layers)

        def emit(f, c, values):
            for q in range(2):
                b_fb[q, plan.fb_rows(f, c), :] = values[q]
                ff[q, (f * 4 + c) * S : (f * 4 + c + 1) * S, :] = values[q]

        boundary_fluxes(plan, layer, ghost_reader(gb, layer, levels_s), emit)
        plan.pack_averages(plan.ff_at(ff), rb, send_s, packets, 0, half_r)
        plan.upward(recv, 48, cc, children_s, parents_s, plan.native_at([g0, g1]), slab_put(up), back_r)
        corrected_cot_of(plan.slab_at(up), levels_s, cot_fb)
        plan.pack_quarters(cot_fb, table_s, packets, 16)

    ghosts1, fluxes1, up2, corrcot2, packets = run(
        first_flux,
        "first_flux",
        [levels, send, table, children, parents],
        [(native_guidance,), layers1, received1, half, half_back],
        [(plan.fb, False), (plan.fb, False), (plan.slab, False), (plan.fb, False),
         ((peers, 32, COL), False)],
        ghost_scratch + [vm(*plan.ff), vm(*plan.coarse), vm((S + 1) * 16, COL)],
    )
    received2 = exchange(packets)

    quarter_sums = [vm(S * 16, COL) for _ in range(6)]
    face_sums = [vm(2, S * 8, COL) for _ in range(6)]

    def flux_cot_of(recv, row0, cot_fb, table_s, send_s, sums, kinds, flux_cot, back_r):
        for s in range(S):
            for f in range(6):
                row = ((f // 2) * S + s) * 8 + (f % 2) * 4
                kinds[row : row + 4, :] = jnp.full((4, COL), table_s[(s * 6 + f) * 8 + 4], jnp.int32)

        def face_out(f, c, wide):
            keep = kinds[plan.fb_rows(f, c), :] != 2
            for q in range(2):
                own = jnp.where(keep, cot_fb[q, plan.fb_rows(f, c), :], 0.0)
                flux_cot[q, (f * 4 + c) * S : (f * 4 + c + 1) * S, :] = own + wide[q]

        plan.take_quarters(recv, row0, send_s, sums, face_out, back_r)

    def first_update(levels_s, send_s, table_s, children_s, partial, b_fb, cot_fb, recv, half_r,
                     back_r, updated, flux_cot, packets, corr, cb, kinds, *sums):
        plan.corrected(b_fb, recv, 0, table_s, corr)
        finished(partial, corr, levels_s, slab_put(updated))
        plan.pack_children(plan.slab_at(updated), cb, children_s, packets, 0, half_r)
        flux_cot_of(recv, 16, cot_fb, table_s, send_s, sums, kinds, flux_cot, back_r)

    updated1, fluxcot2, packets = run(
        first_update,
        "first_update",
        [levels, send, table, children],
        [partial1, fluxes1, corrcot2, received2, half, half_back],
        [(plan.slab, False), (plan.ff, False), ((peers, 16, COL), False)],
        [fb_scratch, vm(*plan.coarse), pltpu.VMEM((3 * S * 8, COL), jnp.int32)] + quarter_sums,
    )
    received3 = exchange(packets)

    def middle_pack(send_s, parents_s, updated, recv, volume, layers, packets, fb):
        volume[...] = updated[...]

        def store(s, x, q, value):
            volume[q, plan.slab_rows(s, x), :] = value

        plan.place_octants(recv, 0, parents_s, store)
        layers_of(plan.slab_at(volume), fb, layers)
        plan.pack_faces(fb, send_s, packets)

    volume2, layers2, packets = run(
        middle_pack,
        "middle_pack",
        [send, parents],
        [updated1, received3],
        [(plan.slab, False), (plan.ff, False), ((peers, 48, COL), False)],
        [fb_scratch],
    )
    received4 = exchange(packets)

    def interior_both(levels_s, volume, cot, partial, through):
        plan.interior(dyn_get(volume), levels_s, dyn_put(partial), dyn_get(cot), dyn_put(through))

    partial2, through2 = run(
        interior_both, "interior_both", [levels], [volume2, up2],
        [(plan.slab, False), (plan.slab, False)], [],
    )

    def second_flux(levels_s, send_s, table_s, layers, recv, flux_cot, half_r, back_r, b_fb,
                    layer_cot, packets, planes, near, kinds, gb, ff, rb, gcot):
        plan.ghosts(recv, table_s, planes, near, kinds, gb, half_r, back_r)
        layer = plan.ff_at(layers)
        ghost = ghost_reader(gb, layer, levels_s)

        def emit(f, c, values):
            for q in range(2):
                b_fb[q, plan.fb_rows(f, c), :] = values[q]
                ff[q, (f * 4 + c) * S : (f * 4 + c + 1) * S, :] = values[q]

        boundary_fluxes(plan, layer, ghost, emit)
        plan.pack_averages(plan.ff_at(ff), rb, send_s, packets, 48, half_r)

        def emit_cot(f, c, inner, outer):
            for q in range(2):
                layer_cot[q, (f * 4 + c) * S : (f * 4 + c + 1) * S, :] = inner[q]
                gcot[q, plan.fb_rows(f, c, True), :] = outer[q]

        boundary_pull(plan, layer, ghost, plan.ff_at(flux_cot), emit_cot)
        plan.pack_ghost_cot(gcot, table_s, planes, near, packets, half_r, back_r)

    fluxes2, layercot2, packets = run(
        second_flux,
        "second_flux",
        [levels, send, table],
        [layers2, received4, fluxcot2, half, half_back],
        [(plan.fb, False), (plan.ff, False), ((peers, 64, COL), False)],
        ghost_scratch + [fb_scratch, vm(*plan.ff), vm(*plan.coarse), fb_scratch],
    )
    received5 = exchange(packets)

    def total_face(layer_cot, sums):
        own = plan.ff_at(layer_cot)

        def face(q, f, c):
            return own(q, f, c) + sums[f][q, pl.ds((f % 2) * 4 + c, S, stride=8), :]

        return face

    def add_layers(through, layer_cot, total, sums, put):
        face = total_face(layer_cot, sums)
        for f in range(6):
            for c in range(4):
                for q in range(2):
                    total[q, (f * 4 + c) * S : (f * 4 + c + 1) * S, :] = face(q, f, c)
        get = plan.slab_at(through)
        summed = plan.ff_at(total)
        for x in range(E):
            for c in range(4):
                for q in range(2):
                    put(q, x, c, get(q, x, c) + plan.spread(summed, q, x, c))

    def second_update(levels_s, send_s, table_s, children_s, parents_s, partial, b_fb, through,
                      layer_cot, recv, half_r, updated, inner, packets, corr, cb, total, *sums):
        plan.corrected(b_fb, recv, 48, table_s, corr)
        finished(partial, corr, levels_s, slab_put(updated))
        plan.pack_children(plan.slab_at(updated), cb, children_s, packets, 0, half_r)
        plan.take_faces(recv, send_s, sums)
        add_layers(through, layer_cot, total, sums, slab_put(inner))
        plan.pack_octants(
            lambda s, x, q: inner[q, plan.slab_rows(s, x), :], parents_s, packets, 16
        )

    updated2, inner_cot, packets = run(
        second_update,
        "second_update",
        [levels, send, table, children, parents],
        [partial2, fluxes2, through2, layercot2, received5, half],
        [(plan.slab, False), (plan.slab, False), ((peers, 32, COL), False)],
        [fb_scratch, vm(*plan.coarse), vm(*plan.ff)] + face_sums,
    )
    received6 = exchange(packets)

    native_planes = [vm(S * 4 * E, COL), vm(S * 4 * E, COL)]

    def last_state(levels_s, table_s, children_s, parents_s, updated, inner, recv, back_r,
                   final, up, cot_fb, packets, n0, n1, cc, sems):
        plan.upward(recv, 16, cc, children_s, parents_s, plan.slab_at(inner), slab_put(up), back_r)
        corrected_cot_of(plan.slab_at(up), levels_s, cot_fb)
        plan.pack_quarters(cot_fb, table_s, packets, 0)
        planes = [n0, n1]
        get = plan.slab_at(updated)
        for x in range(E):
            for c in range(4):
                for q in range(2):
                    planes[q][pl.ds(c * E + x, S, stride=4 * E), :] = get(q, x, c)

        def store(s, x, q, value):
            planes[q][plan.native_rows(s, x), :] = value

        plan.place_octants(recv, 0, parents_s, store)
        write_native(planes, final, sems)

    final_fields, up1, corrcot1, packets = run(
        last_state,
        "last_state",
        [levels, table, children, parents],
        [updated2, inner_cot, received6, half_back],
        [(plan.native, True), (plan.slab, False), (plan.fb, False), ((peers, 16, COL), False)],
        native_planes + [vm((S + 1) * 16, COL), pltpu.SemaphoreType.DMA((2,))],
    )
    received7 = exchange(packets)

    def interior_back(levels_s, volume, cot, through):
        plan.interior(dyn_get(volume), levels_s, None, dyn_get(cot), dyn_put(through))

    (through1,) = run(
        interior_back, "interior_back", [levels], [volume1, up1], [(plan.slab, False)], []
    )

    def first_pull(levels_s, send_s, table_s, layers, gb, cot_fb, recv, half_r, back_r, layer_cot,
                   packets, planes, near, kinds, flux_cot, gcot, *sums):
        flux_cot_of(recv, 0, cot_fb, table_s, send_s, sums, kinds, flux_cot, back_r)
        layer = plan.ff_at(layers)

        def emit_cot(f, c, inner, outer):
            for q in range(2):
                layer_cot[q, (f * 4 + c) * S : (f * 4 + c + 1) * S, :] = inner[q]
                gcot[q, plan.fb_rows(f, c, True), :] = outer[q]

        boundary_pull(plan, layer, ghost_reader(gb, layer, levels_s), plan.ff_at(flux_cot), emit_cot)
        plan.pack_ghost_cot(gcot, table_s, planes, near, packets, half_r, back_r)

    layercot1, packets = run(
        first_pull,
        "first_pull",
        [levels, send, table],
        [layers1, ghosts1, corrcot1, received7, half, half_back],
        [(plan.ff, False), ((peers, 48, COL), False)],
        ghost_scratch + [vm(*plan.ff), fb_scratch] + quarter_sums,
    )
    received8 = exchange(packets)

    def last_cot(send_s, through, layer_cot, recv, gradient, total, n0, n1, sems, *sums):
        plan.take_faces(recv, send_s, sums)
        planes = [n0, n1]

        def put(q, x, c, value):
            planes[q][pl.ds(c * E + x, S, stride=4 * E), :] = value

        add_layers(through, layer_cot, total, sums, put)
        write_native(planes, gradient, sems)

    (gradient,) = run(
        last_cot,
        "last_cot",
        [send],
        [through1, layercot1, received8],
        [(plan.native, True)],
        [vm(*plan.ff)] + native_planes + [pltpu.SemaphoreType.DMA((2,))] + face_sums,
    )
    return (final_fields.reshape(fields.shape), gradient.reshape(fields.shape))


def solution(mesh):
    placed = (
        P("blk", None, None, None),
        P("blk", None, None, None),
        P("blk"),
        P("blk", None, None),
        P("blk", None, None),
        P("blk", None, None),
        P("blk", None),
        P("blk", None),
    )
    return jax.shard_map(
        on_device,
        mesh=mesh,
        in_specs=placed,
        out_specs=(P("blk", None, None, None), P("blk", None, None, None)),
        check_vma=False,
    )
```

time: 723 us -> 219 us (0.30); the launches traced: 709 us -> 219 us
  local copies, waits for them, and re-layouts: 272 us -> 10.7 us
  other arithmetic: 216 us -> 0.09 us
  blocking collectives: 0 us -> 69.4 us
  loops' own time: 48 us -> 0 us
  Pallas kernels: 0 us -> 45.2 us
  starting transfers between devices: 59.4 us -> 17.5 us
  matrix products: 33.1 us -> 0 us
    scatter-add x42 -> x0, other arithmetic: 109 us -> none  [the longest x4 59.7 us: assemble(): picked = received.reshape(-1, 4, square)[row_ids]]
    all_to_all x0 -> x4, blocking collectives: none -> 69.4 us  [exchange(): lax.all_to_all(packets, 'blk', split_axis=0, concat_axis=0, tiled=True)]
    pad x4 -> x0, local copies, waits for them, and re-layouts: 56.1 us -> none  [the longest x2 28.1 us: face_layers(): volume[:, :, extent - 1::extent].reshape(4, square)]
    another operation x4 -> x0, loops' own time: 48 us -> none  [the longest x2 25.5 us: backward_step(): through = lax.fori_loop(0, live_count, backward_process_block, upward)]
    pallas_call x0 -> x12, Pallas kernels: none -> 45.2 us  [run(): pl.pallas_call(body, name=name, grid=(1,), in_specs=specs, out_specs=out_...]
    all_to_all x12 -> x4, starting transfers between devices: 59.4 us -> 17.5 us  [exchange(): lax.all_to_all(packets, 'blk', split_axis=0, concat_axis=0, tiled=True)]
    mul x292 -> x0, other arithmetic: 39.8 us -> none  [the longest x6 14.6 us: pack_faces(): return flattened[row_ids] * present]
    slice x31 -> x0, local copies, waits for them, and re-layouts: 34.3 us -> none  [the longest x7 14.5 us: face_layers(): volume[:, :, 0::extent].reshape(4, square)]
  transfers between devices with their start and end apart: 12 -> 4, of which waited for: 6 -> 4; matrix products, arithmetic and copies ran while one was open for 29% -> 0% of each run, Pallas kernels for 0% -> 5%
where the time goes in v1:
time: 219 us
  waiting for transfers between devices  74.6 us (34%)
  blocking collectives  69.4 us (32%)
  Pallas kernels  45.2 us (21%)
  starting transfers between devices  17.5 us (8%)
  local copies, waits for them, and re-layouts  10.7 us (5%)
    all_to_all x4, waiting for transfers between devices, exchange(): lax.all_to_all(packets, 'blk', split_axis=0, concat_axis=0, tiled=True)  74.6 us
    all_to_all x4, blocking collectives, exchange(): lax.all_to_all(packets, 'blk', split_axis=0, concat_axis=0, tiled=True)  69.4 us
    pallas_call x12, Pallas kernels, run(): pl.pallas_call(body, name=name, grid=(1,), in_specs=specs, out_specs=out_...  45.2 us
    all_to_all x4, starting transfers between devices, exchange(): lax.all_to_all(packets, 'blk', split_axis=0, concat_axis=0, tiled=True)  17.5 us
    unnamed x39, local copies, waits for them, and re-layouts  9.58 us
  transfers between devices with their start and end apart: 4, of which 4 were waited for; matrix products, arithmetic and copies ran while one was open for 0% of the time, Pallas kernels for 5%

profile of v1, /device:TPU:0, one launch (start us, length us, event | category | flops | bytes accessed | tf_op | source)
XLA Modules:
  0.0 218.6 jit_solution(14460545479183530924)
XLA Ops:
  0.6 0.0 copy-start.17
  0.6 0.8 reshape.38.parents_s
  1.4 0.0 copy-done.17
  1.4 0.1 copy.27
  1.5 0.1 reshape.39.send_s
  1.6 0.0 copy-start
  1.6 1.0 copy-done
  2.7 0.0 copy-start.4
  2.7 1.0 copy-done.4
  3.7 2.7 %first_pack.1 = (f32[2,512,128]{2,1,0:T(8,128)S(1)}, f32[2,192,128]{2,1,0:T(8,128)S(1)}, f32[32,64,128]{2,1,0:T(8,128)}) custom-call(s32[192]{0:T(256)S(1)} %reshape.39.send_s, s32[64]{0:T(128)S(1)} %reshape.38.parents_s, f32[512,256]{1,0:T(8,128)S(1)} %bitcast.25, f32[512,256]{1,0:T(8,128)S(1)} %bitcast.26, f32[512,256]{1,0:T(8,128)S(1)} %bitcast.21, ...), custom_call_target="tpu_custom_call" | custom-call | tf_op jit(solution)/shard_map/first_pack/pallas_call | solution.py:601
  6.4 0.0 copy-start.15
  6.4 0.0 copy-start.1
  6.4 7.4 %all-to-all-start = ((f32[32,64,128]{2,1,0:T(8,128)}), f32[32,64,128]{2,1,0:T(8,128)S(1)}, u32[]{:S(2)}, u32[]{:S(2)}) async-start(f32[32,64,128]{2,1,0:T(8,128)} %get-tuple-element.32), calls=%async_computation | async-start | bytes 2097152 | tf_op jit(solution)/shard_map/all_to_all | solution.py:696
  13.8 0.0 copy-done.15
  13.9 0.0 copy-start.16
  13.9 0.1 copy.19
  14.0 0.6 copy-done.16
  14.6 0.1 copy.20
  14.7 0.0 copy-start.2
  14.7 0.0 copy-start.3
  14.8 0.1 copy.26
  15.0 0.1 reshape.36.table_s
  15.1 25.0 %all-to-all-done.recv = f32[32,64,128]{2,1,0:T(8,128)S(1)} async-done(((f32[32,64,128]{2,1,0:T(8,128)}), f32[32,64,128]{2,1,0:T(8,128)S(1)}, u32[]{:S(2)}, u32[]{:S(2)}) %all-to-all-start) | async-done | bytes 1048608 | tf_op jit(solution)/shard_map/all_to_all | solution.py:696
  40.0 0.0 copy-start.13
  40.0 0.0 copy-start.14
  40.0 0.0 copy-done.1
  40.0 0.0 copy-done.2
  40.0 0.0 copy-done.3
  40.1 0.6 copy-done.13
  40.7 0.0 copy-done.14
  40.7 5.6 %first_flux.1 = (f32[2,192,128]{2,1,0:T(8,128)S(1)}, f32[2,192,128]{2,1,0:T(8,128)S(1)}, f32[2,512,128]{2,1,0:T(8,128)S(1)}, f32[2,192,128]{2,1,0:T(8,128)S(1)}, f32[32,32,128]{2,1,0:T(8,128)}) custom-call(s32[8]{0:T(128)S(1)} %copy-done.13, s32[192]{0:T(256)S(1)} %reshape.39.send_s, s32[384]{0:T(512)S(1)} %reshape.36.table_s, s32[32]{0:T(128)S(1)} %bitcast.27, ...), custom_call_target="tpu_custom_call" | custom-call | tf_op jit(solution)/shard_map/first_flux/pallas_call | solution.py:601
  46.3 0.0 copy-start.11
  46.3 0.7 copy-done.11
  47.0 3.8 %all-to-all-start.1 = ((f32[32,32,128]{2,1,0:T(8,128)}), f32[32,32,128]{2,1,0:T(8,128)S(1)}, u32[]{:S(2)}, u32[]{:S(2)}) async-start(f32[32,32,128]{2,1,0:T(8,128)} %get-tuple-element.35), calls=%async_computation.1 | async-start | bytes 1048576 | tf_op jit(solution)/shard_map/all_to_all | solution.py:696
  50.8 0.0 copy-start.12
  50.8 3.5 %interior_first.1.partial = f32[2,512,128]{2,1,0:T(8,128)S(1)} custom-call(s32[8]{0:T(128)S(1)} %copy-done.13, f32[2,512,128]{2,1,0:T(8,128)S(1)} %get-tuple-element.30.volume), custom_call_target="tpu_custom_call" | custom-call | tf_op jit(solution)/shard_map/interior_first/pallas_call | solution.py:601
  54.3 12.1 %all-to-all-done.1.recv = f32[32,32,128]{2,1,0:T(8,128)S(1)} async-done(((f32[32,32,128]{2,1,0:T(8,128)}), f32[32,32,128]{2,1,0:T(8,128)S(1)}, u32[]{:S(2)}, u32[]{:S(2)}) %all-to-all-start.1) | async-done | bytes 524320 | tf_op jit(solution)/shard_map/all_to_all | solution.py:696
  66.4 0.0 copy-done.12
  66.4 3.7 %first_update.1 = (f32[2,512,128]{2,1,0:T(8,128)S(1)}, f32[2,192,128]{2,1,0:T(8,128)S(1)}, f32[32,16,128]{2,1,0:T(8,128)S(1)}) custom-call(s32[8]{0:T(128)S(1)} %copy-done.13, s32[192]{0:T(256)S(1)} %reshape.39.send_s, s32[384]{0:T(512)S(1)} %reshape.36.table_s, s32[32]{0:T(128)S(1)} %bitcast.28, f32[2,512,128]{2,1,0:T(8,128)S(1)} %interior_first.1.partial, ...), custom_call_target="tpu_custom_call" | custom-call | tf_op jit(solution)/shard_map/first_update/pallas_call | solution.py:601
  70.2 13.5 %all_to_all.40.recv = f32[32,16,128]{2,1,0:T(8,128)S(1)} all-to-all(f32[32,16,128]{2,1,0:T(8,128)S(1)} %get-tuple-element.37), channel_id=1, replica_groups=mesh['blk'=32] {'blk'}, dimensions={0} | all-to-all | bytes 524288 | tf_op jit(solution)/shard_map/all_to_all | solution.py:696
  83.7 1.7 middle_pack.1
  85.3 22.9 %all_to_all.41.recv = f32[32,48,128]{2,1,0:T(8,128)S(1)} all-to-all(f32[32,48,128]{2,1,0:T(8,128)S(1)} %get-tuple-element.42), channel_id=1, replica_groups=mesh['blk'=32] {'blk'}, dimensions={0} | all-to-all | bytes 1572864 | tf_op jit(solution)/shard_map/all_to_all | solution.py:696
  108.2 4.9 %second_flux.1 = (f32[2,192,128]{2,1,0:T(8,128)S(1)}, f32[2,192,128]{2,1,0:T(8,128)S(1)}, f32[32,64,128]{2,1,0:T(8,128)}) custom-call(s32[8]{0:T(128)S(1)} %copy-done.13, s32[192]{0:T(256)S(1)} %reshape.39.send_s, s32[384]{0:T(512)S(1)} %reshape.36.table_s, f32[2,192,128]{2,1,0:T(8,128)S(1)} %get-tuple-element.41.layers, ...), custom_call_target="tpu_custom_call" | custom-call | tf_op jit(solution)/shard_map/second_flux/pallas_call | solution.py:601
  113.1 0.0 copy-start.9
  113.1 0.7 copy-done.9
  113.7 3.6 %all-to-all-start.4 = ((f32[32,64,128]{2,1,0:T(8,128)}), f32[32,64,128]{2,1,0:T(8,128)S(1)}, u32[]{:S(2)}, u32[]{:S(2)}) async-start(f32[32,64,128]{2,1,0:T(8,128)} %get-tuple-element.47), calls=%async_computation.4 | async-start | bytes 2097152 | tf_op jit(solution)/shard_map/all_to_all | solution.py:696
  117.4 3.9 %interior_both.1 = (f32[2,512,128]{2,1,0:T(8,128)S(1)}, f32[2,512,128]{2,1,0:T(8,128)S(1)}) custom-call(s32[8]{0:T(128)S(1)} %copy-done.13, f32[2,512,128]{2,1,0:T(8,128)S(1)} %get-tuple-element.38.volume, f32[2,512,128]{2,1,0:T(8,128)S(1)} %get-tuple-element.39.cot), custom_call_target="tpu_custom_call" | custom-call | tf_op jit(solution)/shard_map/interior_both/pallas_call | solution.py:601
  121.3 0.0 copy-start.5
  121.3 0.8 copy-done.5
  122.1 0.0 copy-start.7
  122.1 0.8 copy-done.7
  122.9 20.7 %all-to-all-done.4.recv = f32[32,64,128]{2,1,0:T(8,128)S(1)} async-done(((f32[32,64,128]{2,1,0:T(8,128)}), f32[32,64,128]{2,1,0:T(8,128)S(1)}, u32[]{:S(2)}, u32[]{:S(2)}) %all-to-all-start.4) | async-done | bytes 1048608 | tf_op jit(solution)/shard_map/all_to_all | solution.py:696
  143.6 1.0 copy-done.6
  144.6 1.0 copy-done.8
  145.7 0.9 copy-done.10
  146.6 4.1 %second_update.1 = (f32[2,512,128]{2,1,0:T(8,128)S(1)}, f32[2,512,128]{2,1,0:T(8,128)S(1)}, f32[32,32,128]{2,1,0:T(8,128)S(1)}) custom-call(s32[8]{0:T(128)S(1)} %copy-done.13, s32[192]{0:T(256)S(1)} %reshape.39.send_s, s32[384]{0:T(512)S(1)} %reshape.36.table_s, s32[32]{0:T(128)S(1)} %bitcast.29, s32[64]{0:T(128)S(1)} %reshape.38.parents_s, ...), custom_call_target="tpu_custom_call" | custom-call | tf_op jit(solution)/shard_map/second_update/pallas_call | solution.py:601
  150.7 19.5 %all_to_all.42.recv = f32[32,32,128]{2,1,0:T(8,128)S(1)} all-to-all(f32[32,32,128]{2,1,0:T(8,128)S(1)} %get-tuple-element.50), channel_id=1, replica_groups=mesh['blk'=32] {'blk'}, dimensions={0} | all-to-all | bytes 1048576 | tf_op jit(solution)/shard_map/all_to_all | solution.py:696
  170.2 4.8 %last_state.1 = (f32[512,256]{1,0:T(8,128)}, f32[2,512,128]{2,1,0:T(8,128)S(1)}, f32[2,192,128]{2,1,0:T(8,128)S(1)}, f32[32,16,128]{2,1,0:T(8,128)S(1)}) custom-call(s32[8]{0:T(128)S(1)} %copy-done.13, s32[384]{0:T(512)S(1)} %reshape.36.table_s, s32[32]{0:T(128)S(1)} %bitcast.30, s32[64]{0:T(128)S(1)} %reshape.38.parents_s, ...), custom_call_target="tpu_custom_call" | custom-call | tf_op jit(solution)/shard_map/last_state/pallas_call | solution.py:601
  175.0 13.6 %all_to_all.43.recv = f32[32,16,128]{2,1,0:T(8,128)S(1)} all-to-all(f32[32,16,128]{2,1,0:T(8,128)S(1)} %get-tuple-element.55), channel_id=1, replica_groups=mesh['blk'=32] {'blk'}, dimensions={0} | all-to-all | bytes 524288 | tf_op jit(solution)/shard_map/all_to_all | solution.py:696
  188.6 4.2 %first_pull.1 = (f32[2,192,128]{2,1,0:T(8,128)S(1)}, f32[32,48,128]{2,1,0:T(8,128)}) custom-call(s32[8]{0:T(128)S(1)} %copy-done.13, s32[192]{0:T(256)S(1)} %reshape.39.send_s, s32[384]{0:T(512)S(1)} %reshape.36.table_s, f32[2,192,128]{2,1,0:T(8,128)S(1)} %get-tuple-element.31.layers, f32[2,192,128]{2,1,0:T(8,128)S(1)} %get-tuple-element.53.gb, ...), custom_call_target="tpu_custom_call" | custom-call | tf_op jit(solution)/shard_map/first_pull/pallas_call | solution.py:601
  192.8 2.6 %all-to-all-start.7 = ((f32[32,48,128]{2,1,0:T(8,128)}), f32[32,48,128]{2,1,0:T(8,128)S(1)}, u32[]{:S(2)}, u32[]{:S(2)}) async-start(f32[32,48,128]{2,1,0:T(8,128)} %get-tuple-element.57), calls=%async_computation.7 | async-start | bytes 1572864 | tf_op jit(solution)/shard_map/all_to_all | solution.py:696
  195.5 3.7 %interior_back.1.through = f32[2,512,128]{2,1,0:T(8,128)S(1)} custom-call(s32[8]{0:T(128)S(1)} %copy-done.13, f32[2,512,128]{2,1,0:T(8,128)S(1)} %get-tuple-element.30.volume, f32[2,512,128]{2,1,0:T(8,128)S(1)} %get-tuple-element.52.cot), custom_call_target="tpu_custom_call" | custom-call | tf_op jit(solution)/shard_map/interior_back/pallas_call | solution.py:601
  199.2 16.8 %all-to-all-done.7.recv = f32[32,48,128]{2,1,0:T(8,128)S(1)} async-done(((f32[32,48,128]{2,1,0:T(8,128)}), f32[32,48,128]{2,1,0:T(8,128)S(1)}, u32[]{:S(2)}, u32[]{:S(2)}) %all-to-all-start.7) | async-done | bytes 786464 | tf_op jit(solution)/shard_map/all_to_all | solution.py:696
  216.0 2.4 %last_cot.1 = f32[512,256]{1,0:T(8,128)} custom-call(s32[192]{0:T(256)S(1)} %reshape.39.send_s, f32[2,512,128]{2,1,0:T(8,128)S(1)} %interior_back.1.through, f32[2,192,128]{2,1,0:T(8,128)S(1)} %get-tuple-element.56.layer_cot, f32[32,48,128]{2,1,0:T(8,128)S(1)} %all-to-all-done.7.recv), custom_call_target="tpu_custom_call" | custom-call | tf_op jit(solution)/shard_map/last_cot/pallas_call | solution.py:601
  (14 shorter events, 0.1 us)
Async XLA Ops:
  0.6 0.8 copy-start.17
  1.6 1.0 copy-start
  2.7 1.0 copy-start.4
  6.4 7.4 %copy-start.15 = (s32[8,6,4]{0,2,1:T(4,128)S(1)}, s32[8,6,4]{0,2,1:T(4,128)}, u32[]{:S(2)}) copy-start(s32[8,6,4]{0,2,1:T(4,128)} %param.14) | copy-start | bytes 2308
  6.4 33.6 %copy-start.1 = (f32[8,4,16,256]{3,2,1,0:T(8,128)S(1)}, f32[8,4,16,256]{3,2,1,0:T(8,128)}, u32[]{:S(2)}) copy-start(f32[8,4,16,256]{3,2,1,0:T(8,128)} %param.11) | copy-start | bytes 1572868
  6.4 33.6 %all-to-all-start = ((f32[32,64,128]{2,1,0:T(8,128)}), f32[32,64,128]{2,1,0:T(8,128)S(1)}, u32[]{:S(2)}, u32[]{:S(2)}) async-start(f32[32,64,128]{2,1,0:T(8,128)} %get-tuple-element.32), calls=%async_computation | async-start | bytes 2097152 | tf_op jit(solution)/shard_map/all_to_all | solution.py:696
  13.9 0.7 copy-start.16
  14.7 25.4 %copy-start.2 = (bf16[512,128]{1,0:T(8,128)(2,1)S(1)}, bf16[512,128]{1,0:T(8,128)(2,1)}, u32[]{:S(2)}) copy-start(bf16[512,128]{1,0:T(8,128)(2,1)} %constant.44.clone.half_r) | copy-start | bytes 393220
  14.7 25.3 %copy-start.3 = (bf16[128,512]{1,0:T(8,128)(2,1)S(1)}, bf16[128,512]{1,0:T(8,128)(2,1)}, u32[]{:S(2)}) copy-start(bf16[128,512]{1,0:T(8,128)(2,1)} %constant.45.clone.back_r) | copy-start | bytes 393220
  40.0 0.7 copy-start.13
  40.0 0.7 copy-start.14
  46.3 0.7 copy-start.11
  47.0 19.4 %all-to-all-start.1 = ((f32[32,32,128]{2,1,0:T(8,128)}), f32[32,32,128]{2,1,0:T(8,128)S(1)}, u32[]{:S(2)}, u32[]{:S(2)}) async-start(f32[32,32,128]{2,1,0:T(8,128)} %get-tuple-element.35), calls=%async_computation.1 | async-start | bytes 1048576 | tf_op jit(solution)/shard_map/all_to_all | solution.py:696
  50.8 15.6 %copy-start.12 = (f32[2,192,128]{2,1,0:T(8,128)S(1)}, f32[2,192,128]{2,1,0:T(8,128)}, u32[]{:S(2)}) copy-start(f32[2,192,128]{2,1,0:T(8,128)} %copy-done.11) | copy-start | bytes 589828
  113.1 0.7 copy-start.9
  113.7 29.9 %all-to-all-start.4 = ((f32[32,64,128]{2,1,0:T(8,128)}), f32[32,64,128]{2,1,0:T(8,128)S(1)}, u32[]{:S(2)}, u32[]{:S(2)}) async-start(f32[32,64,128]{2,1,0:T(8,128)} %get-tuple-element.47), calls=%async_computation.4 | async-start | bytes 2097152 | tf_op jit(solution)/shard_map/all_to_all | solution.py:696
  121.3 0.8 copy-start.5
  122.1 0.8 copy-start.7
  143.6 1.0 copy-start.6
  144.6 1.0 copy-start.8
  145.7 0.9 copy-start.10
  192.8 23.2 %all-to-all-start.7 = ((f32[32,48,128]{2,1,0:T(8,128)}), f32[32,48,128]{2,1,0:T(8,128)S(1)}, u32[]{:S(2)}, u32[]{:S(2)}) async-start(f32[32,48,128]{2,1,0:T(8,128)} %get-tuple-element.57), calls=%async_computation.7 | async-start | bytes 1572864 | tf_op jit(solution)/shard_map/all_to_all | solution.py:696

commit v2 on v1

--- a/solution.py
+++ b/solution.py
@@ -186,7 +186,7 @@
 
         def one(peer, carry):
             for axis in range(3):
-                slots = [jnp.maximum(send[peer * 6 + axis * 2 + side], 0) for side in range(2)]
+                slots = [jnp.maximum(send[peer, axis * 2 + side], 0) for side in range(2)]
                 for q in range(2):
                     lo, hi = [
                         fb[q, pl.ds(pl.multiple_of((axis * self.S + slot) * 8, 8), 8), :]
@@ -201,7 +201,7 @@
     def take_faces(self, packets, send, sums):
         def one(peer, carry):
             for f in range(6):
-                slot = jnp.maximum(send[peer * 6 + f], 0)
+                slot = jnp.maximum(send[peer, f], 0)
                 rows = pl.ds(pl.multiple_of(slot * 8, 8), 8)
                 for q in range(2):
                     at = (f // 2) * 16 + q * 8
@@ -233,7 +233,7 @@
 
         def one(peer, carry):
             def part(f, at):
-                slot = jnp.maximum(send[peer * 6 + f], 0)
+                slot = jnp.maximum(send[peer, f], 0)
                 return rb[pl.ds(pl.multiple_of(slot * 16 + at, 8), 8), :]
 
             first = jnp.where(low, part(0, 0), part(1, 0))
@@ -277,7 +277,7 @@
         def one(peer, carry):
             block = packets[peer, row0 : row0 + 16, :]
             for f in range(6):
-                slot = jnp.maximum(send[peer * 6 + f], 0)
+                slot = jnp.maximum(send[peer, f], 0)
                 rows = pl.ds(pl.multiple_of(slot * 16, 8), 16)
                 sums[f][rows, :] += block
             return carry
@@ -405,7 +405,7 @@
             def send(s=s):
                 for ox in range(2):
                     for oy in range(2):
-                        peers = [parents[s * 8 + ox * 4 + oy * 2 + oz] for oz in range(2)]
+                        peers = [parents[s, ox * 4 + oy * 2 + oz] for oz in range(2)]
                         for pair in range(H // 2):
                             x = ox * H + pair * 2
                             first, second = load(s, x, oy), load(s, x + 1, oy)
@@ -413,7 +413,7 @@
                             out[peers[0], at : at + 4, :] = jnp.where(low, first, roll(second, H))
                             out[peers[1], at : at + 4, :] = jnp.where(low, roll(first, -H), second)
 
-            pl.when(parents[s * 8] >= 0)(send)
+            pl.when(parents[s, 0] >= 0)(send)
 
     def place_octants(self, packets, row0, parents, store):
         H = self.H
@@ -423,7 +423,7 @@
             def place(s=s):
                 for ox in range(2):
                     for oy in range(2):
-                        peers = [parents[s * 8 + ox * 4 + oy * 2 + oz] for oz in range(2)]
+                        peers = [parents[s, ox * 4 + oy * 2 + oz] for oz in range(2)]
                         for pair in range(H // 2):
                             x = ox * H + pair * 2
                             at = row0 + pair * 4
@@ -432,7 +432,7 @@
                             store(s, x, oy, jnp.where(low, first, roll(second, H)))
                             store(s, x + 1, oy, jnp.where(low, roll(first, -H), second))
 
-            pl.when(parents[s * 8] >= 0)(place)
+            pl.when(parents[s, 0] >= 0)(place)
 
     def slab_rows(self, s, x):
         return pl.ds(x * 4 * self.S + s, 4, stride=self.S)
@@ -440,7 +440,7 @@
     def native_rows(self, s, x):
         return pl.ds(s * 4 * self.E + x, 4, stride=self.E)
 
-    def pack_children(self, get, cb, children, out, row0, half):
+    def average_blocks(self, get, cb, half):
         S = self.S
         rows = []
         for pair in range(self.E // 4):
@@ -456,6 +456,7 @@
         for k in range(16):
             cb[pl.ds(k, S, stride=16), :] = small[k * S : (k + 1) * S]
 
+    def pack_children(self, cb, children, out, row0):
         def one(peer, carry):
             slot = jnp.maximum(children[peer], 0)
             out[peer, row0 : row0 + 16, :] = cb[pl.ds(pl.multiple_of(slot * 16, 8), 16), :]
@@ -477,7 +478,7 @@
         lax.fori_loop(0, self.P, one, 0)
         rows = jnp.concatenate([cc[pl.ds(k, S, stride=16), :] for k in range(16)], axis=0)
         wide = 0.5 * dot2(rows, half_back[...])
-        covered = self.per_slot(lambda s: parents[s * 8]) >= 0
+        covered = self.per_slot(lambda s: parents[s, 0]) >= 0
         for x in range(self.E):
             for c in range(4):
                 row = ((x // 4) * 4 + c) * S
@@ -578,48 +579,43 @@
         lax.fori_loop(0, E, one, start)
 
 
-def run(body, name, scalars, arrays, outs, scratch):
+def run(body, name, scalars, arrays, outs, scratch, aliases=None):
     specs = [pl.BlockSpec(memory_space=pltpu.SMEM) for _ in scalars]
     operands = list(scalars)
     for item in arrays:
         if isinstance(item, tuple):
-            block = (item[0].shape[0], item[0].shape[1] // 2)
-            for q in range(2):
-                specs.append(pl.BlockSpec(block, lambda i, q=q: (0, q)))
-                operands.append(item[0])
+            specs.append(pl.BlockSpec(memory_space=pl.ANY))
+            operands.append(item[0])
         else:
-            zeros = (0,) * item.ndim
-            specs.append(pl.BlockSpec(item.shape, lambda i, zeros=zeros: zeros))
+            specs.append(pl.BlockSpec(memory_space=pltpu.VMEM))
             operands.append(item)
-    out_specs = []
-    for shape, native in outs:
-        if native:
-            out_specs.append(pl.BlockSpec(memory_space=pl.ANY))
-        else:
-            zeros = (0,) * len(shape)
-            out_specs.append(pl.BlockSpec(shape, lambda i, zeros=zeros: zeros))
+    out_specs = [
+        pl.BlockSpec(memory_space=pl.ANY if native else pltpu.VMEM) for shape, native in outs
+    ]
     return pl.pallas_call(
         body,
         name=name,
-        grid=(1,),
         in_specs=specs,
         out_specs=out_specs,
         out_shape=[jax.ShapeDtypeStruct(shape, f32) for shape, native in outs],
         scratch_shapes=scratch,
-        compiler_params=pltpu.CompilerParams(vmem_limit_bytes=48 * 1024 * 1024),
+        input_output_aliases=aliases or {},
+        compiler_params=pltpu.CompilerParams(vmem_limit_bytes=24 * 1024 * 1024),
     )(*operands)
 
 
-def write_native(planes, out, sems):
+def native_copies(planes, whole, sems, inward, rows=None):
+    lanes = planes[0].shape[1]
     copies = []
-    lanes = planes[0].shape[1]
     for q in range(2):
-        copies.append(
-            pltpu.make_async_copy(planes[q], out.at[:, pl.ds(q * lanes, lanes)], sems.at[q])
-        )
-        copies[-1].start()
-    for copy in copies:
-        copy.wait()
+        part = whole.at[:, pl.ds(q * lanes, lanes)]
+        near = planes[q]
+        if rows is not None:
+            part = whole.at[pl.ds(*rows), pl.ds(q * lanes, lanes)]
+            near = planes[q].at[pl.ds(*rows), :]
+        source, target = (part, near) if inward else (near, part)
+        copies.append(pltpu.make_async_copy(source, target, sems.at[q]))
+    return copies
 
 
 def boundary_fluxes(plan, layers, ghost, emit):
@@ -686,9 +682,9 @@
         jnp.zeros_like(kind),
     ]
     table = jnp.stack(columns, axis=-1).astype(jnp.int32).reshape(-1)
-    send = send_faces.reshape(-1)
+    send = send_faces.reshape(peers, 6)
     children = child_send.reshape(-1)
-    parents = parent_peer.reshape(-1)
+    parents = parent_peer
     native_fields = fields.reshape(plan.native)
     native_guidance = guidance.reshape(plan.native)
 
@@ -702,6 +698,11 @@
         return plan.per_slot(lambda s: levels_ref[s]) >= 0
 
     fb_scratch = vm(*plan.fb)
+    kind_scratch = pltpu.VMEM((3 * S * 8, COL), jnp.int32)
+    native_planes = [vm(S * 4 * E, COL), vm(S * 4 * E, COL)]
+    pair_of_sems = pltpu.SemaphoreType.DMA((2,))
+    quarter_sums = [vm(S * 16, COL) for _ in range(6)]
+    face_sums = [vm(2, S * 8, COL) for _ in range(6)]
     signs = [1.0, -1.0, 1.0, -1.0, 1.0, -1.0]
 
     def layers_of(get, fb, ff):
@@ -757,13 +758,67 @@
 
         return put
 
-    ghost_scratch = [
-        vm(8, 3 * S * 8, COL),
-        vm(3 * S * 8, COL),
-        pltpu.VMEM((3 * S * 8, COL), jnp.int32),
-    ]
-
-    def first_pack(send_s, parents_s, f0, f1, g0, g1, volume, layers, packets, fb):
+    ghost_scratch = [vm(8, 3 * S * 8, COL), vm(3 * S * 8, COL), kind_scratch]
+
+    def flux_cot_of(recv, row0, cot_fb, table_s, send_s, sums, kinds, flux_cot, back_r):
+        for s in range(S):
+            for f in range(6):
+                row = ((f // 2) * S + s) * 8 + (f % 2) * 4
+                kinds[row : row + 4, :] = jnp.full((4, COL), table_s[(s * 6 + f) * 8 + 4], jnp.int32)
+
+        def face_out(f, c, wide):
+            keep = kinds[plan.fb_rows(f, c), :] != 2
+            for q in range(2):
+                own = jnp.where(keep, cot_fb[q, plan.fb_rows(f, c), :], 0.0)
+                flux_cot[q, (f * 4 + c) * S : (f * 4 + c + 1) * S, :] = own + wide[q]
+
+        plan.take_quarters(recv, row0, send_s, sums, face_out, back_r)
+
+    def flux_emitter(b_fb, ff):
+        def emit(f, c, values):
+            for q in range(2):
+                b_fb[q, plan.fb_rows(f, c), :] = values[q]
+                ff[q, (f * 4 + c) * S : (f * 4 + c + 1) * S, :] = values[q]
+
+        return emit
+
+    def cot_emitter(layer_cot, gcot):
+        def emit(f, c, inner, outer):
+            for q in range(2):
+                layer_cot[q, (f * 4 + c) * S : (f * 4 + c + 1) * S, :] = inner[q]
+                gcot[q, plan.fb_rows(f, c, True), :] = outer[q]
+
+        return emit
+
+    def carry_packets(source, out, row0):
+        def one(peer, carry):
+            out[peer, row0 : row0 + 16, :] = source[peer, :, :]
+            return carry
+
+        lax.fori_loop(0, peers, one, 0)
+
+    def add_layers(through, layer_cot, total, sums, put):
+        own = plan.ff_at(layer_cot)
+        for f in range(6):
+            for c in range(4):
+                for q in range(2):
+                    added = sums[f][q, pl.ds((f % 2) * 4 + c, S, stride=8), :]
+                    total[q, (f * 4 + c) * S : (f * 4 + c + 1) * S, :] = own(q, f, c) + added
+        get = plan.slab_at(through)
+        summed = plan.ff_at(total)
+        for x in range(E):
+            for c in range(4):
+                for q in range(2):
+                    put(q, x, c, get(q, x, c) + plan.spread(summed, q, x, c))
+
+    def first_pack(send_s, parents_s, fields_r, guide_r, volume, layers, packets, fb, f0, f1, g0,
+                   g1, f_sems, g_sems):
+        inward = native_copies([f0, f1], fields_r, f_sems, True)
+        guided = native_copies([g0, g1], guide_r, g_sems, True)
+        for copy in inward + guided:
+            copy.start()
+        for copy in inward:
+            copy.wait()
         get = plan.native_at([f0, f1])
         for x in range(E):
             for c in range(4):
@@ -771,6 +826,8 @@
                     volume[q, (x * 4 + c) * S : (x * 4 + c + 1) * S, :] = get(q, x, c)
         layers_of(plan.slab_at(volume), fb, layers)
         plan.pack_faces(fb, send_s, packets)
+        for copy in guided:
+            copy.wait()
         planes = [g0, g1]
         plan.pack_octants(lambda s, x, q: planes[q][plan.native_rows(s, x), :], parents_s, packets, 48)
 
@@ -780,7 +837,7 @@
         [send, parents],
         [(native_fields,), (native_guidance,)],
         [(plan.slab, False), (plan.ff, False), ((peers, 64, COL), False)],
-        [fb_scratch],
+        [fb_scratch] + native_planes + native_planes + [pair_of_sems, pair_of_sems],
     )
     received1 = exchange(packets)
 
@@ -789,64 +846,58 @@
 
     (partial1,) = run(interior_first, "interior_first", [levels], [volume1], [(plan.slab, False)], [])
 
-    def first_flux(levels_s, send_s, table_s, children_s, parents_s, g0, g1, layers, recv, half_r,
-                   back_r, gb, b_fb, up, cot_fb, packets, planes, near, kinds, ff, rb, cc):
+    def first_flux(levels_s, send_s, table_s, layers, recv, half_r, back_r, gb, b_fb, packets,
+                   planes, near, kinds, ff, rb):
         plan.ghosts(recv, table_s, planes, near, kinds, gb, half_r, back_r)
         layer = plan.ff_at(layers)
-
-        def emit(f, c, values):
-            for q in range(2):
-                b_fb[q, plan.fb_rows(f, c), :] = values[q]
-                ff[q, (f * 4 + c) * S : (f * 4 + c + 1) * S, :] = values[q]
-
-        boundary_fluxes(plan, layer, ghost_reader(gb, layer, levels_s), emit)
+        boundary_fluxes(plan, layer, ghost_reader(gb, layer, levels_s), flux_emitter(b_fb, ff))
         plan.pack_averages(plan.ff_at(ff), rb, send_s, packets, 0, half_r)
+
+    ghosts1, fluxes1, packets = run(
+        first_flux,
+        "first_flux",
+        [levels, send, table],
+        [layers1, received1, half, half_back],
+        [(plan.fb, False), (plan.fb, False), ((peers, 16, COL), False)],
+        ghost_scratch + [vm(*plan.ff), vm(*plan.coarse)],
+    )
+    received2 = exchange(packets)
+
+    def upward_second(levels_s, table_s, children_s, parents_s, guide_r, recv, back_r, up, cot_fb,
+                      packets, cc, g0, g1, sems):
+        guided = native_copies([g0, g1], guide_r, sems, True)
+        for copy in guided:
+            copy.start()
+        for copy in guided:
+            copy.wait()
         plan.upward(recv, 48, cc, children_s, parents_s, plan.native_at([g0, g1]), slab_put(up), back_r)
         corrected_cot_of(plan.slab_at(up), levels_s, cot_fb)
-        plan.pack_quarters(cot_fb, table_s, packets, 16)
-
-    ghosts1, fluxes1, up2, corrcot2, packets = run(
-        first_flux,
-        "first_flux",
-        [levels, send, table, children, parents],
-        [(native_guidance,), layers1, received1, half, half_back],
-        [(plan.fb, False), (plan.fb, False), (plan.slab, False), (plan.fb, False),
-         ((peers, 32, COL), False)],
-        ghost_scratch + [vm(*plan.ff), vm(*plan.coarse), vm((S + 1) * 16, COL)],
-    )
-    received2 = exchange(packets)
-
-    quarter_sums = [vm(S * 16, COL) for _ in range(6)]
-    face_sums = [vm(2, S * 8, COL) for _ in range(6)]
-
-    def flux_cot_of(recv, row0, cot_fb, table_s, send_s, sums, kinds, flux_cot, back_r):
-        for s in range(S):
-            for f in range(6):
-                row = ((f // 2) * S + s) * 8 + (f % 2) * 4
-                kinds[row : row + 4, :] = jnp.full((4, COL), table_s[(s * 6 + f) * 8 + 4], jnp.int32)
-
-        def face_out(f, c, wide):
-            keep = kinds[plan.fb_rows(f, c), :] != 2
-            for q in range(2):
-                own = jnp.where(keep, cot_fb[q, plan.fb_rows(f, c), :], 0.0)
-                flux_cot[q, (f * 4 + c) * S : (f * 4 + c + 1) * S, :] = own + wide[q]
-
-        plan.take_quarters(recv, row0, send_s, sums, face_out, back_r)
-
-    def first_update(levels_s, send_s, table_s, children_s, partial, b_fb, cot_fb, recv, half_r,
-                     back_r, updated, flux_cot, packets, corr, cb, kinds, *sums):
+        plan.pack_quarters(cot_fb, table_s, packets, 0)
+
+    up2, corrcot2, quarters2 = run(
+        upward_second,
+        "upward_second",
+        [levels, table, children, parents],
+        [(native_guidance,), received1, half_back],
+        [(plan.slab, False), (plan.fb, False), ((peers, 16, COL), False)],
+        [vm((S + 1) * 16, COL)] + native_planes + [pair_of_sems],
+    )
+
+    def first_update(levels_s, table_s, children_s, partial, b_fb, recv, quarters, half_r, updated,
+                     packets, corr, cb):
         plan.corrected(b_fb, recv, 0, table_s, corr)
         finished(partial, corr, levels_s, slab_put(updated))
-        plan.pack_children(plan.slab_at(updated), cb, children_s, packets, 0, half_r)
-        flux_cot_of(recv, 16, cot_fb, table_s, send_s, sums, kinds, flux_cot, back_r)
-
-    updated1, fluxcot2, packets = run(
+        plan.average_blocks(plan.slab_at(updated), cb, half_r)
+        plan.pack_children(cb, children_s, packets, 0)
+        carry_packets(quarters, packets, 16)
+
+    updated1, packets = run(
         first_update,
         "first_update",
-        [levels, send, table, children],
-        [partial1, fluxes1, corrcot2, received2, half, half_back],
-        [(plan.slab, False), (plan.ff, False), ((peers, 16, COL), False)],
-        [fb_scratch, vm(*plan.coarse), pltpu.VMEM((3 * S * 8, COL), jnp.int32)] + quarter_sums,
+        [levels, table, children],
+        [partial1, fluxes1, received2, quarters2, half],
+        [(plan.slab, False), ((peers, 32, COL), False)],
+        [fb_scratch, vm(*plan.coarse)],
     )
     received3 = exchange(packets)
 
@@ -870,6 +921,18 @@
     )
     received4 = exchange(packets)
 
+    def flux_cot_second(send_s, table_s, cot_fb, recv, back_r, flux_cot, kinds, *sums):
+        flux_cot_of(recv, 16, cot_fb, table_s, send_s, sums, kinds, flux_cot, back_r)
+
+    (fluxcot2,) = run(
+        flux_cot_second,
+        "flux_cot_second",
+        [send, table],
+        [corrcot2, received3, half_back],
+        [(plan.ff, False)],
+        [kind_scratch] + quarter_sums,
+    )
+
     def interior_both(levels_s, volume, cot, partial, through):
         plan.interior(dyn_get(volume), levels_s, dyn_put(partial), dyn_get(cot), dyn_put(through))
 
@@ -878,109 +941,100 @@
         [(plan.slab, False), (plan.slab, False)], [],
     )
 
-    def second_flux(levels_s, send_s, table_s, layers, recv, flux_cot, half_r, back_r, b_fb,
-                    layer_cot, packets, planes, near, kinds, gb, ff, rb, gcot):
+    def second_pull(levels_s, table_s, layers, recv, flux_cot, half_r, back_r, gb, layer_cot,
+                    packets, planes, near, kinds, gcot):
         plan.ghosts(recv, table_s, planes, near, kinds, gb, half_r, back_r)
         layer = plan.ff_at(layers)
-        ghost = ghost_reader(gb, layer, levels_s)
-
-        def emit(f, c, values):
-            for q in range(2):
-                b_fb[q, plan.fb_rows(f, c), :] = values[q]
-                ff[q, (f * 4 + c) * S : (f * 4 + c + 1) * S, :] = values[q]
-
-        boundary_fluxes(plan, layer, ghost, emit)
-        plan.pack_averages(plan.ff_at(ff), rb, send_s, packets, 48, half_r)
-
-        def emit_cot(f, c, inner, outer):
-            for q in range(2):
-                layer_cot[q, (f * 4 + c) * S : (f * 4 + c + 1) * S, :] = inner[q]
-                gcot[q, plan.fb_rows(f, c, True), :] = outer[q]
-
-        boundary_pull(plan, layer, ghost, plan.ff_at(flux_cot), emit_cot)
+        boundary_pull(
+            plan, layer, ghost_reader(gb, layer, levels_s), plan.ff_at(flux_cot),
+            cot_emitter(layer_cot, gcot),
+        )
         plan.pack_ghost_cot(gcot, table_s, planes, near, packets, half_r, back_r)
 
-    fluxes2, layercot2, packets = run(
+    ghosts2, layercot2, packets = run(
+        second_pull,
+        "second_pull",
+        [levels, table],
+        [layers2, received4, fluxcot2, half, half_back],
+        [(plan.fb, False), (plan.ff, False), ((peers, 48, COL), False)],
+        ghost_scratch + [fb_scratch],
+    )
+    received5 = exchange(packets)
+
+    def second_flux(levels_s, send_s, layers, gb, half_r, b_fb, packets, ff, rb):
+        layer = plan.ff_at(layers)
+        boundary_fluxes(plan, layer, ghost_reader(gb, layer, levels_s), flux_emitter(b_fb, ff))
+        plan.pack_averages(plan.ff_at(ff), rb, send_s, packets, 0, half_r)
+
+    fluxes2, averages2 = run(
         second_flux,
         "second_flux",
-        [levels, send, table],
-        [layers2, received4, fluxcot2, half, half_back],
-        [(plan.fb, False), (plan.ff, False), ((peers, 64, COL), False)],
-        ghost_scratch + [fb_scratch, vm(*plan.ff), vm(*plan.coarse), fb_scratch],
-    )
-    received5 = exchange(packets)
-
-    def total_face(layer_cot, sums):
-        own = plan.ff_at(layer_cot)
-
-        def face(q, f, c):
-            return own(q, f, c) + sums[f][q, pl.ds((f % 2) * 4 + c, S, stride=8), :]
-
-        return face
-
-    def add_layers(through, layer_cot, total, sums, put):
-        face = total_face(layer_cot, sums)
-        for f in range(6):
-            for c in range(4):
-                for q in range(2):
-                    total[q, (f * 4 + c) * S : (f * 4 + c + 1) * S, :] = face(q, f, c)
-        get = plan.slab_at(through)
-        summed = plan.ff_at(total)
-        for x in range(E):
-            for c in range(4):
-                for q in range(2):
-                    put(q, x, c, get(q, x, c) + plan.spread(summed, q, x, c))
-
-    def second_update(levels_s, send_s, table_s, children_s, parents_s, partial, b_fb, through,
-                      layer_cot, recv, half_r, updated, inner, packets, corr, cb, total, *sums):
-        plan.corrected(b_fb, recv, 48, table_s, corr)
-        finished(partial, corr, levels_s, slab_put(updated))
-        plan.pack_children(plan.slab_at(updated), cb, children_s, packets, 0, half_r)
+        [levels, send],
+        [layers2, ghosts2, half],
+        [(plan.fb, False), ((peers, 16, COL), False)],
+        [vm(*plan.ff), vm(*plan.coarse)],
+    )
+
+    def middle_cot(send_s, parents_s, through, layer_cot, recv, averages, inner, packets, total, *sums):
         plan.take_faces(recv, send_s, sums)
         add_layers(through, layer_cot, total, sums, slab_put(inner))
         plan.pack_octants(
-            lambda s, x, q: inner[q, plan.slab_rows(s, x), :], parents_s, packets, 16
+            lambda s, x, q: inner[q, plan.slab_rows(s, x), :], parents_s, packets, 0
         )
-
-    updated2, inner_cot, packets = run(
+        carry_packets(averages, packets, 16)
+
+    inner_cot, packets = run(
+        middle_cot,
+        "middle_cot",
+        [send, parents],
+        [through2, layercot2, received5, averages2],
+        [(plan.slab, False), ((peers, 32, COL), False)],
+        [vm(*plan.ff)] + face_sums,
+    )
+    received6 = exchange(packets)
+
+    def upward_first(levels_s, table_s, children_s, parents_s, inner, recv, back_r, up, cot_fb,
+                     packets, cc):
+        plan.upward(recv, 0, cc, children_s, parents_s, plan.slab_at(inner), slab_put(up), back_r)
+        corrected_cot_of(plan.slab_at(up), levels_s, cot_fb)
+        plan.pack_quarters(cot_fb, table_s, packets, 0)
+
+    up1, corrcot1, packets = run(
+        upward_first,
+        "upward_first",
+        [levels, table, children, parents],
+        [inner_cot, received6, half_back],
+        [(plan.slab, False), (plan.fb, False), ((peers, 16, COL), False)],
+        [vm((S + 1) * 16, COL)],
+    )
+    received7 = exchange(packets)
+
+    def second_update(levels_s, table_s, partial, b_fb, recv, half_r, final, cb, corr, updated, n0,
+                      n1, sems):
+        plan.corrected(b_fb, recv, 16, table_s, corr)
+        planes = [n0, n1]
+        put_slab = slab_put(updated)
+
+        def put(q, x, c, value):
+            put_slab(q, x, c, value)
+            planes[q][pl.ds(c * E + x, S, stride=4 * E), :] = value
+
+        finished(partial, corr, levels_s, put)
+        copies = native_copies(planes, final, sems, False)
+        for copy in copies:
+            copy.start()
+        plan.average_blocks(plan.slab_at(updated), cb, half_r)
+        for copy in copies:
+            copy.wait()
+
+    final_open, coarse2 = run(
         second_update,
         "second_update",
-        [levels, send, table, children, parents],
-        [partial2, fluxes2, through2, layercot2, received5, half],
-        [(plan.slab, False), (plan.slab, False), ((peers, 32, COL), False)],
-        [fb_scratch, vm(*plan.coarse), vm(*plan.ff)] + face_sums,
-    )
-    received6 = exchange(packets)
-
-    native_planes = [vm(S * 4 * E, COL), vm(S * 4 * E, COL)]
-
-    def last_state(levels_s, table_s, children_s, parents_s, updated, inner, recv, back_r,
-                   final, up, cot_fb, packets, n0, n1, cc, sems):
-        plan.upward(recv, 16, cc, children_s, parents_s, plan.slab_at(inner), slab_put(up), back_r)
-        corrected_cot_of(plan.slab_at(up), levels_s, cot_fb)
-        plan.pack_quarters(cot_fb, table_s, packets, 0)
-        planes = [n0, n1]
-        get = plan.slab_at(updated)
-        for x in range(E):
-            for c in range(4):
-                for q in range(2):
-                    planes[q][pl.ds(c * E + x, S, stride=4 * E), :] = get(q, x, c)
-
-        def store(s, x, q, value):
-            planes[q][plan.native_rows(s, x), :] = value
-
-        plan.place_octants(recv, 0, parents_s, store)
-        write_native(planes, final, sems)
-
-    final_fields, up1, corrcot1, packets = run(
-        last_state,
-        "last_state",
-        [levels, table, children, parents],
-        [updated2, inner_cot, received6, half_back],
-        [(plan.native, True), (plan.slab, False), (plan.fb, False), ((peers, 16, COL), False)],
-        native_planes + [vm((S + 1) * 16, COL), pltpu.SemaphoreType.DMA((2,))],
-    )
-    received7 = exchange(packets)
+        [levels, table],
+        [partial2, fluxes2, received6, half],
+        [(plan.native, True), (plan.coarse, False)],
+        [fb_scratch, vm(*plan.slab)] + native_planes + [pair_of_sems],
+    )
 
     def interior_back(levels_s, volume, cot, through):
         plan.interior(dyn_get(volume), levels_s, None, dyn_get(cot), dyn_put(through))
@@ -989,30 +1043,49 @@
         interior_back, "interior_back", [levels], [volume1, up1], [(plan.slab, False)], []
     )
 
-    def first_pull(levels_s, send_s, table_s, layers, gb, cot_fb, recv, half_r, back_r, layer_cot,
-                   packets, planes, near, kinds, flux_cot, gcot, *sums):
+    def first_pull(levels_s, send_s, table_s, children_s, layers, gb, cot_fb, recv, coarse, half_r,
+                   back_r, layer_cot, packets, planes, near, kinds, flux_cot, gcot, *sums):
+        plan.pack_children(coarse, children_s, packets, 48)
         flux_cot_of(recv, 0, cot_fb, table_s, send_s, sums, kinds, flux_cot, back_r)
         layer = plan.ff_at(layers)
-
-        def emit_cot(f, c, inner, outer):
-            for q in range(2):
-                layer_cot[q, (f * 4 + c) * S : (f * 4 + c + 1) * S, :] = inner[q]
-                gcot[q, plan.fb_rows(f, c, True), :] = outer[q]
-
-        boundary_pull(plan, layer, ghost_reader(gb, layer, levels_s), plan.ff_at(flux_cot), emit_cot)
+        boundary_pull(
+            plan, layer, ghost_reader(gb, layer, levels_s), plan.ff_at(flux_cot),
+            cot_emitter(layer_cot, gcot),
+        )
         plan.pack_ghost_cot(gcot, table_s, planes, near, packets, half_r, back_r)
 
     layercot1, packets = run(
         first_pull,
         "first_pull",
-        [levels, send, table],
-        [layers1, ghosts1, corrcot1, received7, half, half_back],
-        [(plan.ff, False), ((peers, 48, COL), False)],
+        [levels, send, table, children],
+        [layers1, ghosts1, corrcot1, received7, coarse2, half, half_back],
+        [(plan.ff, False), ((peers, 64, COL), False)],
         ghost_scratch + [vm(*plan.ff), fb_scratch] + quarter_sums,
     )
     received8 = exchange(packets)
 
-    def last_cot(send_s, through, layer_cot, recv, gradient, total, n0, n1, sems, *sums):
+    def last_cot(send_s, parents_s, through, layer_cot, recv, open_r, gradient, final, total, n0, n1,
+                 p0, p1, sems, *late):
+        del open_r
+        slot_sems, sums = late[0], late[1:]
+        placed = [p0, p1]
+
+        def store(s, x, q, value):
+            placed[q][plan.native_rows(s, x), :] = value
+
+        plan.place_octants(recv, 48, parents_s, store)
+
+        def each_covered(act):
+            for s in range(S):
+
+                def one(s=s):
+                    rows = (s * 4 * E, 4 * E)
+                    for copy in native_copies(placed, final, slot_sems.at[s], False, rows):
+                        act(copy)
+
+                pl.when(parents_s[s, 0] >= 0)(one)
+
+        each_covered(lambda copy: copy.start())
         plan.take_faces(recv, send_s, sums)
         planes = [n0, n1]
 
@@ -1020,15 +1093,22 @@
             planes[q][pl.ds(c * E + x, S, stride=4 * E), :] = value
 
         add_layers(through, layer_cot, total, sums, put)
-        write_native(planes, gradient, sems)
-
-    (gradient,) = run(
+        copies = native_copies(planes, gradient, sems, False)
+        for copy in copies:
+            copy.start()
+        for copy in copies:
+            copy.wait()
+        each_covered(lambda copy: copy.wait())
+
+    gradient, final_fields = run(
         last_cot,
         "last_cot",
-        [send],
-        [through1, layercot1, received8],
-        [(plan.native, True)],
-        [vm(*plan.ff)] + native_planes + [pltpu.SemaphoreType.DMA((2,))] + face_sums,
+        [send, parents],
+        [through1, layercot1, received8, (final_open,)],
+        [(plan.native, True), (plan.native, True)],
+        [vm(*plan.ff)] + native_planes + native_planes
+        + [pair_of_sems, pltpu.SemaphoreType.DMA((S, 2))] + face_sums,
+        aliases={5: 1},
     )
     return (final_fields.reshape(fields.shape), gradient.reshape(fields.shape))
 

time: 219 us -> 219 us (level)
  blocking collectives: 69.4 us -> 37.9 us
  waiting for transfers between devices: 74.6 us -> 87.5 us
  Pallas kernels: 45.2 us -> 51.7 us
  starting transfers between devices: 17.5 us -> 23.6 us
  local copies, waits for them, and re-layouts: 10.7 us -> 15.8 us
    all_to_all x4 -> x2, blocking collectives: 69.4 us -> 37.9 us  [exchange(): lax.all_to_all(packets, 'blk', split_axis=0, concat_axis=0, tiled=True)]
    all_to_all x4 -> x6, waiting for transfers between devices: 74.6 us -> 87.5 us  [exchange(): lax.all_to_all(packets, 'blk', split_axis=0, concat_axis=0, tiled=True)]
    pallas_call x12 -> x16, Pallas kernels: 45.2 us -> 51.7 us  [run(): pl.pallas_call(body, name=name, in_specs=specs, out_specs=out_specs, out_...]
    all_to_all x4 -> x6, starting transfers between devices: 17.5 us -> 23.6 us  [exchange(): lax.all_to_all(packets, 'blk', split_axis=0, concat_axis=0, tiled=True)]
    unnamed x39 -> x55, local copies, waits for them, and re-layouts: 9.58 us -> 15.6 us
  transfers between devices with their start and end apart: 4 -> 6, of which waited for: 4 -> 6; matrix products, arithmetic and copies ran while one was open for 0% -> 0% of each run, Pallas kernels for 5% -> 10%
where the time goes in v2:
time: 219 us; the launch traced here: 218 us
  waiting for transfers between devices  87.5 us (40%)
  Pallas kernels  51.7 us (24%)
  blocking collectives  37.9 us (17%)
  starting transfers between devices  23.6 us (11%)
  local copies, waits for them, and re-layouts  15.8 us (7%)
    all_to_all x6, waiting for transfers between devices, exchange(): lax.all_to_all(packets, 'blk', split_axis=0, concat_axis=0, tiled=True)  87.5 us
    pallas_call x16, Pallas kernels, run(): pl.pallas_call(body, name=name, in_specs=specs, out_specs=out_specs, out_...  51.7 us
    all_to_all x2, blocking collectives, exchange(): lax.all_to_all(packets, 'blk', split_axis=0, concat_axis=0, tiled=True)  37.9 us
    all_to_all x6, starting transfers between devices, exchange(): lax.all_to_all(packets, 'blk', split_axis=0, concat_axis=0, tiled=True)  23.6 us
    unnamed x55, local copies, waits for them, and re-layouts  15.6 us
  transfers between devices with their start and end apart: 6, of which 6 were waited for; matrix products, arithmetic and copies ran while one was open for 0% of the time, Pallas kernels for 10%

profile of v2, /device:TPU:0, one launch (start us, length us, event | category | flops | bytes accessed | tf_op | source)
XLA Modules:
  0.0 217.7 jit_solution(6141700511646846863)
XLA Ops:
  0.6 0.8 copy.21
  1.4 0.7 copy-done.21
  2.1 1.0 copy-done.2
  3.1 1.0 copy-done.4
  4.2 3.1 %first_pack.1 = (f32[2,512,128]{2,1,0:T(8,128)S(1)}, f32[2,192,128]{2,1,0:T(8,128)S(1)}, f32[32,64,128]{2,1,0:T(8,128)}) custom-call(s32[32,6]{1,0:T(8,128)S(1)} %bitcast.24, s32[8,8]{1,0:T(8,128)S(1)} %copy-done.21, f32[512,256]{1,0:T(8,128)S(1)} %bitcast.32, f32[512,256]{1,0:T(8,128)S(1)} %bitcast.22), custom_call_target="tpu_custom_call" | custom-call | tf_op jit(solution)/shard_map/first_pack/pallas_call | solution.py:595
  7.3 0.0 copy-start.24
  7.3 7.6 %all-to-all-start = ((f32[32,64,128]{2,1,0:T(8,128)}), f32[32,64,128]{2,1,0:T(8,128)S(1)}, u32[]{:S(2)}, u32[]{:S(2)}) async-start(f32[32,64,128]{2,1,0:T(8,128)} %get-tuple-element.36), calls=%async_computation | async-start | bytes 2097152 | tf_op jit(solution)/shard_map/all_to_all | solution.py:692
  14.9 0.0 copy-start.25
  14.9 0.1 copy.22
  15.0 0.6 copy-done.25
  15.6 0.1 copy.23
  15.7 0.0 copy-start
  15.8 0.0 copy-start.1
  15.9 0.1 copy.29
  16.0 0.1 reshape.36.table_s
  16.1 0.0 copy-start.22
  16.1 25.0 %all-to-all-done.recv = f32[32,64,128]{2,1,0:T(8,128)S(1)} async-done(((f32[32,64,128]{2,1,0:T(8,128)}), f32[32,64,128]{2,1,0:T(8,128)S(1)}, u32[]{:S(2)}, u32[]{:S(2)}) %all-to-all-start) | async-done | bytes 1048608 | tf_op jit(solution)/shard_map/all_to_all | solution.py:692
  41.1 0.0 copy-done.1
  41.1 2.7 %first_flux.1 = (f32[2,192,128]{2,1,0:T(8,128)S(1)}, f32[2,192,128]{2,1,0:T(8,128)S(1)}, f32[32,16,128]{2,1,0:T(8,128)}) custom-call(s32[8]{0:T(128)S(1)} %copy-done.22, s32[32,6]{1,0:T(8,128)S(1)} %bitcast.25, s32[384]{0:T(512)S(1)} %reshape.36.table_s, f32[2,192,128]{2,1,0:T(8,128)S(1)} %get-tuple-element.35.layers, f32[32,64,128]{2,1,0:T(8,128)S(1)} %all-to-all-done.recv, ...), custom_call_target="tpu_custom_call" | custom-call | tf_op jit(solution)/shard_map/first_flux/pallas_call | solution.py:595
  43.8 0.7 copy-done.13
  44.5 0.7 copy-done.17
  45.1 3.6 %all-to-all-start.1 = ((f32[32,16,128]{2,1,0:T(8,128)}), f32[32,16,128]{2,1,0:T(8,128)S(1)}, u32[]{:S(2)}, u32[]{:S(2)}) async-start(f32[32,16,128]{2,1,0:T(8,128)} %get-tuple-element.38), calls=%async_computation.1 | async-start | bytes 524288 | tf_op jit(solution)/shard_map/all_to_all | solution.py:692
  48.8 0.0 copy-start.3
  48.8 3.5 %interior_first.1.partial = f32[2,512,128]{2,1,0:T(8,128)S(1)} custom-call(s32[8]{0:T(128)S(1)} %copy-done.22, f32[2,512,128]{2,1,0:T(8,128)S(1)} %get-tuple-element.34.volume), custom_call_target="tpu_custom_call" | custom-call | tf_op jit(solution)/shard_map/interior_first/pallas_call | solution.py:595
  52.3 0.0 copy-start.23
  52.3 0.6 copy-done.23
  53.0 3.8 %upward_second.1 = (f32[2,512,128]{2,1,0:T(8,128)S(1)}, f32[2,192,128]{2,1,0:T(8,128)S(1)}, f32[32,16,128]{2,1,0:T(8,128)S(1)}) custom-call(s32[8]{0:T(128)S(1)} %copy-done.22, s32[384]{0:T(512)S(1)} %reshape.36.table_s, s32[32]{0:T(128)S(1)} %bitcast.33, s32[8,8]{1,0:T(8,128)S(1)} %copy-done.21, f32[512,256]{1,0:T(8,128)S(1)} %bitcast.23, ...), custom_call_target="tpu_custom_call" | custom-call | tf_op jit(solution)/shard_map/upward_second/pallas_call | solution.py:595
  56.8 0.0 copy-start.7
  56.8 0.8 copy-done.7
  57.6 1.8 all-to-all-done.1.recv
  59.3 0.9 copy-done.14
  60.3 3.3 %first_update.1 = (f32[2,512,128]{2,1,0:T(8,128)S(1)}, f32[32,32,128]{2,1,0:T(8,128)S(1)}) custom-call(s32[8]{0:T(128)S(1)} %copy-done.22, s32[384]{0:T(512)S(1)} %reshape.36.table_s, s32[32]{0:T(128)S(1)} %bitcast.34, f32[2,512,128]{2,1,0:T(8,128)S(1)} %interior_first.1.partial, f32[2,192,128]{2,1,0:T(8,128)S(1)} %copy-done.14, ...), custom_call_target="tpu_custom_call" | custom-call | tf_op jit(solution)/shard_map/first_update/pallas_call | solution.py:595
  63.6 18.6 %all_to_all.40.recv = f32[32,32,128]{2,1,0:T(8,128)S(1)} all-to-all(f32[32,32,128]{2,1,0:T(8,128)S(1)} %get-tuple-element.41), channel_id=1, replica_groups=mesh['blk'=32] {'blk'}, dimensions={0} | all-to-all | bytes 1048576 | tf_op jit(solution)/shard_map/all_to_all | solution.py:692
  82.2 2.8 %middle_pack.1 = (f32[2,512,128]{2,1,0:T(8,128)S(1)}, f32[2,192,128]{2,1,0:T(8,128)S(1)}, f32[32,48,128]{2,1,0:T(8,128)}) custom-call(s32[32,6]{1,0:T(8,128)S(1)} %bitcast.26, s32[8,8]{1,0:T(8,128)S(1)} %copy-done.21, f32[2,512,128]{2,1,0:T(8,128)S(1)} %get-tuple-element.40.updated, f32[32,32,128]{2,1,0:T(8,128)S(1)} %all_to_all.40.recv), custom_call_target="tpu_custom_call" | custom-call | tf_op jit(solution)/shard_map/middle_pack/pallas_call | solution.py:595
  85.0 0.8 copy-done.9
  85.8 3.3 %all-to-all-start.3 = ((f32[32,48,128]{2,1,0:T(8,128)}), f32[32,48,128]{2,1,0:T(8,128)S(1)}, u32[]{:S(2)}, u32[]{:S(2)}) async-start(f32[32,48,128]{2,1,0:T(8,128)} %get-tuple-element.46), calls=%async_computation.3 | async-start | bytes 1572864 | tf_op jit(solution)/shard_map/all_to_all | solution.py:692
  89.1 1.5 flux_cot_second.1.flux_cot
  90.6 19.1 %all-to-all-done.3.recv = f32[32,48,128]{2,1,0:T(8,128)S(1)} async-done(((f32[32,48,128]{2,1,0:T(8,128)}), f32[32,48,128]{2,1,0:T(8,128)S(1)}, u32[]{:S(2)}, u32[]{:S(2)}) %all-to-all-start.3) | async-done | bytes 786464 | tf_op jit(solution)/shard_map/all_to_all | solution.py:692
  109.7 4.0 %second_pull.1 = (f32[2,192,128]{2,1,0:T(8,128)S(1)}, f32[2,192,128]{2,1,0:T(8,128)S(1)}, f32[32,48,128]{2,1,0:T(8,128)}) custom-call(s32[8]{0:T(128)S(1)} %copy-done.22, s32[384]{0:T(512)S(1)} %reshape.36.table_s, f32[2,192,128]{2,1,0:T(8,128)S(1)} %get-tuple-element.45.layers, f32[32,48,128]{2,1,0:T(8,128)S(1)} %all-to-all-done.3.recv, ...), custom_call_target="tpu_custom_call" | custom-call | tf_op jit(solution)/shard_map/second_pull/pallas_call | solution.py:595
  113.6 0.7 copy-done.15
  114.3 0.7 copy-done.11
  115.0 3.7 %all-to-all-start.4 = ((f32[32,48,128]{2,1,0:T(8,128)}), f32[32,48,128]{2,1,0:T(8,128)S(1)}, u32[]{:S(2)}, u32[]{:S(2)}) async-start(f32[32,48,128]{2,1,0:T(8,128)} %get-tuple-element.49), calls=%async_computation.4 | async-start | bytes 1572864 | tf_op jit(solution)/shard_map/all_to_all | solution.py:692
  118.7 0.0 copy-start.8
  118.8 1.0 copy-done.8
  119.8 1.0 copy-done.10
  120.8 3.9 %interior_both.1 = (f32[2,512,128]{2,1,0:T(8,128)S(1)}, f32[2,512,128]{2,1,0:T(8,128)S(1)}) custom-call(s32[8]{0:T(128)S(1)} %copy-done.22, f32[2,512,128]{2,1,0:T(8,128)S(1)} %copy-done.10, f32[2,512,128]{2,1,0:T(8,128)S(1)} %copy-done.8), custom_call_target="tpu_custom_call" | custom-call | tf_op jit(solution)/shard_map/interior_both/pallas_call | solution.py:595
  124.7 0.0 copy-start.5
  124.7 0.8 copy-done.5
  125.5 1.5 second_flux.1
  127.0 12.3 %all-to-all-done.4.recv = f32[32,48,128]{2,1,0:T(8,128)S(1)} async-done(((f32[32,48,128]{2,1,0:T(8,128)}), f32[32,48,128]{2,1,0:T(8,128)S(1)}, u32[]{:S(2)}, u32[]{:S(2)}) %all-to-all-start.4) | async-done | bytes 786464 | tf_op jit(solution)/shard_map/all_to_all | solution.py:692
  139.3 0.9 copy-done.12
  140.3 2.1 middle_cot.1
  142.4 19.3 %all_to_all.41.recv = f32[32,32,128]{2,1,0:T(8,128)S(1)} all-to-all(f32[32,32,128]{2,1,0:T(8,128)S(1)} %get-tuple-element.53), channel_id=1, replica_groups=mesh['blk'=32] {'blk'}, dimensions={0} | all-to-all | bytes 1048576 | tf_op jit(solution)/shard_map/all_to_all | solution.py:692
  161.7 4.4 %upward_first.1 = (f32[2,512,128]{2,1,0:T(8,128)S(1)}, f32[2,192,128]{2,1,0:T(8,128)S(1)}, f32[32,16,128]{2,1,0:T(8,128)}) custom-call(s32[8]{0:T(128)S(1)} %copy-done.22, s32[384]{0:T(512)S(1)} %reshape.36.table_s, s32[32]{0:T(128)S(1)} %bitcast.35, s32[8,8]{1,0:T(8,128)S(1)} %copy-done.21, f32[2,512,128]{2,1,0:T(8,128)S(1)} %get-tuple-element.52.inner, ...), custom_call_target="tpu_custom_call" | custom-call | tf_op jit(solution)/shard_map/upward_first/pallas_call | solution.py:595
  166.1 0.7 copy-done.19
  166.8 2.7 %all-to-all-start.6 = ((f32[32,16,128]{2,1,0:T(8,128)}), f32[32,16,128]{2,1,0:T(8,128)S(1)}, u32[]{:S(2)}, u32[]{:S(2)}) async-start(f32[32,16,128]{2,1,0:T(8,128)} %get-tuple-element.57), calls=%async_computation.6 | async-start | bytes 524288 | tf_op jit(solution)/shard_map/all_to_all | solution.py:692
  169.5 3.7 %second_update.1 = (f32[512,256]{1,0:T(8,128)}, f32[128,128]{1,0:T(8,128)S(1)}) custom-call(s32[8]{0:T(128)S(1)} %copy-done.22, s32[384]{0:T(512)S(1)} %reshape.36.table_s, f32[2,512,128]{2,1,0:T(8,128)S(1)} %copy-done.6, f32[2,192,128]{2,1,0:T(8,128)S(1)} %get-tuple-element.59.b_fb, f32[32,32,128]{2,1,0:T(8,128)S(1)} %all_to_all.41.recv, ...), custom_call_target="tpu_custom_call" | custom-call | tf_op jit(solution)/shard_map/second_update/pallas_call | solution.py:595
  173.2 6.9 %all-to-all-done.6.recv = f32[32,16,128]{2,1,0:T(8,128)S(1)} async-done(((f32[32,16,128]{2,1,0:T(8,128)}), f32[32,16,128]{2,1,0:T(8,128)S(1)}, u32[]{:S(2)}, u32[]{:S(2)}) %all-to-all-start.6) | async-done | bytes 262176 | tf_op jit(solution)/shard_map/all_to_all | solution.py:692
  180.1 0.9 copy-done.20
  181.0 4.6 %first_pull.1 = (f32[2,192,128]{2,1,0:T(8,128)S(1)}, f32[32,64,128]{2,1,0:T(8,128)}) custom-call(s32[8]{0:T(128)S(1)} %copy-done.22, s32[32,6]{1,0:T(8,128)S(1)} %bitcast.30, s32[384]{0:T(512)S(1)} %reshape.36.table_s, s32[32]{0:T(128)S(1)} %bitcast.36, f32[2,192,128]{2,1,0:T(8,128)S(1)} %get-tuple-element.35.layers, f32[2,192,128]{2,1,0:T(8,128)S(1)} %copy-done.18, ...), custom_call_target="tpu_custom_call" | custom-call | tf_op jit(solution)/shard_map/first_pull/pallas_call | solution.py:595
  185.7 2.6 %all-to-all-start.7 = ((f32[32,64,128]{2,1,0:T(8,128)}), f32[32,64,128]{2,1,0:T(8,128)S(1)}, u32[]{:S(2)}, u32[]{:S(2)}) async-start(f32[32,64,128]{2,1,0:T(8,128)} %get-tuple-element.62), calls=%async_computation.7 | async-start | bytes 2097152 | tf_op jit(solution)/shard_map/all_to_all | solution.py:692
  188.3 3.7 %interior_back.1.through = f32[2,512,128]{2,1,0:T(8,128)S(1)} custom-call(s32[8]{0:T(128)S(1)} %copy-done.22, f32[2,512,128]{2,1,0:T(8,128)S(1)} %get-tuple-element.34.volume, f32[2,512,128]{2,1,0:T(8,128)S(1)} %get-tuple-element.54.cot), custom_call_target="tpu_custom_call" | custom-call | tf_op jit(solution)/shard_map/interior_back/pallas_call | solution.py:595
  192.0 22.5 %all-to-all-done.7.recv = f32[32,64,128]{2,1,0:T(8,128)S(1)} async-done(((f32[32,64,128]{2,1,0:T(8,128)}), f32[32,64,128]{2,1,0:T(8,128)S(1)}, u32[]{:S(2)}, u32[]{:S(2)}) %all-to-all-start.7) | async-done | bytes 1048608 | tf_op jit(solution)/shard_map/all_to_all | solution.py:692
  214.5 3.0 %last_cot.1 = (f32[512,256]{1,0:T(8,128)}, f32[512,256]{1,0:T(8,128)}) custom-call(s32[32,6]{1,0:T(8,128)S(1)} %bitcast.31, s32[8,8]{1,0:T(8,128)S(1)} %copy-done.21, f32[2,512,128]{2,1,0:T(8,128)S(1)} %interior_back.1.through, f32[2,192,128]{2,1,0:T(8,128)S(1)} %get-tuple-element.61.layer_cot, ...), custom_call_target="tpu_custom_call", output_to_operand_aliasing={{1}: (5, {})} | custom-call | tf_op jit(solution)/shard_map/last_cot/pallas_call | solution.py:595
  (34 shorter events, 0.1 us)
Async XLA Ops:
  1.4 0.7 copy-start.21
  2.1 1.0 copy-start.2
  3.1 1.0 copy-start.4
  7.3 7.7 %copy-start.24 = (s32[8,6,4]{0,2,1:T(4,128)S(1)}, s32[8,6,4]{0,2,1:T(4,128)}, u32[]{:S(2)}) copy-start(s32[8,6,4]{0,2,1:T(4,128)} %param.14) | copy-start | bytes 2308
  7.3 33.8 %all-to-all-start = ((f32[32,64,128]{2,1,0:T(8,128)}), f32[32,64,128]{2,1,0:T(8,128)S(1)}, u32[]{:S(2)}, u32[]{:S(2)}) async-start(f32[32,64,128]{2,1,0:T(8,128)} %get-tuple-element.36), calls=%async_computation | async-start | bytes 2097152 | tf_op jit(solution)/shard_map/all_to_all | solution.py:692
  14.9 0.7 copy-start.25
  15.7 25.3 %copy-start = (bf16[512,128]{1,0:T(8,128)(2,1)S(1)}, bf16[512,128]{1,0:T(8,128)(2,1)}, u32[]{:S(2)}) copy-start(bf16[512,128]{1,0:T(8,128)(2,1)} %constant.44.clone.half_r) | copy-start | bytes 393220
  15.8 25.3 %copy-start.1 = (bf16[128,512]{1,0:T(8,128)(2,1)S(1)}, bf16[128,512]{1,0:T(8,128)(2,1)}, u32[]{:S(2)}) copy-start(bf16[128,512]{1,0:T(8,128)(2,1)} %constant.45.clone.back_r) | copy-start | bytes 393220
  16.1 25.0 %copy-start.22 = (s32[8]{0:T(128)S(1)}, s32[8]{0:T(128)}, u32[]{:S(2)}) copy-start(s32[8]{0:T(128)} %levels_s.21) | copy-start | bytes 100
  43.8 0.7 copy-start.13
  44.5 0.7 copy-start.17
  45.1 14.2 %all-to-all-start.1 = ((f32[32,16,128]{2,1,0:T(8,128)}), f32[32,16,128]{2,1,0:T(8,128)S(1)}, u32[]{:S(2)}, u32[]{:S(2)}) async-start(f32[32,16,128]{2,1,0:T(8,128)} %get-tuple-element.38), calls=%async_computation.1 | async-start | bytes 524288 | tf_op jit(solution)/shard_map/all_to_all | solution.py:692
  48.8 3.5 %copy-start.3 = (f32[8,4,16,256]{3,2,1,0:T(8,128)S(1)}, f32[8,4,16,256]{3,2,1,0:T(8,128)}, u32[]{:S(2)}) copy-start(f32[8,4,16,256]{3,2,1,0:T(8,128)} %param.11) | copy-start | bytes 1572868
  52.3 0.7 copy-start.23
  56.8 0.8 copy-start.7
  59.3 0.9 copy-start.14
  85.0 0.8 copy-start.9
  85.8 23.8 %all-to-all-start.3 = ((f32[32,48,128]{2,1,0:T(8,128)}), f32[32,48,128]{2,1,0:T(8,128)S(1)}, u32[]{:S(2)}, u32[]{:S(2)}) async-start(f32[32,48,128]{2,1,0:T(8,128)} %get-tuple-element.46), calls=%async_computation.3 | async-start | bytes 1572864 | tf_op jit(solution)/shard_map/all_to_all | solution.py:692
  113.6 0.7 copy-start.15
  114.3 0.7 copy-start.11
  115.0 24.3 %all-to-all-start.4 = ((f32[32,48,128]{2,1,0:T(8,128)}), f32[32,48,128]{2,1,0:T(8,128)S(1)}, u32[]{:S(2)}, u32[]{:S(2)}) async-start(f32[32,48,128]{2,1,0:T(8,128)} %get-tuple-element.49), calls=%async_computation.4 | async-start | bytes 1572864 | tf_op jit(solution)/shard_map/all_to_all | solution.py:692
  118.7 1.0 copy-start.8
  119.8 1.0 copy-start.10
  120.8 4.7 %copy-start.16 = (f32[2,192,128]{2,1,0:T(8,128)S(1)}, f32[2,192,128]{2,1,0:T(8,128)}, u32[]{:S(2)}) copy-start(f32[2,192,128]{2,1,0:T(8,128)} %copy-done.15) | copy-start | bytes 589828
  124.7 0.8 copy-start.5
  139.3 0.9 copy-start.12
  166.1 0.7 copy-start.19
  166.8 2.7 %copy-start.6 = (f32[2,512,128]{2,1,0:T(8,128)S(1)}, f32[2,512,128]{2,1,0:T(8,128)}, u32[]{:S(2)}) copy-start(f32[2,512,128]{2,1,0:T(8,128)} %copy-done.5) | copy-start | bytes 1572868
  166.8 13.3 %all-to-all-start.6 = ((f32[32,16,128]{2,1,0:T(8,128)}), f32[32,16,128]{2,1,0:T(8,128)S(1)}, u32[]{:S(2)}, u32[]{:S(2)}) async-start(f32[32,16,128]{2,1,0:T(8,128)} %get-tuple-element.57), calls=%async_computation.6 | async-start | bytes 524288 | tf_op jit(solution)/shard_map/all_to_all | solution.py:692
  169.5 10.6 %copy-start.18 = (f32[2,192,128]{2,1,0:T(8,128)S(1)}, f32[2,192,128]{2,1,0:T(8,128)}, u32[]{:S(2)}) copy-start(f32[2,192,128]{2,1,0:T(8,128)} %copy-done.17) | copy-start | bytes 589828
  180.1 0.9 copy-start.20
  185.7 28.8 %all-to-all-start.7 = ((f32[32,64,128]{2,1,0:T(8,128)}), f32[32,64,128]{2,1,0:T(8,128)S(1)}, u32[]{:S(2)}, u32[]{:S(2)}) async-start(f32[32,64,128]{2,1,0:T(8,128)} %get-tuple-element.62), calls=%async_computation.7 | async-start | bytes 2097152 | tf_op jit(solution)/shard_map/all_to_all | solution.py:692

commit v3 on v2

--- a/solution.py
+++ b/solution.py
@@ -183,9 +183,9 @@
 
     def pack_faces(self, fb, send, out):
         sub = lax.broadcasted_iota(jnp.int32, (8, self.COL), 0)
-
-        def one(peer, carry):
-            for axis in range(3):
+        for axis in range(3):
+
+            def one(peer, carry, axis=axis):
                 slots = [jnp.maximum(send[peer, axis * 2 + side], 0) for side in range(2)]
                 for q in range(2):
                     lo, hi = [
@@ -193,10 +193,11 @@
                         for slot in slots
                     ]
                     row = axis * 16 + q * 8
-                    out[peer, row : row + 8, :] = jnp.where(sub < 4, lo, hi)
-            return carry
-
-        lax.fori_loop(0, self.P, one, 0)
+                    out.ref[peer, row : row + 8, :] = jnp.where(sub < 4, lo, hi)
+                return carry
+
+            lax.fori_loop(0, self.P, one, 0, unroll=4)
+            out.send(axis * 16, 16)
 
     def take_faces(self, packets, send, sums):
         def one(peer, carry):
@@ -331,11 +332,10 @@
         low = self.low(4)
 
         def clear(peer, carry):
-            out[peer, 0:48, :] = jnp.zeros((48, COL), f32)
+            out.ref[peer, 0:48, :] = jnp.zeros((48, COL), f32)
             return carry
 
         lax.fori_loop(0, self.P, clear, 0)
-        rows_all = 3 * S * 8
         for h in range(2):
             for g in range(2):
                 spread = dot2(gb[h, :, :], half_back[:, g * 2 * COL : (g + 1) * 2 * COL])
@@ -343,9 +343,8 @@
                     wide[(h * 2 + g) * 2 + q, :, :] = spread[:, q * COL : (q + 1) * COL]
         both = jnp.concatenate([gb[0, :, :], gb[1, :, :]], axis=1)
         near[...] = 4.0 * dot2(both, half[0 : 2 * COL, :])
-        del rows_all
-        for s in range(S):
-            for f in range(6):
+        for f in range(6):
+            for s in range(S):
                 base = (s * 6 + f) * 8
                 axis, half_row = f // 2, (1 - f % 2) * 4
                 row = (axis * S + s) * 8 + half_row
@@ -355,7 +354,7 @@
                     peer = table[base]
                     for q in range(2):
                         at = axis * 16 + q * 8 + half_row
-                        out[peer, at : at + 4, :] += gb[q, row : row + 4, :]
+                        out.ref[peer, at : at + 4, :] += gb[q, row : row + 4, :]
 
                 def coarse(base=base, axis=axis, half_row=half_row, row=row):
                     peer = table[base]
@@ -363,18 +362,20 @@
                     values = jnp.where(table[base + 6] == 1, roll(values, H), values)
                     for q in range(2):
                         at = axis * 16 + q * 8 + half_row
-                        out[peer, at : at + 4, :] += jnp.where(table[base + 5] == q, values, 0.0)
+                        out.ref[peer, at : at + 4, :] += jnp.where(table[base + 5] == q, values, 0.0)
 
                 def fine(base=base, axis=axis, half_row=half_row, row=row):
                     for k in range(4):
                         peer = table[base + k]
                         for q in range(2):
                             at = axis * 16 + q * 8 + half_row
-                            out[peer, at : at + 4, :] += wide[k * 2 + q, row : row + 4, :]
+                            out.ref[peer, at : at + 4, :] += wide[k * 2 + q, row : row + 4, :]
 
                 pl.when(kind == 0)(same)
                 pl.when(kind == 1)(coarse)
                 pl.when(kind == 2)(fine)
+            if f % 2 == 1:
+                out.send((f // 2) * 16, 16)
 
     def corrected(self, b_fb, packets, row0, table, out):
         H = self.H
@@ -579,28 +580,111 @@
         lax.fori_loop(0, E, one, start)
 
 
+class Arriving:
+    def __init__(self, copies, ref):
+        self.copies = copies
+        self.ref = ref
+        for copy in copies:
+            copy.start()
+
+    def get(self):
+        for copy in self.copies:
+            copy.wait()
+        self.copies = []
+        return self.ref
+
+
+class Leaving:
+    def __init__(self, ref, target, sems):
+        self.ref = ref
+        self.target = target
+        self.sems = sems
+        self.copies = []
+
+    def send(self, first=None, count=None):
+        near, far = self.ref, self.target
+        if count is not None:
+            near = near.at[:, pl.ds(first, count), :]
+            far = far.at[:, pl.ds(first, count), :]
+        copy = pltpu.make_async_copy(near, far, self.sems.at[len(self.copies)])
+        copy.start()
+        self.copies.append(copy)
+
+    def finish(self):
+        for copy in self.copies:
+            copy.wait()
+
+
+class Late:
+    def __init__(self, array, native=False, raw=False):
+        self.array = array
+        self.native = native
+        self.raw = raw
+
+
 def run(body, name, scalars, arrays, outs, scratch, aliases=None):
+    hbm = pltpu.MemorySpace.HBM
     specs = [pl.BlockSpec(memory_space=pltpu.SMEM) for _ in scalars]
     operands = list(scalars)
-    for item in arrays:
-        if isinstance(item, tuple):
-            specs.append(pl.BlockSpec(memory_space=pl.ANY))
-            operands.append(item[0])
+    extra = []
+    arriving, leaving = {}, {}
+    for index, item in enumerate(arrays):
+        if isinstance(item, Late):
+            specs.append(pl.BlockSpec(memory_space=hbm))
+            operands.append(pltpu.with_memory_space_constraint(item.array, hbm))
+            if not item.raw:
+                shape = item.array.shape
+                arriving[index] = (len(extra), item.native)
+                if item.native:
+                    half = (shape[0], shape[1] // 2)
+                    extra += [pltpu.VMEM(half, f32), pltpu.VMEM(half, f32)]
+                    extra.append(pltpu.SemaphoreType.DMA((2,)))
+                else:
+                    extra += [pltpu.VMEM(shape, f32), pltpu.SemaphoreType.DMA((1,))]
         else:
             specs.append(pl.BlockSpec(memory_space=pltpu.VMEM))
             operands.append(item)
-    out_specs = [
-        pl.BlockSpec(memory_space=pl.ANY if native else pltpu.VMEM) for shape, native in outs
-    ]
+    out_specs = []
+    for index, (shape, mode) in enumerate(outs):
+        out_specs.append(pl.BlockSpec(memory_space=hbm if mode else pltpu.VMEM))
+        if mode == "late":
+            leaving[index] = len(extra)
+            extra += [pltpu.VMEM(shape, f32), pltpu.SemaphoreType.DMA((4,))]
+
+    def wrapped(*refs):
+        n_scalar, n_in, n_out = len(scalars), len(arrays), len(outs)
+        scalar_refs = list(refs[:n_scalar])
+        in_refs = list(refs[n_scalar : n_scalar + n_in])
+        out_refs = list(refs[n_scalar + n_in : n_scalar + n_in + n_out])
+        rest = refs[n_scalar + n_in + n_out :]
+        own, late = rest[: len(scratch)], rest[len(scratch) :]
+        for index, (at, native) in arriving.items():
+            if native:
+                planes = [late[at], late[at + 1]]
+                copies = native_copies(planes, in_refs[index], late[at + 2], True)
+                in_refs[index] = Arriving(copies, planes)
+            else:
+                copy = pltpu.make_async_copy(in_refs[index], late[at], late[at + 1].at[0])
+                in_refs[index] = Arriving([copy], late[at])
+        for index, at in leaving.items():
+            out_refs[index] = Leaving(late[at], out_refs[index], late[at + 1])
+        body(*scalar_refs, *in_refs, *out_refs, *own)
+        for index in arriving:
+            in_refs[index].get()
+        for index in leaving:
+            out_refs[index].finish()
+
     return pl.pallas_call(
-        body,
+        wrapped,
         name=name,
         in_specs=specs,
         out_specs=out_specs,
-        out_shape=[jax.ShapeDtypeStruct(shape, f32) for shape, native in outs],
-        scratch_shapes=scratch,
+        out_shape=[
+            hbm(shape, f32) if mode else jax.ShapeDtypeStruct(shape, f32) for shape, mode in outs
+        ],
+        scratch_shapes=list(scratch) + extra,
         input_output_aliases=aliases or {},
-        compiler_params=pltpu.CompilerParams(vmem_limit_bytes=24 * 1024 * 1024),
+        compiler_params=pltpu.CompilerParams(vmem_limit_bytes=32 * 1024 * 1024),
     )(*operands)
 
 
@@ -811,207 +895,230 @@
                 for q in range(2):
                     put(q, x, c, get(q, x, c) + plan.spread(summed, q, x, c))
 
-    def first_pack(send_s, parents_s, fields_r, guide_r, volume, layers, packets, fb, f0, f1, g0,
-                   g1, f_sems, g_sems):
-        inward = native_copies([f0, f1], fields_r, f_sems, True)
-        guided = native_copies([g0, g1], guide_r, g_sems, True)
-        for copy in inward + guided:
-            copy.start()
-        for copy in inward:
-            copy.wait()
-        get = plan.native_at([f0, f1])
+    def first_pack(send_s, parents_s, fields_r, guide_r, volume, layers, packets, fb):
+        get = plan.native_at(fields_r.get())
         for x in range(E):
             for c in range(4):
                 for q in range(2):
-                    volume[q, (x * 4 + c) * S : (x * 4 + c + 1) * S, :] = get(q, x, c)
-        layers_of(plan.slab_at(volume), fb, layers)
+                    volume.ref[q, (x * 4 + c) * S : (x * 4 + c + 1) * S, :] = get(q, x, c)
+        volume.send()
+        layers_of(plan.slab_at(volume.ref), fb, layers.ref)
+        layers.send()
         plan.pack_faces(fb, send_s, packets)
-        for copy in guided:
-            copy.wait()
-        planes = [g0, g1]
-        plan.pack_octants(lambda s, x, q: planes[q][plan.native_rows(s, x), :], parents_s, packets, 48)
+        planes = guide_r.get()
+        plan.pack_octants(
+            lambda s, x, q: planes[q][plan.native_rows(s, x), :], parents_s, packets.ref, 48
+        )
+        packets.send(48, 16)
 
     volume1, layers1, packets = run(
         first_pack,
         "first_pack",
         [send, parents],
-        [(native_fields,), (native_guidance,)],
-        [(plan.slab, False), (plan.ff, False), ((peers, 64, COL), False)],
-        [fb_scratch] + native_planes + native_planes + [pair_of_sems, pair_of_sems],
+        [Late(native_fields, native=True), Late(native_guidance, native=True)],
+        [(plan.slab, "late"), (plan.ff, "late"), ((peers, 64, COL), "late")],
+        [fb_scratch],
     )
     received1 = exchange(packets)
 
-    def interior_first(levels_s, volume, partial):
-        plan.interior(dyn_get(volume), levels_s, dyn_put(partial))
-
-    (partial1,) = run(interior_first, "interior_first", [levels], [volume1], [(plan.slab, False)], [])
-
-    def first_flux(levels_s, send_s, table_s, layers, recv, half_r, back_r, gb, b_fb, packets,
+    def interior_first(levels_s, volume, partial, done):
+        plan.interior(dyn_get(volume.get()), levels_s, dyn_put(partial.ref))
+        partial.send()
+        done[...] = jnp.zeros(done.shape, f32)
+
+    partial1, done1 = run(
+        interior_first, "interior_first", [levels], [Late(volume1)],
+        [(plan.slab, "late"), ((8, COL), None)], [],
+    )
+
+    def first_flux(levels_s, send_s, table_s, layers, after, recv, half_r, back_r, gb, b_fb, packets,
                    planes, near, kinds, ff, rb):
-        plan.ghosts(recv, table_s, planes, near, kinds, gb, half_r, back_r)
-        layer = plan.ff_at(layers)
-        boundary_fluxes(plan, layer, ghost_reader(gb, layer, levels_s), flux_emitter(b_fb, ff))
+        del after
+        plan.ghosts(recv, table_s, planes, near, kinds, gb.ref, half_r, back_r)
+        gb.send()
+        layer = plan.ff_at(layers.get())
+        boundary_fluxes(plan, layer, ghost_reader(gb.ref, layer, levels_s), flux_emitter(b_fb.ref, ff))
+        b_fb.send()
         plan.pack_averages(plan.ff_at(ff), rb, send_s, packets, 0, half_r)
 
     ghosts1, fluxes1, packets = run(
         first_flux,
         "first_flux",
         [levels, send, table],
-        [layers1, received1, half, half_back],
-        [(plan.fb, False), (plan.fb, False), ((peers, 16, COL), False)],
+        [Late(layers1), done1, received1, half, half_back],
+        [(plan.fb, "late"), (plan.fb, "late"), ((peers, 16, COL), None)],
         ghost_scratch + [vm(*plan.ff), vm(*plan.coarse)],
     )
     received2 = exchange(packets)
 
     def upward_second(levels_s, table_s, children_s, parents_s, guide_r, recv, back_r, up, cot_fb,
-                      packets, cc, g0, g1, sems):
-        guided = native_copies([g0, g1], guide_r, sems, True)
-        for copy in guided:
-            copy.start()
-        for copy in guided:
-            copy.wait()
-        plan.upward(recv, 48, cc, children_s, parents_s, plan.native_at([g0, g1]), slab_put(up), back_r)
-        corrected_cot_of(plan.slab_at(up), levels_s, cot_fb)
-        plan.pack_quarters(cot_fb, table_s, packets, 0)
+                      packets, cc):
+        planes = guide_r.get()
+        plan.upward(recv, 48, cc, children_s, parents_s, plan.native_at(planes), slab_put(up.ref), back_r)
+        up.send()
+        corrected_cot_of(plan.slab_at(up.ref), levels_s, cot_fb.ref)
+        cot_fb.send()
+        plan.pack_quarters(cot_fb.ref, table_s, packets.ref, 0)
+        packets.send()
 
     up2, corrcot2, quarters2 = run(
         upward_second,
         "upward_second",
         [levels, table, children, parents],
-        [(native_guidance,), received1, half_back],
-        [(plan.slab, False), (plan.fb, False), ((peers, 16, COL), False)],
-        [vm((S + 1) * 16, COL)] + native_planes + [pair_of_sems],
+        [Late(native_guidance, native=True), received1, half_back],
+        [(plan.slab, "late"), (plan.fb, "late"), ((peers, 16, COL), "late")],
+        [vm((S + 1) * 16, COL)],
     )
 
     def first_update(levels_s, table_s, children_s, partial, b_fb, recv, quarters, half_r, updated,
                      packets, corr, cb):
-        plan.corrected(b_fb, recv, 0, table_s, corr)
-        finished(partial, corr, levels_s, slab_put(updated))
-        plan.average_blocks(plan.slab_at(updated), cb, half_r)
+        plan.corrected(b_fb.get(), recv, 0, table_s, corr)
+        finished(partial.get(), corr, levels_s, slab_put(updated.ref))
+        updated.send()
+        plan.average_blocks(plan.slab_at(updated.ref), cb, half_r)
         plan.pack_children(cb, children_s, packets, 0)
-        carry_packets(quarters, packets, 16)
+        carry_packets(quarters.get(), packets, 16)
 
     updated1, packets = run(
         first_update,
         "first_update",
         [levels, table, children],
-        [partial1, fluxes1, received2, quarters2, half],
-        [(plan.slab, False), ((peers, 32, COL), False)],
+        [Late(partial1), Late(fluxes1), received2, Late(quarters2), half],
+        [(plan.slab, "late"), ((peers, 32, COL), None)],
         [fb_scratch, vm(*plan.coarse)],
     )
     received3 = exchange(packets)
 
-    def middle_pack(send_s, parents_s, updated, recv, volume, layers, packets, fb):
-        volume[...] = updated[...]
+    def middle_pack(send_s, parents_s, updated, recv, volume, layers, packets, fb, sems):
+        copy = pltpu.make_async_copy(updated, volume.ref, sems.at[0])
+        copy.start()
+        copy.wait()
 
         def store(s, x, q, value):
-            volume[q, plan.slab_rows(s, x), :] = value
+            volume.ref[q, plan.slab_rows(s, x), :] = value
 
         plan.place_octants(recv, 0, parents_s, store)
-        layers_of(plan.slab_at(volume), fb, layers)
+        volume.send()
+        layers_of(plan.slab_at(volume.ref), fb, layers.ref)
+        layers.send()
         plan.pack_faces(fb, send_s, packets)
 
     volume2, layers2, packets = run(
         middle_pack,
         "middle_pack",
         [send, parents],
-        [updated1, received3],
-        [(plan.slab, False), (plan.ff, False), ((peers, 48, COL), False)],
-        [fb_scratch],
+        [Late(updated1, raw=True), received3],
+        [(plan.slab, "late"), (plan.ff, "late"), ((peers, 48, COL), "late")],
+        [fb_scratch, pair_of_sems],
     )
     received4 = exchange(packets)
 
     def flux_cot_second(send_s, table_s, cot_fb, recv, back_r, flux_cot, kinds, *sums):
-        flux_cot_of(recv, 16, cot_fb, table_s, send_s, sums, kinds, flux_cot, back_r)
+        flux_cot_of(recv, 16, cot_fb.get(), table_s, send_s, sums, kinds, flux_cot.ref, back_r)
+        flux_cot.send()
 
     (fluxcot2,) = run(
         flux_cot_second,
         "flux_cot_second",
         [send, table],
-        [corrcot2, received3, half_back],
-        [(plan.ff, False)],
+        [Late(corrcot2), received3, half_back],
+        [(plan.ff, "late")],
         [kind_scratch] + quarter_sums,
     )
 
     def interior_both(levels_s, volume, cot, partial, through):
-        plan.interior(dyn_get(volume), levels_s, dyn_put(partial), dyn_get(cot), dyn_put(through))
+        plan.interior(
+            dyn_get(volume.get()), levels_s, dyn_put(partial.ref), dyn_get(cot.get()), dyn_put(through.ref)
+        )
+        partial.send()
+        through.send()
 
     partial2, through2 = run(
-        interior_both, "interior_both", [levels], [volume2, up2],
-        [(plan.slab, False), (plan.slab, False)], [],
+        interior_both, "interior_both", [levels], [Late(volume2), Late(up2)],
+        [(plan.slab, "late"), (plan.slab, "late")], [],
     )
 
     def second_pull(levels_s, table_s, layers, recv, flux_cot, half_r, back_r, gb, layer_cot,
                     packets, planes, near, kinds, gcot):
-        plan.ghosts(recv, table_s, planes, near, kinds, gb, half_r, back_r)
-        layer = plan.ff_at(layers)
+        plan.ghosts(recv, table_s, planes, near, kinds, gb.ref, half_r, back_r)
+        gb.send()
+        layer = plan.ff_at(layers.get())
         boundary_pull(
-            plan, layer, ghost_reader(gb, layer, levels_s), plan.ff_at(flux_cot),
-            cot_emitter(layer_cot, gcot),
+            plan, layer, ghost_reader(gb.ref, layer, levels_s), plan.ff_at(flux_cot.get()),
+            cot_emitter(layer_cot.ref, gcot),
         )
+        layer_cot.send()
         plan.pack_ghost_cot(gcot, table_s, planes, near, packets, half_r, back_r)
 
     ghosts2, layercot2, packets = run(
         second_pull,
         "second_pull",
         [levels, table],
-        [layers2, received4, fluxcot2, half, half_back],
-        [(plan.fb, False), (plan.ff, False), ((peers, 48, COL), False)],
+        [Late(layers2), received4, Late(fluxcot2), half, half_back],
+        [(plan.fb, "late"), (plan.ff, "late"), ((peers, 48, COL), "late")],
         ghost_scratch + [fb_scratch],
     )
     received5 = exchange(packets)
 
     def second_flux(levels_s, send_s, layers, gb, half_r, b_fb, packets, ff, rb):
-        layer = plan.ff_at(layers)
-        boundary_fluxes(plan, layer, ghost_reader(gb, layer, levels_s), flux_emitter(b_fb, ff))
-        plan.pack_averages(plan.ff_at(ff), rb, send_s, packets, 0, half_r)
+        layer = plan.ff_at(layers.get())
+        boundary_fluxes(plan, layer, ghost_reader(gb.get(), layer, levels_s), flux_emitter(b_fb.ref, ff))
+        b_fb.send()
+        plan.pack_averages(plan.ff_at(ff), rb, send_s, packets.ref, 0, half_r)
+        packets.send()
 
     fluxes2, averages2 = run(
         second_flux,
         "second_flux",
         [levels, send],
-        [layers2, ghosts2, half],
-        [(plan.fb, False), ((peers, 16, COL), False)],
+        [Late(layers2), Late(ghosts2), half],
+        [(plan.fb, "late"), ((peers, 16, COL), "late")],
         [vm(*plan.ff), vm(*plan.coarse)],
     )
 
     def middle_cot(send_s, parents_s, through, layer_cot, recv, averages, inner, packets, total, *sums):
         plan.take_faces(recv, send_s, sums)
-        add_layers(through, layer_cot, total, sums, slab_put(inner))
+        carry_packets(averages.get(), packets, 16)
+        add_layers(through.get(), layer_cot.get(), total, sums, slab_put(inner.ref))
+        inner.send()
         plan.pack_octants(
-            lambda s, x, q: inner[q, plan.slab_rows(s, x), :], parents_s, packets, 0
+            lambda s, x, q: inner.ref[q, plan.slab_rows(s, x), :], parents_s, packets, 0
         )
-        carry_packets(averages, packets, 16)
 
     inner_cot, packets = run(
         middle_cot,
         "middle_cot",
         [send, parents],
-        [through2, layercot2, received5, averages2],
-        [(plan.slab, False), ((peers, 32, COL), False)],
+        [Late(through2), Late(layercot2), received5, Late(averages2)],
+        [(plan.slab, "late"), ((peers, 32, COL), None)],
         [vm(*plan.ff)] + face_sums,
     )
     received6 = exchange(packets)
 
     def upward_first(levels_s, table_s, children_s, parents_s, inner, recv, back_r, up, cot_fb,
                      packets, cc):
-        plan.upward(recv, 0, cc, children_s, parents_s, plan.slab_at(inner), slab_put(up), back_r)
-        corrected_cot_of(plan.slab_at(up), levels_s, cot_fb)
-        plan.pack_quarters(cot_fb, table_s, packets, 0)
+        plan.upward(
+            recv, 0, cc, children_s, parents_s, lambda q, x, c: plan.slab_at(inner.get())(q, x, c),
+            slab_put(up.ref), back_r,
+        )
+        up.send()
+        corrected_cot_of(plan.slab_at(up.ref), levels_s, cot_fb.ref)
+        cot_fb.send()
+        plan.pack_quarters(cot_fb.ref, table_s, packets, 0)
 
     up1, corrcot1, packets = run(
         upward_first,
         "upward_first",
         [levels, table, children, parents],
-        [inner_cot, received6, half_back],
-        [(plan.slab, False), (plan.fb, False), ((peers, 16, COL), False)],
+        [Late(inner_cot), received6, half_back],
+        [(plan.slab, "late"), (plan.fb, "late"), ((peers, 16, COL), None)],
         [vm((S + 1) * 16, COL)],
     )
     received7 = exchange(packets)
 
     def second_update(levels_s, table_s, partial, b_fb, recv, half_r, final, cb, corr, updated, n0,
                       n1, sems):
-        plan.corrected(b_fb, recv, 16, table_s, corr)
+        plan.corrected(b_fb.get(), recv, 16, table_s, corr)
         planes = [n0, n1]
         put_slab = slab_put(updated)
 
@@ -1019,7 +1126,7 @@
             put_slab(q, x, c, value)
             planes[q][pl.ds(c * E + x, S, stride=4 * E), :] = value
 
-        finished(partial, corr, levels_s, put)
+        finished(partial.get(), corr, levels_s, put)
         copies = native_copies(planes, final, sems, False)
         for copy in copies:
             copy.start()
@@ -1031,43 +1138,48 @@
         second_update,
         "second_update",
         [levels, table],
-        [partial2, fluxes2, received6, half],
-        [(plan.native, True), (plan.coarse, False)],
+        [Late(partial2), Late(fluxes2), received6, half],
+        [(plan.native, "raw"), (plan.coarse, None)],
         [fb_scratch, vm(*plan.slab)] + native_planes + [pair_of_sems],
     )
 
     def interior_back(levels_s, volume, cot, through):
-        plan.interior(dyn_get(volume), levels_s, None, dyn_get(cot), dyn_put(through))
+        plan.interior(
+            dyn_get(volume.get()), levels_s, None, dyn_get(cot.get()), dyn_put(through.ref)
+        )
+        through.send()
 
     (through1,) = run(
-        interior_back, "interior_back", [levels], [volume1, up1], [(plan.slab, False)], []
+        interior_back, "interior_back", [levels], [Late(volume1), Late(up1)],
+        [(plan.slab, "late")], [],
     )
 
     def first_pull(levels_s, send_s, table_s, children_s, layers, gb, cot_fb, recv, coarse, half_r,
                    back_r, layer_cot, packets, planes, near, kinds, flux_cot, gcot, *sums):
-        plan.pack_children(coarse, children_s, packets, 48)
-        flux_cot_of(recv, 0, cot_fb, table_s, send_s, sums, kinds, flux_cot, back_r)
-        layer = plan.ff_at(layers)
+        plan.pack_children(coarse, children_s, packets.ref, 48)
+        packets.send(48, 16)
+        flux_cot_of(recv, 0, cot_fb.get(), table_s, send_s, sums, kinds, flux_cot, back_r)
+        layer = plan.ff_at(layers.get())
         boundary_pull(
-            plan, layer, ghost_reader(gb, layer, levels_s), plan.ff_at(flux_cot),
-            cot_emitter(layer_cot, gcot),
+            plan, layer, ghost_reader(gb.get(), layer, levels_s), plan.ff_at(flux_cot),
+            cot_emitter(layer_cot.ref, gcot),
         )
+        layer_cot.send()
         plan.pack_ghost_cot(gcot, table_s, planes, near, packets, half_r, back_r)
 
     layercot1, packets = run(
         first_pull,
         "first_pull",
         [levels, send, table, children],
-        [layers1, ghosts1, corrcot1, received7, coarse2, half, half_back],
-        [(plan.ff, False), ((peers, 64, COL), False)],
+        [Late(layers1), Late(ghosts1), Late(corrcot1), received7, coarse2, half, half_back],
+        [(plan.ff, "late"), ((peers, 64, COL), "late")],
         ghost_scratch + [vm(*plan.ff), fb_scratch] + quarter_sums,
     )
     received8 = exchange(packets)
 
     def last_cot(send_s, parents_s, through, layer_cot, recv, open_r, gradient, final, total, n0, n1,
-                 p0, p1, sems, *late):
+                 p0, p1, sems, slot_sems, *sums):
         del open_r
-        slot_sems, sums = late[0], late[1:]
         placed = [p0, p1]
 
         def store(s, x, q, value):
@@ -1092,7 +1204,7 @@
         def put(q, x, c, value):
             planes[q][pl.ds(c * E + x, S, stride=4 * E), :] = value
 
-        add_layers(through, layer_cot, total, sums, put)
+        add_layers(through.get(), layer_cot.get(), total, sums, put)
         copies = native_copies(planes, gradient, sems, False)
         for copy in copies:
             copy.start()
@@ -1104,8 +1216,8 @@
         last_cot,
         "last_cot",
         [send, parents],
-        [through1, layercot1, received8, (final_open,)],
-        [(plan.native, True), (plan.native, True)],
+        [Late(through1), Late(layercot1), received8, Late(final_open, raw=True)],
+        [(plan.native, "raw"), (plan.native, "raw")],
         [vm(*plan.ff)] + native_planes + native_planes
         + [pair_of_sems, pltpu.SemaphoreType.DMA((S, 2))] + face_sums,
         aliases={5: 1},

time: 219 us -> 217 us (level)
  Pallas kernels: 51.7 us -> 74.9 us
  local copies, waits for them, and re-layouts: 15.8 us -> 3.79 us
  waiting for transfers between devices: 87.5 us -> 77.5 us
    pallas_call x16, Pallas kernels: 51.7 us -> 74.9 us  [run(): pl.pallas_call(wrapped, name=name, in_specs=specs, out_specs=out_specs, o...]
    unnamed x55 -> x17, local copies, waits for them, and re-layouts: 15.6 us -> 3.57 us
    all_to_all x6, waiting for transfers between devices: 87.5 us -> 77.5 us  [exchange(): lax.all_to_all(packets, 'blk', split_axis=0, concat_axis=0, tiled=True)]
  transfers between devices with their start and end apart: 6 -> 6, of which waited for: 6 -> 6; matrix products, arithmetic and copies ran while one was open for 0% -> 0% of each run, Pallas kernels for 10% -> 16%
where the time goes in v3:
time: 217 us; the launch traced here: 215 us
  waiting for transfers between devices  77.5 us (36%)
  Pallas kernels  74.9 us (35%)
  blocking collectives  36.4 us (17%)
  starting transfers between devices  21.8 us (10%)
  local copies, waits for them, and re-layouts  3.79 us (2%)
    all_to_all x6, waiting for transfers between devices, exchange(): lax.all_to_all(packets, 'blk', split_axis=0, concat_axis=0, tiled=True)  77.5 us
    pallas_call x16, Pallas kernels, run(): pl.pallas_call(wrapped, name=name, in_specs=specs, out_specs=out_specs, o...  74.9 us
    all_to_all x2, blocking collectives, exchange(): lax.all_to_all(packets, 'blk', split_axis=0, concat_axis=0, tiled=True)  36.4 us
    all_to_all x6, starting transfers between devices, exchange(): lax.all_to_all(packets, 'blk', split_axis=0, concat_axis=0, tiled=True)  21.8 us
  transfers between devices with their start and end apart: 6, of which 6 were waited for; matrix products, arithmetic and copies ran while one was open for 0% of the time, Pallas kernels for 16%

profile of v3, /device:TPU:0, one launch (start us, length us, event | category | flops | bytes accessed | tf_op | source)
XLA Modules:
  0.0 215.5 jit_solution(1005391578103193073)
XLA Ops:
  0.6 0.8 copy.21
  1.4 0.0 copy-start.2
  1.4 0.7 copy-done.2
  2.1 4.3 %first_pack.1 = (f32[2,512,128]{2,1,0:T(8,128)}, f32[2,192,128]{2,1,0:T(8,128)}, f32[32,64,128]{2,1,0:T(8,128)}) custom-call(s32[32,6]{1,0:T(8,128)S(1)} %bitcast.22, s32[8,8]{1,0:T(8,128)S(1)} %copy-done.2, f32[512,256]{1,0:T(8,128)} %bitcast.36, f32[512,256]{1,0:T(8,128)} %bitcast.34), custom_call_target="tpu_custom_call" | custom-call | tf_op jit(solution)/shard_map/first_pack/pallas_call | solution.py:677
  6.3 0.0 copy-start.5
  6.4 7.0 %all-to-all-start = ((f32[32,64,128]{2,1,0:T(8,128)}), f32[32,64,128]{2,1,0:T(8,128)S(1)}, u32[]{:S(2)}, u32[]{:S(2)}) async-start(f32[32,64,128]{2,1,0:T(8,128)} %get-tuple-element.40), calls=%async_computation | async-start | bytes 2097152 | tf_op jit(solution)/shard_map/all_to_all | solution.py:776
  13.4 0.0 copy-done.5
  13.4 0.0 copy-start.6
  13.4 0.1 copy.22
  13.5 0.6 copy-done.6
  14.1 0.1 copy.23
  14.4 0.1 copy.29
  14.5 0.1 reshape.36.refs_2_.refs_1_
  14.6 0.0 copy-start.3
  14.6 0.6 copy-done.3
  15.3 0.0 copy-start
  15.3 0.0 copy-start.1
  15.3 5.4 %interior_first.1 = (f32[2,512,128]{2,1,0:T(8,128)}, f32[8,128]{1,0:T(8,128)S(1)}) custom-call(s32[8]{0:T(128)S(1)} %copy-done.3, f32[2,512,128]{2,1,0:T(8,128)} %get-tuple-element.36.refs_1_), custom_call_target="tpu_custom_call" | custom-call | tf_op jit(solution)/shard_map/interior_first/pallas_call | solution.py:677
  20.7 18.9 %all-to-all-done.refs_5_ = f32[32,64,128]{2,1,0:T(8,128)S(1)} async-done(((f32[32,64,128]{2,1,0:T(8,128)}), f32[32,64,128]{2,1,0:T(8,128)S(1)}, u32[]{:S(2)}, u32[]{:S(2)}) %all-to-all-start) | async-done | bytes 1048608 | tf_op jit(solution)/shard_map/all_to_all | solution.py:776
  39.6 0.0 copy-done
  39.6 0.0 copy-done.1
  39.6 3.8 %first_flux.1 = (f32[2,192,128]{2,1,0:T(8,128)}, f32[2,192,128]{2,1,0:T(8,128)}, f32[32,16,128]{2,1,0:T(8,128)}) custom-call(s32[8]{0:T(128)S(1)} %copy-done.3, s32[32,6]{1,0:T(8,128)S(1)} %bitcast.23, s32[384]{0:T(512)S(1)} %reshape.36.refs_2_.refs_1_, f32[2,192,128]{2,1,0:T(8,128)} %get-tuple-element.38.refs_3_.refs_4_, ...), custom_call_target="tpu_custom_call" | custom-call | tf_op jit(solution)/shard_map/first_flux/pallas_call | solution.py:677
  43.4 3.6 %all-to-all-start.1 = ((f32[32,16,128]{2,1,0:T(8,128)}), f32[32,16,128]{2,1,0:T(8,128)S(1)}, u32[]{:S(2)}, u32[]{:S(2)}) async-start(f32[32,16,128]{2,1,0:T(8,128)} %get-tuple-element.42), calls=%async_computation.1 | async-start | bytes 524288 | tf_op jit(solution)/shard_map/all_to_all | solution.py:776
  47.1 0.0 copy-start.4
  47.1 0.6 copy-done.4
  47.7 5.8 %upward_second.1 = (f32[2,512,128]{2,1,0:T(8,128)}, f32[2,192,128]{2,1,0:T(8,128)}, f32[32,16,128]{2,1,0:T(8,128)}) custom-call(s32[8]{0:T(128)S(1)} %copy-done.3, s32[384]{0:T(512)S(1)} %reshape.36.refs_2_.refs_1_, s32[32]{0:T(128)S(1)} %bitcast.30, s32[8,8]{1,0:T(8,128)S(1)} %copy-done.2, f32[512,256]{1,0:T(8,128)} %bitcast.35, ...), custom_call_target="tpu_custom_call" | custom-call | tf_op jit(solution)/shard_map/upward_second/pallas_call | solution.py:677
  53.5 4.1 %all-to-all-done.1.refs_5_ = f32[32,16,128]{2,1,0:T(8,128)S(1)} async-done(((f32[32,16,128]{2,1,0:T(8,128)}), f32[32,16,128]{2,1,0:T(8,128)S(1)}, u32[]{:S(2)}, u32[]{:S(2)}) %all-to-all-start.1) | async-done | bytes 262176 | tf_op jit(solution)/shard_map/all_to_all | solution.py:776
  57.6 4.9 %first_update.1 = (f32[2,512,128]{2,1,0:T(8,128)}, f32[32,32,128]{2,1,0:T(8,128)S(1)}) custom-call(s32[8]{0:T(128)S(1)} %copy-done.3, s32[384]{0:T(512)S(1)} %reshape.36.refs_2_.refs_1_, s32[32]{0:T(128)S(1)} %bitcast.31, f32[2,512,128]{2,1,0:T(8,128)} %get-tuple-element.37.refs_3_, f32[2,192,128]{2,1,0:T(8,128)} %get-tuple-element.41.refs_4_, ...), custom_call_target="tpu_custom_call" | custom-call | tf_op jit(solution)/shard_map/first_update/pallas_call | solution.py:677
  62.6 17.3 %all_to_all.40.refs_3_ = f32[32,32,128]{2,1,0:T(8,128)S(1)} all-to-all(f32[32,32,128]{2,1,0:T(8,128)S(1)} %get-tuple-element.45), channel_id=1, replica_groups=mesh['blk'=32] {'blk'}, dimensions={0} | all-to-all | bytes 1048576 | tf_op jit(solution)/shard_map/all_to_all | solution.py:776
  79.9 4.1 %middle_pack.1 = (f32[2,512,128]{2,1,0:T(8,128)}, f32[2,192,128]{2,1,0:T(8,128)}, f32[32,48,128]{2,1,0:T(8,128)}) custom-call(s32[32,6]{1,0:T(8,128)S(1)} %bitcast.24, s32[8,8]{1,0:T(8,128)S(1)} %copy-done.2, f32[2,512,128]{2,1,0:T(8,128)} %get-tuple-element.44.refs_2_, f32[32,32,128]{2,1,0:T(8,128)S(1)} %all_to_all.40.refs_3_), custom_call_target="tpu_custom_call" | custom-call | tf_op jit(solution)/shard_map/middle_pack/pallas_call | solution.py:677
  84.0 2.7 %all-to-all-start.3 = ((f32[32,48,128]{2,1,0:T(8,128)}), f32[32,48,128]{2,1,0:T(8,128)S(1)}, u32[]{:S(2)}, u32[]{:S(2)}) async-start(f32[32,48,128]{2,1,0:T(8,128)} %get-tuple-element.50), calls=%async_computation.3 | async-start | bytes 1572864 | tf_op jit(solution)/shard_map/all_to_all | solution.py:776
  86.7 3.2 %flux_cot_second.1.refs_4_ = f32[2,192,128]{2,1,0:T(8,128)} custom-call(s32[32,6]{1,0:T(8,128)S(1)} %bitcast.25, s32[384]{0:T(512)S(1)} %reshape.36.refs_2_.refs_1_, f32[2,192,128]{2,1,0:T(8,128)} %get-tuple-element.51.refs_2_, f32[32,32,128]{2,1,0:T(8,128)S(1)} %all_to_all.40.refs_3_, bf16[128,512]{1,0:T(8,128)(2,1)S(1)} %copy-done.1), custom_call_target="tpu_custom_call" | custom-call | tf_op jit(solution)/shard_map/flux_cot_second/pallas_call | solution.py:677
  89.8 17.4 %all-to-all-done.3.refs_3_ = f32[32,48,128]{2,1,0:T(8,128)S(1)} async-done(((f32[32,48,128]{2,1,0:T(8,128)}), f32[32,48,128]{2,1,0:T(8,128)S(1)}, u32[]{:S(2)}, u32[]{:S(2)}) %all-to-all-start.3) | async-done | bytes 786464 | tf_op jit(solution)/shard_map/all_to_all | solution.py:776
  107.2 5.1 %second_pull.1 = (f32[2,192,128]{2,1,0:T(8,128)}, f32[2,192,128]{2,1,0:T(8,128)}, f32[32,48,128]{2,1,0:T(8,128)}) custom-call(s32[8]{0:T(128)S(1)} %copy-done.3, s32[384]{0:T(512)S(1)} %reshape.36.refs_2_.refs_1_, f32[2,192,128]{2,1,0:T(8,128)} %get-tuple-element.49.refs_2_, f32[32,48,128]{2,1,0:T(8,128)S(1)} %all-to-all-done.3.refs_3_, ...), custom_call_target="tpu_custom_call" | custom-call | tf_op jit(solution)/shard_map/second_pull/pallas_call | solution.py:677
  112.4 3.2 %all-to-all-start.4 = ((f32[32,48,128]{2,1,0:T(8,128)}), f32[32,48,128]{2,1,0:T(8,128)S(1)}, u32[]{:S(2)}, u32[]{:S(2)}) async-start(f32[32,48,128]{2,1,0:T(8,128)} %get-tuple-element.53), calls=%async_computation.4 | async-start | bytes 1572864 | tf_op jit(solution)/shard_map/all_to_all | solution.py:776
  115.6 6.1 %interior_both.1 = (f32[2,512,128]{2,1,0:T(8,128)}, f32[2,512,128]{2,1,0:T(8,128)}) custom-call(s32[8]{0:T(128)S(1)} %copy-done.3, f32[2,512,128]{2,1,0:T(8,128)} %get-tuple-element.46.refs_1_, f32[2,512,128]{2,1,0:T(8,128)} %get-tuple-element.47.refs_2_), custom_call_target="tpu_custom_call" | custom-call | tf_op jit(solution)/shard_map/interior_both/pallas_call | solution.py:677
  121.7 3.3 %second_flux.1 = (f32[2,192,128]{2,1,0:T(8,128)}, f32[32,16,128]{2,1,0:T(8,128)}) custom-call(s32[8]{0:T(128)S(1)} %copy-done.3, s32[32,6]{1,0:T(8,128)S(1)} %bitcast.26, f32[2,192,128]{2,1,0:T(8,128)} %get-tuple-element.49.refs_2_, f32[2,192,128]{2,1,0:T(8,128)} %get-tuple-element.54.refs_3_, bf16[512,128]{1,0:T(8,128)(2,1)S(1)} %copy-done), custom_call_target="tpu_custom_call" | custom-call | tf_op jit(solution)/shard_map/second_flux/pallas_call | solution.py:677
  125.1 11.1 %all-to-all-done.4.refs_4_ = f32[32,48,128]{2,1,0:T(8,128)S(1)} async-done(((f32[32,48,128]{2,1,0:T(8,128)}), f32[32,48,128]{2,1,0:T(8,128)S(1)}, u32[]{:S(2)}, u32[]{:S(2)}) %all-to-all-start.4) | async-done | bytes 786464 | tf_op jit(solution)/shard_map/all_to_all | solution.py:776
  136.2 3.5 %middle_cot.1 = (f32[2,512,128]{2,1,0:T(8,128)}, f32[32,32,128]{2,1,0:T(8,128)S(1)}) custom-call(s32[32,6]{1,0:T(8,128)S(1)} %bitcast.27, s32[8,8]{1,0:T(8,128)S(1)} %copy-done.2, f32[2,512,128]{2,1,0:T(8,128)} %get-tuple-element.48.refs_2_, f32[2,192,128]{2,1,0:T(8,128)} %get-tuple-element.52.refs_3_, f32[32,48,128]{2,1,0:T(8,128)S(1)} %all-to-all-done.4.refs_4_, ...), custom_call_target="tpu_custom_call" | custom-call | tf_op jit(solution)/shard_map/middle_cot/pallas_call | solution.py:677
  139.7 19.0 %all_to_all.41.refs_5_.refs_4_ = f32[32,32,128]{2,1,0:T(8,128)S(1)} all-to-all(f32[32,32,128]{2,1,0:T(8,128)S(1)} %get-tuple-element.57), channel_id=1, replica_groups=mesh['blk'=32] {'blk'}, dimensions={0} | all-to-all | bytes 1048576 | tf_op jit(solution)/shard_map/all_to_all | solution.py:776
  158.7 5.3 %upward_first.1 = (f32[2,512,128]{2,1,0:T(8,128)}, f32[2,192,128]{2,1,0:T(8,128)}, f32[32,16,128]{2,1,0:T(8,128)}) custom-call(s32[8]{0:T(128)S(1)} %copy-done.3, s32[384]{0:T(512)S(1)} %reshape.36.refs_2_.refs_1_, s32[32]{0:T(128)S(1)} %bitcast.32, s32[8,8]{1,0:T(8,128)S(1)} %copy-done.2, f32[2,512,128]{2,1,0:T(8,128)} %get-tuple-element.56.refs_4_, ...), custom_call_target="tpu_custom_call" | custom-call | tf_op jit(solution)/shard_map/upward_first/pallas_call | solution.py:677
  164.0 2.6 %all-to-all-start.6 = ((f32[32,16,128]{2,1,0:T(8,128)}), f32[32,16,128]{2,1,0:T(8,128)S(1)}, u32[]{:S(2)}, u32[]{:S(2)}) async-start(f32[32,16,128]{2,1,0:T(8,128)} %get-tuple-element.61), calls=%async_computation.6 | async-start | bytes 524288 | tf_op jit(solution)/shard_map/all_to_all | solution.py:776
  166.6 5.0 %second_update.1 = (f32[512,256]{1,0:T(8,128)}, f32[128,128]{1,0:T(8,128)S(1)}) custom-call(s32[8]{0:T(128)S(1)} %copy-done.3, s32[384]{0:T(512)S(1)} %reshape.36.refs_2_.refs_1_, f32[2,512,128]{2,1,0:T(8,128)} %get-tuple-element.62.refs_2_, f32[2,192,128]{2,1,0:T(8,128)} %get-tuple-element.63.refs_3_, f32[32,32,128]{2,1,0:T(8,128)S(1)} %all_to_all.41.refs_5_.refs_4_, ...), custom_call_target="tpu_custom_call" | custom-call | tf_op jit(solution)/shard_map/second_update/pallas_call | solution.py:677
  171.6 5.6 %all-to-all-done.6.refs_7_ = f32[32,16,128]{2,1,0:T(8,128)S(1)} async-done(((f32[32,16,128]{2,1,0:T(8,128)}), f32[32,16,128]{2,1,0:T(8,128)S(1)}, u32[]{:S(2)}, u32[]{:S(2)}) %all-to-all-start.6) | async-done | bytes 262176 | tf_op jit(solution)/shard_map/all_to_all | solution.py:776
  177.2 5.8 %first_pull.1 = (f32[2,192,128]{2,1,0:T(8,128)}, f32[32,64,128]{2,1,0:T(8,128)}) custom-call(s32[8]{0:T(128)S(1)} %copy-done.3, s32[32,6]{1,0:T(8,128)S(1)} %bitcast.28, s32[384]{0:T(512)S(1)} %reshape.36.refs_2_.refs_1_, s32[32]{0:T(128)S(1)} %bitcast.33, f32[2,192,128]{2,1,0:T(8,128)} %get-tuple-element.38.refs_3_.refs_4_, ...), custom_call_target="tpu_custom_call" | custom-call | tf_op jit(solution)/shard_map/first_pull/pallas_call | solution.py:677
  183.0 2.7 %all-to-all-start.7 = ((f32[32,64,128]{2,1,0:T(8,128)}), f32[32,64,128]{2,1,0:T(8,128)S(1)}, u32[]{:S(2)}, u32[]{:S(2)}) async-start(f32[32,64,128]{2,1,0:T(8,128)} %get-tuple-element.66), calls=%async_computation.7 | async-start | bytes 2097152 | tf_op jit(solution)/shard_map/all_to_all | solution.py:776
  185.7 5.8 %interior_back.1.refs_2_ = f32[2,512,128]{2,1,0:T(8,128)} custom-call(s32[8]{0:T(128)S(1)} %copy-done.3, f32[2,512,128]{2,1,0:T(8,128)} %get-tuple-element.36.refs_1_, f32[2,512,128]{2,1,0:T(8,128)} %get-tuple-element.58.refs_2_), custom_call_target="tpu_custom_call" | custom-call | tf_op jit(solution)/shard_map/interior_back/pallas_call | solution.py:677
  191.4 20.4 %all-to-all-done.7.refs_4_ = f32[32,64,128]{2,1,0:T(8,128)S(1)} async-done(((f32[32,64,128]{2,1,0:T(8,128)}), f32[32,64,128]{2,1,0:T(8,128)S(1)}, u32[]{:S(2)}, u32[]{:S(2)}) %all-to-all-start.7) | async-done | bytes 1048608 | tf_op jit(solution)/shard_map/all_to_all | solution.py:776
  211.8 3.5 %last_cot.1 = (f32[512,256]{1,0:T(8,128)}, f32[512,256]{1,0:T(8,128)}) custom-call(s32[32,6]{1,0:T(8,128)S(1)} %bitcast.29, s32[8,8]{1,0:T(8,128)S(1)} %copy-done.2, f32[2,512,128]{2,1,0:T(8,128)} %interior_back.1.refs_2_, f32[2,192,128]{2,1,0:T(8,128)} %get-tuple-element.65.refs_3_, ...), custom_call_target="tpu_custom_call", output_to_operand_aliasing={{1}: (5, {})} | custom-call | tf_op jit(solution)/shard_map/last_cot/pallas_call | solution.py:677
  (11 shorter events, 0.1 us)
Async XLA Ops:
  1.4 0.7 copy-start.2
  6.3 7.1 %copy-start.5 = (s32[8,6,4]{0,2,1:T(4,128)S(1)}, s32[8,6,4]{0,2,1:T(4,128)}, u32[]{:S(2)}) copy-start(s32[8,6,4]{0,2,1:T(4,128)} %param.14) | copy-start | bytes 2308
  6.4 33.3 %all-to-all-start = ((f32[32,64,128]{2,1,0:T(8,128)}), f32[32,64,128]{2,1,0:T(8,128)S(1)}, u32[]{:S(2)}, u32[]{:S(2)}) async-start(f32[32,64,128]{2,1,0:T(8,128)} %get-tuple-element.40), calls=%async_computation | async-start | bytes 2097152 | tf_op jit(solution)/shard_map/all_to_all | solution.py:776
  13.4 0.7 copy-start.6
  14.6 0.7 copy-start.3
  15.3 24.3 %copy-start = (bf16[512,128]{1,0:T(8,128)(2,1)S(1)}, bf16[512,128]{1,0:T(8,128)(2,1)}, u32[]{:S(2)}) copy-start(bf16[512,128]{1,0:T(8,128)(2,1)} %constant.44.clone.refs_6_.refs_7_.refs_5_.refs_4_.refs_9_) | copy-start | bytes 393220
  15.3 24.3 %copy-start.1 = (bf16[128,512]{1,0:T(8,128)(2,1)S(1)}, bf16[128,512]{1,0:T(8,128)(2,1)}, u32[]{:S(2)}) copy-start(bf16[128,512]{1,0:T(8,128)(2,1)} %constant.45.clone.refs_7_.refs_6_.refs_4_.refs_10_) | copy-start | bytes 393220
  43.4 14.2 %all-to-all-start.1 = ((f32[32,16,128]{2,1,0:T(8,128)}), f32[32,16,128]{2,1,0:T(8,128)S(1)}, u32[]{:S(2)}, u32[]{:S(2)}) async-start(f32[32,16,128]{2,1,0:T(8,128)} %get-tuple-element.42), calls=%async_computation.1 | async-start | bytes 524288 | tf_op jit(solution)/shard_map/all_to_all | solution.py:776
  47.1 0.7 copy-start.4
  84.0 23.3 %all-to-all-start.3 = ((f32[32,48,128]{2,1,0:T(8,128)}), f32[32,48,128]{2,1,0:T(8,128)S(1)}, u32[]{:S(2)}, u32[]{:S(2)}) async-start(f32[32,48,128]{2,1,0:T(8,128)} %get-tuple-element.50), calls=%async_computation.3 | async-start | bytes 1572864 | tf_op jit(solution)/shard_map/all_to_all | solution.py:776
  112.4 23.8 %all-to-all-start.4 = ((f32[32,48,128]{2,1,0:T(8,128)}), f32[32,48,128]{2,1,0:T(8,128)S(1)}, u32[]{:S(2)}, u32[]{:S(2)}) async-start(f32[32,48,128]{2,1,0:T(8,128)} %get-tuple-element.53), calls=%async_computation.4 | async-start | bytes 1572864 | tf_op jit(solution)/shard_map/all_to_all | solution.py:776
  164.0 13.2 %all-to-all-start.6 = ((f32[32,16,128]{2,1,0:T(8,128)}), f32[32,16,128]{2,1,0:T(8,128)S(1)}, u32[]{:S(2)}, u32[]{:S(2)}) async-start(f32[32,16,128]{2,1,0:T(8,128)} %get-tuple-element.61), calls=%async_computation.6 | async-start | bytes 524288 | tf_op jit(solution)/shard_map/all_to_all | solution.py:776
  183.0 28.9 %all-to-all-start.7 = ((f32[32,64,128]{2,1,0:T(8,128)}), f32[32,64,128]{2,1,0:T(8,128)S(1)}, u32[]{:S(2)}, u32[]{:S(2)}) async-start(f32[32,64,128]{2,1,0:T(8,128)} %get-tuple-element.66), calls=%async_computation.7 | async-start | bytes 2097152 | tf_op jit(solution)/shard_map/all_to_all | solution.py:776

commit v4 on v3

--- a/solution.py
+++ b/solution.py
@@ -36,6 +36,10 @@
     lanes = values.shape[1]
     shift = shift % lanes
     return values if shift == 0 else pltpu.roll(values, shift, 1)
+
+
+def tile(packets, peer, row):
+    return packets.at[peer, row // 4] if len(packets.shape) == 4 else packets.at[peer, row : row + 4]
 
 
 def flux_of(behind, beyond, normal, inv_behind, inv_beyond):
@@ -100,7 +104,8 @@
         self.ff = (2, 6 * 4 * slots, self.COL)
         self.fb = (2, 3 * slots * 8, self.COL)
         self.native = (slots * 4 * extent, 2 * self.COL)
-        self.coarse = (slots * 16, self.COL)
+        self.coarse = (slots * 32, self.COL)
+        self.small = (slots * 24, self.COL)
 
     def lane(self, rows):
         return lax.broadcasted_iota(jnp.int32, (rows, self.COL), 1)
@@ -225,22 +230,16 @@
                 )
         small = dot2(jnp.concatenate(rows, axis=0), half[...])
         for k in range(12):
-            rb[pl.ds(k, S, stride=16), :] = small[k * S : (k + 1) * S]
-        zero = jnp.zeros((S, COL), f32)
-        for k in range(12, 16):
-            rb[pl.ds(k, S, stride=16), :] = zero
-        sub = lax.broadcasted_iota(jnp.int32, (8, COL), 0)
-        low = self.low(8)
+            rb[pl.ds((k // 4) * 8 + k % 4, S, stride=24), :] = small[k * S : (k + 1) * S]
+        low = self.low(4)
 
         def one(peer, carry):
-            def part(f, at):
-                slot = jnp.maximum(send[peer, f], 0)
-                return rb[pl.ds(pl.multiple_of(slot * 16 + at, 8), 8), :]
-
-            first = jnp.where(low, part(0, 0), part(1, 0))
-            second = jnp.where(low, part(2, 0), part(3, 0))
-            out[peer, row0 : row0 + 8, :] = jnp.where(sub < 4, first, second)
-            out[peer, row0 + 8 : row0 + 16, :] = jnp.where(low, part(4, 8), part(5, 8))
+            for axis in range(3):
+                lo, hi = [
+                    rb[pl.ds(pl.multiple_of(slot * 24 + axis * 8, 8), 4), :]
+                    for slot in [jnp.maximum(send[peer, axis * 2 + side], 0) for side in range(2)]
+                ]
+                tile(out, peer, row0 + axis * 4)[...] = jnp.where(low, lo, hi)
             return carry
 
         lax.fori_loop(0, self.P, one, 0)
@@ -250,7 +249,8 @@
         low = self.low(4)
 
         def clear(peer, carry):
-            out[peer, row0 : row0 + 16, :] = jnp.zeros((16, self.COL), f32)
+            for axis in range(3):
+                tile(out, peer, row0 + axis * 4)[...] = jnp.zeros((4, self.COL), f32)
             return carry
 
         lax.fori_loop(0, self.P, clear, 0)
@@ -268,7 +268,7 @@
                         for g in range(2):
                             moved = roll(values, H * ((1 - side) - g))
                             peer = table[base + h * 2 + g]
-                            out[peer, at : at + 4, :] += jnp.where(keep, moved, 0.0)
+                            tile(out, peer, at)[...] += jnp.where(keep, moved, 0.0)
 
                 pl.when(table[base + 4] == 2)(send_quarters)
 
@@ -276,20 +276,20 @@
         S, COL = self.S, self.COL
 
         def one(peer, carry):
-            block = packets[peer, row0 : row0 + 16, :]
-            for f in range(6):
-                slot = jnp.maximum(send[peer, f], 0)
-                rows = pl.ds(pl.multiple_of(slot * 16, 8), 16)
-                sums[f][rows, :] += block
+            for axis in range(3):
+                block = tile(packets, peer, row0 + axis * 4)[...]
+                for f in (axis * 2, axis * 2 + 1):
+                    slot = jnp.maximum(send[peer, f], 0)
+                    sums[f][pl.ds(pl.multiple_of(slot * 8, 8), 4), :] += block
             return carry
 
         for f in range(6):
             sums[f][...] = jnp.zeros(sums[f].shape, f32)
         lax.fori_loop(0, self.P, one, 0)
         for f in range(6):
-            axis, side = f // 2, f % 2
+            side = f % 2
             rows = jnp.concatenate(
-                [sums[f][pl.ds(axis * 4 + c, S, stride=16), :] for c in range(4)], axis=0
+                [sums[f][pl.ds(c, S, stride=8), :] for c in range(4)], axis=0
             )
             wide = dot2(rows, half_back[:, side * 2 * COL : (side + 1) * 2 * COL])
             for c in range(4):
@@ -392,7 +392,7 @@
                     for h in range(2):
                         got = []
                         for g in range(2):
-                            values = packets[table[base + h * 2 + g], at : at + 4, :]
+                            values = tile(packets, table[base + h * 2 + g], at)[...]
                             got.append(roll(values, H * (g - (1 - side))))
                         out[h, row : row + 4, :] = jnp.where(low, got[0], got[1])
 
@@ -411,8 +411,8 @@
                             x = ox * H + pair * 2
                             first, second = load(s, x, oy), load(s, x + 1, oy)
                             at = row0 + pair * 4
-                            out[peers[0], at : at + 4, :] = jnp.where(low, first, roll(second, H))
-                            out[peers[1], at : at + 4, :] = jnp.where(low, roll(first, -H), second)
+                            tile(out, peers[0], at)[...] = jnp.where(low, first, roll(second, H))
+                            tile(out, peers[1], at)[...] = jnp.where(low, roll(first, -H), second)
 
             pl.when(parents[s, 0] >= 0)(send)
 
@@ -428,8 +428,8 @@
                         for pair in range(H // 2):
                             x = ox * H + pair * 2
                             at = row0 + pair * 4
-                            first = packets[peers[0], at : at + 4, :]
-                            second = packets[peers[1], at : at + 4, :]
+                            first = tile(packets, peers[0], at)[...]
+                            second = tile(packets, peers[1], at)[...]
                             store(s, x, oy, jnp.where(low, first, roll(second, H)))
                             store(s, x + 1, oy, jnp.where(low, roll(first, -H), second))
 
@@ -455,12 +455,14 @@
                 )
         small = 0.5 * dot2(jnp.concatenate(rows, axis=0), half[...])
         for k in range(16):
-            cb[pl.ds(k, S, stride=16), :] = small[k * S : (k + 1) * S]
+            cb[pl.ds((k // 4) * 8 + k % 4, S, stride=32), :] = small[k * S : (k + 1) * S]
 
     def pack_children(self, cb, children, out, row0):
         def one(peer, carry):
             slot = jnp.maximum(children[peer], 0)
-            out[peer, row0 : row0 + 16, :] = cb[pl.ds(pl.multiple_of(slot * 16, 8), 16), :]
+            for part in range(4):
+                rows = pl.ds(pl.multiple_of(slot * 32 + part * 8, 8), 4)
+                tile(out, peer, row0 + part * 4)[...] = cb[rows, :]
             return carry
 
         lax.fori_loop(0, self.P, one, 0)
@@ -472,12 +474,15 @@
         def one(peer, carry):
             child = children[peer]
             slot = jnp.where(child < 0, S, child)
-            rows = pl.ds(pl.multiple_of(slot * 16, 8), 16)
-            cc[rows, :] += jnp.where(child < 0, 0.0, packets[peer, row0 : row0 + 16, :])
+            for part in range(4):
+                rows = pl.ds(pl.multiple_of(slot * 32 + part * 8, 8), 4)
+                cc[rows, :] += tile(packets, peer, row0 + part * 4)[...]
             return carry
 
         lax.fori_loop(0, self.P, one, 0)
-        rows = jnp.concatenate([cc[pl.ds(k, S, stride=16), :] for k in range(16)], axis=0)
+        rows = jnp.concatenate(
+            [cc[pl.ds((k // 4) * 8 + k % 4, S, stride=32), :] for k in range(16)], axis=0
+        )
         wide = 0.5 * dot2(rows, half_back[...])
         covered = self.per_slot(lambda s: parents[s, 0]) >= 0
         for x in range(self.E):
@@ -785,7 +790,7 @@
     kind_scratch = pltpu.VMEM((3 * S * 8, COL), jnp.int32)
     native_planes = [vm(S * 4 * E, COL), vm(S * 4 * E, COL)]
     pair_of_sems = pltpu.SemaphoreType.DMA((2,))
-    quarter_sums = [vm(S * 16, COL) for _ in range(6)]
+    quarter_sums = [vm(S * 8, COL) for _ in range(6)]
     face_sums = [vm(2, S * 8, COL) for _ in range(6)]
     signs = [1.0, -1.0, 1.0, -1.0, 1.0, -1.0]
 
@@ -876,7 +881,8 @@
 
     def carry_packets(source, out, row0):
         def one(peer, carry):
-            out[peer, row0 : row0 + 16, :] = source[peer, :, :]
+            for axis in range(3):
+                tile(out, peer, row0 + axis * 4)[...] = tile(source, peer, axis * 4)[...]
             return carry
 
         lax.fori_loop(0, peers, one, 0)
@@ -936,7 +942,7 @@
         del after
         plan.ghosts(recv, table_s, planes, near, kinds, gb.ref, half_r, back_r)
         gb.send()
-        layer = plan.ff_at(layers.get())
+        layer = plan.ff_at(layers)
         boundary_fluxes(plan, layer, ghost_reader(gb.ref, layer, levels_s), flux_emitter(b_fb.ref, ff))
         b_fb.send()
         plan.pack_averages(plan.ff_at(ff), rb, send_s, packets, 0, half_r)
@@ -945,9 +951,9 @@
         first_flux,
         "first_flux",
         [levels, send, table],
-        [Late(layers1), done1, received1, half, half_back],
-        [(plan.fb, "late"), (plan.fb, "late"), ((peers, 16, COL), None)],
-        ghost_scratch + [vm(*plan.ff), vm(*plan.coarse)],
+        [layers1, done1, received1, half, half_back],
+        [(plan.fb, "late"), (plan.fb, "late"), ((peers, 3, 4, COL), None)],
+        ghost_scratch + [vm(*plan.ff), vm(*plan.small)],
     )
     received2 = exchange(packets)
 
@@ -966,16 +972,15 @@
         "upward_second",
         [levels, table, children, parents],
         [Late(native_guidance, native=True), received1, half_back],
-        [(plan.slab, "late"), (plan.fb, "late"), ((peers, 16, COL), "late")],
-        [vm((S + 1) * 16, COL)],
+        [(plan.slab, "late"), (plan.fb, "late"), ((peers, 3, 4, COL), "late")],
+        [vm((S + 1) * 32, COL)],
     )
 
     def first_update(levels_s, table_s, children_s, partial, b_fb, recv, quarters, half_r, updated,
                      packets, corr, cb):
-        plan.corrected(b_fb.get(), recv, 0, table_s, corr)
-        finished(partial.get(), corr, levels_s, slab_put(updated.ref))
-        updated.send()
-        plan.average_blocks(plan.slab_at(updated.ref), cb, half_r)
+        plan.corrected(b_fb, recv, 0, table_s, corr)
+        finished(partial, corr, levels_s, slab_put(updated))
+        plan.average_blocks(plan.slab_at(updated), cb, half_r)
         plan.pack_children(cb, children_s, packets, 0)
         carry_packets(quarters.get(), packets, 16)
 
@@ -983,16 +988,14 @@
         first_update,
         "first_update",
         [levels, table, children],
-        [Late(partial1), Late(fluxes1), received2, Late(quarters2), half],
-        [(plan.slab, "late"), ((peers, 32, COL), None)],
+        [partial1, fluxes1, received2, Late(quarters2), half],
+        [(plan.slab, None), ((peers, 7, 4, COL), None)],
         [fb_scratch, vm(*plan.coarse)],
     )
     received3 = exchange(packets)
 
-    def middle_pack(send_s, parents_s, updated, recv, volume, layers, packets, fb, sems):
-        copy = pltpu.make_async_copy(updated, volume.ref, sems.at[0])
-        copy.start()
-        copy.wait()
+    def middle_pack(send_s, parents_s, updated, recv, volume, layers, packets, fb):
+        volume.ref[...] = updated[...]
 
         def store(s, x, q, value):
             volume.ref[q, plan.slab_rows(s, x), :] = value
@@ -1007,9 +1010,9 @@
         middle_pack,
         "middle_pack",
         [send, parents],
-        [Late(updated1, raw=True), received3],
+        [updated1, received3],
         [(plan.slab, "late"), (plan.ff, "late"), ((peers, 48, COL), "late")],
-        [fb_scratch, pair_of_sems],
+        [fb_scratch],
     )
     received4 = exchange(packets)
 
@@ -1042,7 +1045,7 @@
                     packets, planes, near, kinds, gcot):
         plan.ghosts(recv, table_s, planes, near, kinds, gb.ref, half_r, back_r)
         gb.send()
-        layer = plan.ff_at(layers.get())
+        layer = plan.ff_at(layers)
         boundary_pull(
             plan, layer, ghost_reader(gb.ref, layer, levels_s), plan.ff_at(flux_cot.get()),
             cot_emitter(layer_cot.ref, gcot),
@@ -1054,7 +1057,7 @@
         second_pull,
         "second_pull",
         [levels, table],
-        [Late(layers2), received4, Late(fluxcot2), half, half_back],
+        [layers2, received4, Late(fluxcot2), half, half_back],
         [(plan.fb, "late"), (plan.ff, "late"), ((peers, 48, COL), "late")],
         ghost_scratch + [fb_scratch],
     )
@@ -1072,17 +1075,16 @@
         "second_flux",
         [levels, send],
         [Late(layers2), Late(ghosts2), half],
-        [(plan.fb, "late"), ((peers, 16, COL), "late")],
-        [vm(*plan.ff), vm(*plan.coarse)],
+        [(plan.fb, "late"), ((peers, 3, 4, COL), "late")],
+        [vm(*plan.ff), vm(*plan.small)],
     )
 
     def middle_cot(send_s, parents_s, through, layer_cot, recv, averages, inner, packets, total, *sums):
         plan.take_faces(recv, send_s, sums)
         carry_packets(averages.get(), packets, 16)
-        add_layers(through.get(), layer_cot.get(), total, sums, slab_put(inner.ref))
-        inner.send()
+        add_layers(through.get(), layer_cot.get(), total, sums, slab_put(inner))
         plan.pack_octants(
-            lambda s, x, q: inner.ref[q, plan.slab_rows(s, x), :], parents_s, packets, 0
+            lambda s, x, q: inner[q, plan.slab_rows(s, x), :], parents_s, packets, 0
         )
 
     inner_cot, packets = run(
@@ -1090,7 +1092,7 @@
         "middle_cot",
         [send, parents],
         [Late(through2), Late(layercot2), received5, Late(averages2)],
-        [(plan.slab, "late"), ((peers, 32, COL), None)],
+        [(plan.slab, None), ((peers, 7, 4, COL), None)],
         [vm(*plan.ff)] + face_sums,
     )
     received6 = exchange(packets)
@@ -1098,8 +1100,7 @@
     def upward_first(levels_s, table_s, children_s, parents_s, inner, recv, back_r, up, cot_fb,
                      packets, cc):
         plan.upward(
-            recv, 0, cc, children_s, parents_s, lambda q, x, c: plan.slab_at(inner.get())(q, x, c),
-            slab_put(up.ref), back_r,
+            recv, 0, cc, children_s, parents_s, plan.slab_at(inner), slab_put(up.ref), back_r
         )
         up.send()
         corrected_cot_of(plan.slab_at(up.ref), levels_s, cot_fb.ref)
@@ -1110,9 +1111,9 @@
         upward_first,
         "upward_first",
         [levels, table, children, parents],
-        [Late(inner_cot), received6, half_back],
-        [(plan.slab, "late"), (plan.fb, "late"), ((peers, 16, COL), None)],
-        [vm((S + 1) * 16, COL)],
+        [inner_cot, received6, half_back],
+        [(plan.slab, "late"), (plan.fb, "late"), ((peers, 3, 4, COL), None)],
+        [vm((S + 1) * 32, COL)],
     )
     received7 = exchange(packets)
 
@@ -1158,10 +1159,10 @@
                    back_r, layer_cot, packets, planes, near, kinds, flux_cot, gcot, *sums):
         plan.pack_children(coarse, children_s, packets.ref, 48)
         packets.send(48, 16)
-        flux_cot_of(recv, 0, cot_fb.get(), table_s, send_s, sums, kinds, flux_cot, back_r)
-        layer = plan.ff_at(layers.get())
+        flux_cot_of(recv, 0, cot_fb, table_s, send_s, sums, kinds, flux_cot, back_r)
+        layer = plan.ff_at(layers)
         boundary_pull(
-            plan, layer, ghost_reader(gb.get(), layer, levels_s), plan.ff_at(flux_cot),
+            plan, layer, ghost_reader(gb, layer, levels_s), plan.ff_at(flux_cot),
             cot_emitter(layer_cot.ref, gcot),
         )
         layer_cot.send()
@@ -1171,7 +1172,7 @@
         first_pull,
         "first_pull",
         [levels, send, table, children],
-        [Late(layers1), Late(ghosts1), Late(corrcot1), received7, coarse2, half, half_back],
+        [layers1, ghosts1, corrcot1, received7, coarse2, half, half_back],
         [(plan.ff, "late"), ((peers, 64, COL), "late")],
         ghost_scratch + [vm(*plan.ff), fb_scratch] + quarter_sums,
     )

time: 217 us -> 206 us (0.949)
  Pallas kernels: 74.9 us -> 68.4 us
  waiting for transfers between devices: 77.5 us -> 74.1 us
  blocking collectives: 36.4 us -> 34 us
    pallas_call x16, Pallas kernels: 74.9 us -> 68.4 us  [run(): pl.pallas_call(wrapped, name=name, in_specs=specs, out_specs=out_specs, o...]
    all_to_all x6, waiting for transfers between devices: 77.5 us -> 74.1 us  [exchange(): lax.all_to_all(packets, 'blk', split_axis=0, concat_axis=0, tiled=True)]
    all_to_all x2, blocking collectives: 36.4 us -> 34 us  [exchange(): lax.all_to_all(packets, 'blk', split_axis=0, concat_axis=0, tiled=True)]
  transfers between devices with their start and end apart: 6 -> 6, of which waited for: 6 -> 6; matrix products, arithmetic and copies ran while one was open for 0% -> 0% of each run, Pallas kernels for 16% -> 17%
where the time goes in v4:
time: 206 us; the launch traced here: 204 us
  waiting for transfers between devices  74.1 us (36%)
  Pallas kernels  68.4 us (33%)
  blocking collectives  34 us (17%)
  starting transfers between devices  22.2 us (11%)
  local copies, waits for them, and re-layouts  3.82 us (2%)
    all_to_all x6, waiting for transfers between devices, exchange(): lax.all_to_all(packets, 'blk', split_axis=0, concat_axis=0, tiled=True)  74.1 us
    pallas_call x16, Pallas kernels, run(): pl.pallas_call(wrapped, name=name, in_specs=specs, out_specs=out_specs, o...  68.4 us
    all_to_all x2, blocking collectives, exchange(): lax.all_to_all(packets, 'blk', split_axis=0, concat_axis=0, tiled=True)  34 us
    all_to_all x6, starting transfers between devices, exchange(): lax.all_to_all(packets, 'blk', split_axis=0, concat_axis=0, tiled=True)  22.2 us
  transfers between devices with their start and end apart: 6, of which 6 were waited for; matrix products, arithmetic and copies ran while one was open for 0% of the time, Pallas kernels for 17%

profile of v4, /device:TPU:0, one launch (start us, length us, event | category | flops | bytes accessed | tf_op | source)
XLA Modules:
  0.0 203.7 jit_solution(5877747523751869209)
XLA Ops:
  0.6 0.8 copy.21
  1.4 0.0 copy-start.8
  1.4 0.7 copy-done.8
  2.1 4.0 %first_pack.1 = (f32[2,512,128]{2,1,0:T(8,128)}, f32[2,192,128]{2,1,0:T(8,128)}, f32[32,64,128]{2,1,0:T(8,128)}) custom-call(s32[32,6]{1,0:T(8,128)S(1)} %bitcast.22, s32[8,8]{1,0:T(8,128)S(1)} %copy-done.8, f32[512,256]{1,0:T(8,128)} %bitcast.36, f32[512,256]{1,0:T(8,128)} %bitcast.34), custom_call_target="tpu_custom_call" | custom-call | tf_op jit(solution)/shard_map/first_pack/pallas_call | solution.py:682
  6.1 0.0 copy-start.11
  6.1 7.3 %all-to-all-start = ((f32[32,64,128]{2,1,0:T(8,128)}), f32[32,64,128]{2,1,0:T(8,128)S(1)}, u32[]{:S(2)}, u32[]{:S(2)}) async-start(f32[32,64,128]{2,1,0:T(8,128)} %get-tuple-element.40), calls=%async_computation | async-start | bytes 2097152 | tf_op jit(solution)/shard_map/all_to_all | solution.py:781
  13.4 0.0 copy-done.11
  13.4 0.0 copy-start.12
  13.5 0.1 copy.22
  13.6 0.6 copy-done.12
  14.2 0.1 copy.23
  14.4 0.1 copy.29
  14.5 0.1 reshape.36.refs_2_.refs_1_
  14.6 0.0 copy-start.9
  14.6 0.6 copy-done.9
  15.3 0.0 copy-start
  15.3 0.0 copy-start.1
  15.3 0.0 copy-start.3
  15.3 5.4 %interior_first.1 = (f32[2,512,128]{2,1,0:T(8,128)}, f32[8,128]{1,0:T(8,128)S(1)}) custom-call(s32[8]{0:T(128)S(1)} %copy-done.9, f32[2,512,128]{2,1,0:T(8,128)} %get-tuple-element.36.refs_1_), custom_call_target="tpu_custom_call" | custom-call | tf_op jit(solution)/shard_map/interior_first/pallas_call | solution.py:682
  20.7 18.9 %all-to-all-done.refs_5_ = f32[32,64,128]{2,1,0:T(8,128)S(1)} async-done(((f32[32,64,128]{2,1,0:T(8,128)}), f32[32,64,128]{2,1,0:T(8,128)S(1)}, u32[]{:S(2)}, u32[]{:S(2)}) %all-to-all-start) | async-done | bytes 1048608 | tf_op jit(solution)/shard_map/all_to_all | solution.py:781
  39.6 0.0 copy-done
  39.6 0.0 copy-done.1
  39.6 0.0 copy-done.3
  39.6 3.0 %first_flux.1 = (f32[2,192,128]{2,1,0:T(8,128)}, f32[2,192,128]{2,1,0:T(8,128)}, f32[32,3,4,128]{3,2,1,0:T(4,128)}) custom-call(s32[8]{0:T(128)S(1)} %copy-done.9, s32[32,6]{1,0:T(8,128)S(1)} %bitcast.23, s32[384]{0:T(512)S(1)} %reshape.36.refs_2_.refs_1_, f32[2,192,128]{2,1,0:T(8,128)S(1)} %copy-done.3, f32[8,128]{1,0:T(8,128)S(1)} %get-tuple-element.39.refs_4_, ...), custom_call_target="tpu_custom_call" | custom-call | tf_op jit(solution)/shard_map/first_flux/pallas_call | solution.py:682
  42.6 3.6 %all-to-all-start.1 = ((f32[32,3,4,128]{3,2,1,0:T(4,128)}), f32[32,3,4,128]{3,2,1,0:T(4,128)S(1)}, u32[]{:S(2)}, u32[]{:S(2)}) async-start(f32[32,3,4,128]{3,2,1,0:T(4,128)} %get-tuple-element.42), calls=%async_computation.1 | async-start | bytes 393216 | tf_op jit(solution)/shard_map/all_to_all | solution.py:781
  46.2 0.0 copy-start.10
  46.2 0.6 copy-done.10
  46.9 0.0 copy-start.4
  46.9 0.0 copy-start.7
  46.9 5.9 %upward_second.1 = (f32[2,512,128]{2,1,0:T(8,128)}, f32[2,192,128]{2,1,0:T(8,128)}, f32[32,3,4,128]{3,2,1,0:T(4,128)}) custom-call(s32[8]{0:T(128)S(1)} %copy-done.9, s32[384]{0:T(512)S(1)} %reshape.36.refs_2_.refs_1_, s32[32]{0:T(128)S(1)} %bitcast.30, s32[8,8]{1,0:T(8,128)S(1)} %copy-done.8, f32[512,256]{1,0:T(8,128)} %bitcast.35, ...), custom_call_target="tpu_custom_call" | custom-call | tf_op jit(solution)/shard_map/upward_second/pallas_call | solution.py:682
  52.8 2.4 %all-to-all-done.1.refs_5_ = f32[32,3,4,128]{3,2,1,0:T(4,128)S(1)} async-done(((f32[32,3,4,128]{3,2,1,0:T(4,128)}), f32[32,3,4,128]{3,2,1,0:T(4,128)S(1)}, u32[]{:S(2)}, u32[]{:S(2)}) %all-to-all-start.1) | async-done | bytes 196640 | tf_op jit(solution)/shard_map/all_to_all | solution.py:781
  55.2 0.0 copy-done.4
  55.2 0.0 copy-done.7
  55.2 3.6 %first_update.1 = (f32[2,512,128]{2,1,0:T(8,128)S(1)}, f32[32,7,4,128]{3,2,1,0:T(4,128)S(1)}) custom-call(s32[8]{0:T(128)S(1)} %copy-done.9, s32[384]{0:T(512)S(1)} %reshape.36.refs_2_.refs_1_, s32[32]{0:T(128)S(1)} %bitcast.31, f32[2,512,128]{2,1,0:T(8,128)S(1)} %copy-done.4, f32[2,192,128]{2,1,0:T(8,128)S(1)} %copy-done.7, ...), custom_call_target="tpu_custom_call" | custom-call | tf_op jit(solution)/shard_map/first_update/pallas_call | solution.py:682
  58.8 16.1 %all_to_all.40.refs_3_ = f32[32,7,4,128]{3,2,1,0:T(4,128)S(1)} all-to-all(f32[32,7,4,128]{3,2,1,0:T(4,128)S(1)} %get-tuple-element.45), channel_id=1, replica_groups=mesh['blk'=32] {'blk'}, dimensions={0} | all-to-all | bytes 917504 | tf_op jit(solution)/shard_map/all_to_all | solution.py:781
  75.0 2.8 %middle_pack.1 = (f32[2,512,128]{2,1,0:T(8,128)}, f32[2,192,128]{2,1,0:T(8,128)}, f32[32,48,128]{2,1,0:T(8,128)}) custom-call(s32[32,6]{1,0:T(8,128)S(1)} %bitcast.24, s32[8,8]{1,0:T(8,128)S(1)} %copy-done.8, f32[2,512,128]{2,1,0:T(8,128)S(1)} %get-tuple-element.44.refs_2_, f32[32,7,4,128]{3,2,1,0:T(4,128)S(1)} %all_to_all.40.refs_3_), custom_call_target="tpu_custom_call" | custom-call | tf_op jit(solution)/shard_map/middle_pack/pallas_call | solution.py:682
  77.8 2.7 %all-to-all-start.3 = ((f32[32,48,128]{2,1,0:T(8,128)}), f32[32,48,128]{2,1,0:T(8,128)S(1)}, u32[]{:S(2)}, u32[]{:S(2)}) async-start(f32[32,48,128]{2,1,0:T(8,128)} %get-tuple-element.50), calls=%async_computation.3 | async-start | bytes 1572864 | tf_op jit(solution)/shard_map/all_to_all | solution.py:781
  80.5 0.0 copy-start.2
  80.5 3.2 %flux_cot_second.1.refs_4_ = f32[2,192,128]{2,1,0:T(8,128)} custom-call(s32[32,6]{1,0:T(8,128)S(1)} %bitcast.25, s32[384]{0:T(512)S(1)} %reshape.36.refs_2_.refs_1_, f32[2,192,128]{2,1,0:T(8,128)} %get-tuple-element.51.refs_2_, f32[32,7,4,128]{3,2,1,0:T(4,128)S(1)} %all_to_all.40.refs_3_, bf16[128,512]{1,0:T(8,128)(2,1)S(1)} %copy-done), custom_call_target="tpu_custom_call" | custom-call | tf_op jit(solution)/shard_map/flux_cot_second/pallas_call | solution.py:682
  83.7 17.4 %all-to-all-done.3.refs_3_ = f32[32,48,128]{2,1,0:T(8,128)S(1)} async-done(((f32[32,48,128]{2,1,0:T(8,128)}), f32[32,48,128]{2,1,0:T(8,128)S(1)}, u32[]{:S(2)}, u32[]{:S(2)}) %all-to-all-start.3) | async-done | bytes 786464 | tf_op jit(solution)/shard_map/all_to_all | solution.py:781
  101.0 0.0 copy-done.2
  101.1 4.8 %second_pull.1 = (f32[2,192,128]{2,1,0:T(8,128)}, f32[2,192,128]{2,1,0:T(8,128)}, f32[32,48,128]{2,1,0:T(8,128)}) custom-call(s32[8]{0:T(128)S(1)} %copy-done.9, s32[384]{0:T(512)S(1)} %reshape.36.refs_2_.refs_1_, f32[2,192,128]{2,1,0:T(8,128)S(1)} %copy-done.2, f32[32,48,128]{2,1,0:T(8,128)S(1)} %all-to-all-done.3.refs_3_, ...), custom_call_target="tpu_custom_call" | custom-call | tf_op jit(solution)/shard_map/second_pull/pallas_call | solution.py:682
  105.8 3.3 %all-to-all-start.4 = ((f32[32,48,128]{2,1,0:T(8,128)}), f32[32,48,128]{2,1,0:T(8,128)S(1)}, u32[]{:S(2)}, u32[]{:S(2)}) async-start(f32[32,48,128]{2,1,0:T(8,128)} %get-tuple-element.53), calls=%async_computation.4 | async-start | bytes 1572864 | tf_op jit(solution)/shard_map/all_to_all | solution.py:781
  109.2 6.2 %interior_both.1 = (f32[2,512,128]{2,1,0:T(8,128)}, f32[2,512,128]{2,1,0:T(8,128)}) custom-call(s32[8]{0:T(128)S(1)} %copy-done.9, f32[2,512,128]{2,1,0:T(8,128)} %get-tuple-element.46.refs_1_, f32[2,512,128]{2,1,0:T(8,128)} %get-tuple-element.47.refs_2_), custom_call_target="tpu_custom_call" | custom-call | tf_op jit(solution)/shard_map/interior_both/pallas_call | solution.py:682
  115.3 3.3 %second_flux.1 = (f32[2,192,128]{2,1,0:T(8,128)}, f32[32,3,4,128]{3,2,1,0:T(4,128)}) custom-call(s32[8]{0:T(128)S(1)} %copy-done.9, s32[32,6]{1,0:T(8,128)S(1)} %bitcast.26, f32[2,192,128]{2,1,0:T(8,128)} %get-tuple-element.49.refs_2_, f32[2,192,128]{2,1,0:T(8,128)} %get-tuple-element.54.refs_3_, bf16[512,128]{1,0:T(8,128)(2,1)S(1)} %copy-done.1), custom_call_target="tpu_custom_call" | custom-call | tf_op jit(solution)/shard_map/second_flux/pallas_call | solution.py:682
  118.7 11.1 %all-to-all-done.4.refs_4_ = f32[32,48,128]{2,1,0:T(8,128)S(1)} async-done(((f32[32,48,128]{2,1,0:T(8,128)}), f32[32,48,128]{2,1,0:T(8,128)S(1)}, u32[]{:S(2)}, u32[]{:S(2)}) %all-to-all-start.4) | async-done | bytes 786464 | tf_op jit(solution)/shard_map/all_to_all | solution.py:781
  129.8 2.8 %middle_cot.1 = (f32[2,512,128]{2,1,0:T(8,128)S(1)}, f32[32,7,4,128]{3,2,1,0:T(4,128)S(1)}) custom-call(s32[32,6]{1,0:T(8,128)S(1)} %bitcast.27, s32[8,8]{1,0:T(8,128)S(1)} %copy-done.8, f32[2,512,128]{2,1,0:T(8,128)} %get-tuple-element.48.refs_2_, f32[2,192,128]{2,1,0:T(8,128)} %get-tuple-element.52.refs_3_, f32[32,48,128]{2,1,0:T(8,128)S(1)} %all-to-all-done.4.refs_4_, ...), custom_call_target="tpu_custom_call" | custom-call | tf_op jit(solution)/shard_map/middle_cot/pallas_call | solution.py:682
  132.5 17.9 %all_to_all.41.refs_5_.refs_4_ = f32[32,7,4,128]{3,2,1,0:T(4,128)S(1)} all-to-all(f32[32,7,4,128]{3,2,1,0:T(4,128)S(1)} %get-tuple-element.57), channel_id=1, replica_groups=mesh['blk'=32] {'blk'}, dimensions={0} | all-to-all | bytes 917504 | tf_op jit(solution)/shard_map/all_to_all | solution.py:781
  150.4 4.8 %upward_first.1 = (f32[2,512,128]{2,1,0:T(8,128)}, f32[2,192,128]{2,1,0:T(8,128)}, f32[32,3,4,128]{3,2,1,0:T(4,128)}) custom-call(s32[8]{0:T(128)S(1)} %copy-done.9, s32[384]{0:T(512)S(1)} %reshape.36.refs_2_.refs_1_, s32[32]{0:T(128)S(1)} %bitcast.32, s32[8,8]{1,0:T(8,128)S(1)} %copy-done.8, f32[2,512,128]{2,1,0:T(8,128)S(1)} %get-tuple-element.56.refs_4_, ...), custom_call_target="tpu_custom_call" | custom-call | tf_op jit(solution)/shard_map/upward_first/pallas_call | solution.py:682
  155.2 2.6 %all-to-all-start.6 = ((f32[32,3,4,128]{3,2,1,0:T(4,128)}), f32[32,3,4,128]{3,2,1,0:T(4,128)S(1)}, u32[]{:S(2)}, u32[]{:S(2)}) async-start(f32[32,3,4,128]{3,2,1,0:T(4,128)} %get-tuple-element.61), calls=%async_computation.6 | async-start | bytes 393216 | tf_op jit(solution)/shard_map/all_to_all | solution.py:781
  157.8 0.0 copy-start.5
  157.8 0.0 copy-start.6
  157.8 5.1 %second_update.1 = (f32[512,256]{1,0:T(8,128)}, f32[256,128]{1,0:T(8,128)S(1)}) custom-call(s32[8]{0:T(128)S(1)} %copy-done.9, s32[384]{0:T(512)S(1)} %reshape.36.refs_2_.refs_1_, f32[2,512,128]{2,1,0:T(8,128)} %get-tuple-element.62.refs_2_, f32[2,192,128]{2,1,0:T(8,128)} %get-tuple-element.63.refs_3_, f32[32,7,4,128]{3,2,1,0:T(4,128)S(1)} %all_to_all.41.refs_5_.refs_4_, ...), custom_call_target="tpu_custom_call" | custom-call | tf_op jit(solution)/shard_map/second_update/pallas_call | solution.py:682
  162.8 3.9 %all-to-all-done.6.refs_7_ = f32[32,3,4,128]{3,2,1,0:T(4,128)S(1)} async-done(((f32[32,3,4,128]{3,2,1,0:T(4,128)}), f32[32,3,4,128]{3,2,1,0:T(4,128)S(1)}, u32[]{:S(2)}, u32[]{:S(2)}) %all-to-all-start.6) | async-done | bytes 196640 | tf_op jit(solution)/shard_map/all_to_all | solution.py:781
  166.7 0.0 copy-done.5
  166.7 0.0 copy-done.6
  166.7 4.5 %first_pull.1 = (f32[2,192,128]{2,1,0:T(8,128)}, f32[32,64,128]{2,1,0:T(8,128)}) custom-call(s32[8]{0:T(128)S(1)} %copy-done.9, s32[32,6]{1,0:T(8,128)S(1)} %bitcast.28, s32[384]{0:T(512)S(1)} %reshape.36.refs_2_.refs_1_, s32[32]{0:T(128)S(1)} %bitcast.33, f32[2,192,128]{2,1,0:T(8,128)S(1)} %copy-done.3, f32[2,192,128]{2,1,0:T(8,128)S(1)} %copy-done.5, ...), custom_call_target="tpu_custom_call" | custom-call | tf_op jit(solution)/shard_map/first_pull/pallas_call | solution.py:682
  171.2 2.7 %all-to-all-start.7 = ((f32[32,64,128]{2,1,0:T(8,128)}), f32[32,64,128]{2,1,0:T(8,128)S(1)}, u32[]{:S(2)}, u32[]{:S(2)}) async-start(f32[32,64,128]{2,1,0:T(8,128)} %get-tuple-element.66), calls=%async_computation.7 | async-start | bytes 2097152 | tf_op jit(solution)/shard_map/all_to_all | solution.py:781
  173.9 5.8 %interior_back.1.refs_2_ = f32[2,512,128]{2,1,0:T(8,128)} custom-call(s32[8]{0:T(128)S(1)} %copy-done.9, f32[2,512,128]{2,1,0:T(8,128)} %get-tuple-element.36.refs_1_, f32[2,512,128]{2,1,0:T(8,128)} %get-tuple-element.58.refs_2_), custom_call_target="tpu_custom_call" | custom-call | tf_op jit(solution)/shard_map/interior_back/pallas_call | solution.py:682
  179.7 20.4 %all-to-all-done.7.refs_4_ = f32[32,64,128]{2,1,0:T(8,128)S(1)} async-done(((f32[32,64,128]{2,1,0:T(8,128)}), f32[32,64,128]{2,1,0:T(8,128)S(1)}, u32[]{:S(2)}, u32[]{:S(2)}) %all-to-all-start.7) | async-done | bytes 1048608 | tf_op jit(solution)/shard_map/all_to_all | solution.py:781
  200.1 3.5 %last_cot.1 = (f32[512,256]{1,0:T(8,128)}, f32[512,256]{1,0:T(8,128)}) custom-call(s32[32,6]{1,0:T(8,128)S(1)} %bitcast.29, s32[8,8]{1,0:T(8,128)S(1)} %copy-done.8, f32[2,512,128]{2,1,0:T(8,128)} %interior_back.1.refs_2_, f32[2,192,128]{2,1,0:T(8,128)} %get-tuple-element.65.refs_3_, ...), custom_call_target="tpu_custom_call", output_to_operand_aliasing={{1}: (5, {})} | custom-call | tf_op jit(solution)/shard_map/last_cot/pallas_call | solution.py:682
  (11 shorter events, 0.1 us)
Async XLA Ops:
  1.4 0.7 copy-start.8
  6.1 7.4 %copy-start.11 = (s32[8,6,4]{0,2,1:T(4,128)S(1)}, s32[8,6,4]{0,2,1:T(4,128)}, u32[]{:S(2)}) copy-start(s32[8,6,4]{0,2,1:T(4,128)} %param.14) | copy-start | bytes 2308
  6.1 33.5 %all-to-all-start = ((f32[32,64,128]{2,1,0:T(8,128)}), f32[32,64,128]{2,1,0:T(8,128)S(1)}, u32[]{:S(2)}, u32[]{:S(2)}) async-start(f32[32,64,128]{2,1,0:T(8,128)} %get-tuple-element.40), calls=%async_computation | async-start | bytes 2097152 | tf_op jit(solution)/shard_map/all_to_all | solution.py:781
  13.4 0.7 copy-start.12
  14.6 0.7 copy-start.9
  15.3 24.3 %copy-start = (bf16[128,512]{1,0:T(8,128)(2,1)S(1)}, bf16[128,512]{1,0:T(8,128)(2,1)}, u32[]{:S(2)}) copy-start(bf16[128,512]{1,0:T(8,128)(2,1)} %constant.45.clone.refs_7_.refs_6_.refs_4_.refs_10_) | copy-start | bytes 393220
  15.3 24.3 %copy-start.1 = (bf16[512,128]{1,0:T(8,128)(2,1)S(1)}, bf16[512,128]{1,0:T(8,128)(2,1)}, u32[]{:S(2)}) copy-start(bf16[512,128]{1,0:T(8,128)(2,1)} %constant.44.clone.refs_6_.refs_7_.refs_5_.refs_4_.refs_9_) | copy-start | bytes 393220
  15.3 24.3 %copy-start.3 = (f32[2,192,128]{2,1,0:T(8,128)S(1)}, f32[2,192,128]{2,1,0:T(8,128)}, u32[]{:S(2)}) copy-start(f32[2,192,128]{2,1,0:T(8,128)} %get-tuple-element.38.refs_3_.refs_4_) | copy-start | bytes 589828
  42.6 12.6 %all-to-all-start.1 = ((f32[32,3,4,128]{3,2,1,0:T(4,128)}), f32[32,3,4,128]{3,2,1,0:T(4,128)S(1)}, u32[]{:S(2)}, u32[]{:S(2)}) async-start(f32[32,3,4,128]{3,2,1,0:T(4,128)} %get-tuple-element.42), calls=%async_computation.1 | async-start | bytes 393216 | tf_op jit(solution)/shard_map/all_to_all | solution.py:781
  46.2 0.7 copy-start.10
  46.9 8.3 %copy-start.4 = (f32[2,512,128]{2,1,0:T(8,128)S(1)}, f32[2,512,128]{2,1,0:T(8,128)}, u32[]{:S(2)}) copy-start(f32[2,512,128]{2,1,0:T(8,128)} %get-tuple-element.37.refs_3_) | copy-start | bytes 1572868
  46.9 8.3 %copy-start.7 = (f32[2,192,128]{2,1,0:T(8,128)S(1)}, f32[2,192,128]{2,1,0:T(8,128)}, u32[]{:S(2)}) copy-start(f32[2,192,128]{2,1,0:T(8,128)} %get-tuple-element.41.refs_4_) | copy-start | bytes 589828
  77.8 23.3 %all-to-all-start.3 = ((f32[32,48,128]{2,1,0:T(8,128)}), f32[32,48,128]{2,1,0:T(8,128)S(1)}, u32[]{:S(2)}, u32[]{:S(2)}) async-start(f32[32,48,128]{2,1,0:T(8,128)} %get-tuple-element.50), calls=%async_computation.3 | async-start | bytes 1572864 | tf_op jit(solution)/shard_map/all_to_all | solution.py:781
  80.5 20.6 %copy-start.2 = (f32[2,192,128]{2,1,0:T(8,128)S(1)}, f32[2,192,128]{2,1,0:T(8,128)}, u32[]{:S(2)}) copy-start(f32[2,192,128]{2,1,0:T(8,128)} %get-tuple-element.49.refs_2_) | copy-start | bytes 589828
  105.8 23.9 %all-to-all-start.4 = ((f32[32,48,128]{2,1,0:T(8,128)}), f32[32,48,128]{2,1,0:T(8,128)S(1)}, u32[]{:S(2)}, u32[]{:S(2)}) async-start(f32[32,48,128]{2,1,0:T(8,128)} %get-tuple-element.53), calls=%async_computation.4 | async-start | bytes 1572864 | tf_op jit(solution)/shard_map/all_to_all | solution.py:781
  155.2 11.6 %all-to-all-start.6 = ((f32[32,3,4,128]{3,2,1,0:T(4,128)}), f32[32,3,4,128]{3,2,1,0:T(4,128)S(1)}, u32[]{:S(2)}, u32[]{:S(2)}) async-start(f32[32,3,4,128]{3,2,1,0:T(4,128)} %get-tuple-element.61), calls=%async_computation.6 | async-start | bytes 393216 | tf_op jit(solution)/shard_map/all_to_all | solution.py:781
  157.8 9.0 %copy-start.5 = (f32[2,192,128]{2,1,0:T(8,128)S(1)}, f32[2,192,128]{2,1,0:T(8,128)}, u32[]{:S(2)}) copy-start(f32[2,192,128]{2,1,0:T(8,128)} %get-tuple-element.59.refs_5_) | copy-start | bytes 589828
  157.8 8.9 %copy-start.6 = (f32[2,192,128]{2,1,0:T(8,128)S(1)}, f32[2,192,128]{2,1,0:T(8,128)}, u32[]{:S(2)}) copy-start(f32[2,192,128]{2,1,0:T(8,128)} %get-tuple-element.60.refs_6_) | copy-start | bytes 589828
  171.2 28.9 %all-to-all-start.7 = ((f32[32,64,128]{2,1,0:T(8,128)}), f32[32,64,128]{2,1,0:T(8,128)S(1)}, u32[]{:S(2)}, u32[]{:S(2)}) async-start(f32[32,64,128]{2,1,0:T(8,128)} %get-tuple-element.66), calls=%async_computation.7 | async-start | bytes 2097152 | tf_op jit(solution)/shard_map/all_to_all | solution.py:781

commit v5 on v4

--- a/solution.py
+++ b/solution.py
@@ -211,12 +211,12 @@
                 rows = pl.ds(pl.multiple_of(slot * 8, 8), 8)
                 for q in range(2):
                     at = (f // 2) * 16 + q * 8
-                    sums[f][q, rows, :] += packets[peer, at : at + 8, :]
+                    sums[f * 2 + q][rows, :] += packets[peer, at : at + 8, :]
             return carry
 
-        for f in range(6):
-            sums[f][...] = jnp.zeros(sums[f].shape, f32)
-        lax.fori_loop(0, self.P, one, 0)
+        for part in sums:
+            part[...] = jnp.zeros(part.shape, f32)
+        lax.fori_loop(0, self.P, one, 0, unroll=4)
 
     def pack_averages(self, face, rb, send, out, row0, half):
         S, COL = self.S, self.COL
@@ -242,7 +242,7 @@
                 tile(out, peer, row0 + axis * 4)[...] = jnp.where(low, lo, hi)
             return carry
 
-        lax.fori_loop(0, self.P, one, 0)
+        lax.fori_loop(0, self.P, one, 0, unroll=4)
 
     def pack_quarters(self, fb, table, out, row0):
         E, H = self.E, self.H
@@ -253,7 +253,7 @@
                 tile(out, peer, row0 + axis * 4)[...] = jnp.zeros((4, self.COL), f32)
             return carry
 
-        lax.fori_loop(0, self.P, clear, 0)
+        lax.fori_loop(0, self.P, clear, 0, unroll=4)
         for s in range(self.S):
             for f in range(6):
                 base = (s * 6 + f) * 8
@@ -285,7 +285,7 @@
 
         for f in range(6):
             sums[f][...] = jnp.zeros(sums[f].shape, f32)
-        lax.fori_loop(0, self.P, one, 0)
+        lax.fori_loop(0, self.P, one, 0, unroll=4)
         for f in range(6):
             side = f % 2
             rows = jnp.concatenate(
@@ -327,15 +327,16 @@
                 value = jnp.where(kind == 1, coarse[:, h * COL : (h + 1) * COL], planes[h, rows, :])
                 gb[h, rows, :] = jnp.where(kind == 2, fine, value)
 
-    def pack_ghost_cot(self, gb, table, wide, near, out, half, half_back):
+    def pack_ghost_cot(self, gb, table, wide, near, out, parts, half, half_back):
         S, COL, H = self.S, self.COL, self.H
         low = self.low(4)
 
         def clear(peer, carry):
-            out.ref[peer, 0:48, :] = jnp.zeros((48, COL), f32)
+            for part in parts:
+                part[peer, :, :] = jnp.zeros((24, COL), f32)
             return carry
 
-        lax.fori_loop(0, self.P, clear, 0)
+        lax.fori_loop(0, self.P, clear, 0, unroll=4)
         for h in range(2):
             for g in range(2):
                 spread = dot2(gb[h, :, :], half_back[:, g * 2 * COL : (g + 1) * 2 * COL])
@@ -353,29 +354,30 @@
                 def same(base=base, axis=axis, half_row=half_row, row=row):
                     peer = table[base]
                     for q in range(2):
-                        at = axis * 16 + q * 8 + half_row
-                        out.ref[peer, at : at + 4, :] += gb[q, row : row + 4, :]
+                        at = axis * 8 + half_row
+                        parts[q][peer, at : at + 4, :] += gb[q, row : row + 4, :]
 
                 def coarse(base=base, axis=axis, half_row=half_row, row=row):
                     peer = table[base]
                     values = near[row : row + 4, :]
                     values = jnp.where(table[base + 6] == 1, roll(values, H), values)
                     for q in range(2):
-                        at = axis * 16 + q * 8 + half_row
-                        out.ref[peer, at : at + 4, :] += jnp.where(table[base + 5] == q, values, 0.0)
+                        at = axis * 8 + half_row
+                        parts[q][peer, at : at + 4, :] += jnp.where(table[base + 5] == q, values, 0.0)
 
                 def fine(base=base, axis=axis, half_row=half_row, row=row):
                     for k in range(4):
                         peer = table[base + k]
                         for q in range(2):
-                            at = axis * 16 + q * 8 + half_row
-                            out.ref[peer, at : at + 4, :] += wide[k * 2 + q, row : row + 4, :]
+                            at = axis * 8 + half_row
+                            parts[q][peer, at : at + 4, :] += wide[k * 2 + q, row : row + 4, :]
 
                 pl.when(kind == 0)(same)
                 pl.when(kind == 1)(coarse)
                 pl.when(kind == 2)(fine)
             if f % 2 == 1:
-                out.send((f // 2) * 16, 16)
+                for q in range(2):
+                    out.send((f // 2) * 16 + q * 8, 8, parts[q], (f // 2) * 8)
 
     def corrected(self, b_fb, packets, row0, table, out):
         H = self.H
@@ -465,7 +467,7 @@
                 tile(out, peer, row0 + part * 4)[...] = cb[rows, :]
             return carry
 
-        lax.fori_loop(0, self.P, one, 0)
+        lax.fori_loop(0, self.P, one, 0, unroll=4)
 
     def upward(self, packets, row0, cc, children, parents, get, put, half_back):
         S, COL = self.S, self.COL
@@ -479,7 +481,7 @@
                 cc[rows, :] += tile(packets, peer, row0 + part * 4)[...]
             return carry
 
-        lax.fori_loop(0, self.P, one, 0)
+        lax.fori_loop(0, self.P, one, 0, unroll=4)
         rows = jnp.concatenate(
             [cc[pl.ds((k // 4) * 8 + k % 4, S, stride=32), :] for k in range(16)], axis=0
         )
@@ -606,10 +608,10 @@
         self.sems = sems
         self.copies = []
 
-    def send(self, first=None, count=None):
-        near, far = self.ref, self.target
+    def send(self, first=None, count=None, ref=None, start=None):
+        near, far = self.ref if ref is None else ref, self.target
         if count is not None:
-            near = near.at[:, pl.ds(first, count), :]
+            near = near.at[:, pl.ds(first if start is None else start, count), :]
             far = far.at[:, pl.ds(first, count), :]
         copy = pltpu.make_async_copy(near, far, self.sems.at[len(self.copies)])
         copy.start()
@@ -654,7 +656,7 @@
         out_specs.append(pl.BlockSpec(memory_space=hbm if mode else pltpu.VMEM))
         if mode == "late":
             leaving[index] = len(extra)
-            extra += [pltpu.VMEM(shape, f32), pltpu.SemaphoreType.DMA((4,))]
+            extra += [pltpu.VMEM(shape, f32), pltpu.SemaphoreType.DMA((8,))]
 
     def wrapped(*refs):
         n_scalar, n_in, n_out = len(scalars), len(arrays), len(outs)
@@ -791,7 +793,8 @@
     native_planes = [vm(S * 4 * E, COL), vm(S * 4 * E, COL)]
     pair_of_sems = pltpu.SemaphoreType.DMA((2,))
     quarter_sums = [vm(S * 8, COL) for _ in range(6)]
-    face_sums = [vm(2, S * 8, COL) for _ in range(6)]
+    face_sums = [vm(S * 8, COL) for _ in range(12)]
+    cot_halves = [vm(peers, 24, COL) for _ in range(2)]
     signs = [1.0, -1.0, 1.0, -1.0, 1.0, -1.0]
 
     def layers_of(get, fb, ff):
@@ -885,14 +888,14 @@
                 tile(out, peer, row0 + axis * 4)[...] = tile(source, peer, axis * 4)[...]
             return carry
 
-        lax.fori_loop(0, peers, one, 0)
+        lax.fori_loop(0, peers, one, 0, unroll=4)
 
     def add_layers(through, layer_cot, total, sums, put):
         own = plan.ff_at(layer_cot)
         for f in range(6):
             for c in range(4):
                 for q in range(2):
-                    added = sums[f][q, pl.ds((f % 2) * 4 + c, S, stride=8), :]
+                    added = sums[f * 2 + q][pl.ds((f % 2) * 4 + c, S, stride=8), :]
                     total[q, (f * 4 + c) * S : (f * 4 + c + 1) * S, :] = own(q, f, c) + added
         get = plan.slab_at(through)
         summed = plan.ff_at(total)
@@ -906,9 +909,8 @@
         for x in range(E):
             for c in range(4):
                 for q in range(2):
-                    volume.ref[q, (x * 4 + c) * S : (x * 4 + c + 1) * S, :] = get(q, x, c)
-        volume.send()
-        layers_of(plan.slab_at(volume.ref), fb, layers.ref)
+                    volume[q, (x * 4 + c) * S : (x * 4 + c + 1) * S, :] = get(q, x, c)
+        layers_of(plan.slab_at(volume), fb, layers.ref)
         layers.send()
         plan.pack_faces(fb, send_s, packets)
         planes = guide_r.get()
@@ -917,24 +919,36 @@
         )
         packets.send(48, 16)
 
-    volume1, layers1, packets = run(
+    state1, layers1, packets = run(
         first_pack,
         "first_pack",
         [send, parents],
         [Late(native_fields, native=True), Late(native_guidance, native=True)],
-        [(plan.slab, "late"), (plan.ff, "late"), ((peers, 64, COL), "late")],
+        [(plan.slab, None), (plan.ff, "late"), ((peers, 64, COL), "late")],
         [fb_scratch],
     )
     received1 = exchange(packets)
 
-    def interior_first(levels_s, volume, partial, done):
-        plan.interior(dyn_get(volume.get()), levels_s, dyn_put(partial.ref))
+    def interior_first(levels_s, volume, guide_r, partial, kept, guide_slab, done, sems):
+        copy = pltpu.make_async_copy(volume, kept, sems.at[0])
+        copy.start()
+        get = plan.native_at(guide_r.get())
+        put = slab_put(guide_slab.ref)
+        for x in range(E):
+            for c in range(4):
+                for q in range(2):
+                    put(q, x, c, get(q, x, c))
+        guide_slab.send()
+        plan.interior(dyn_get(volume), levels_s, dyn_put(partial.ref))
         partial.send()
         done[...] = jnp.zeros(done.shape, f32)
-
-    partial1, done1 = run(
-        interior_first, "interior_first", [levels], [Late(volume1)],
-        [(plan.slab, "late"), ((8, COL), None)], [],
+        copy.wait()
+
+    partial1, volume1, guide1, done1 = run(
+        interior_first, "interior_first", [levels],
+        [state1, Late(native_guidance, native=True)],
+        [(plan.slab, "late"), (plan.slab, "raw"), (plan.slab, "late"), ((8, COL), None)],
+        [pair_of_sems],
     )
 
     def first_flux(levels_s, send_s, table_s, layers, after, recv, half_r, back_r, gb, b_fb, packets,
@@ -959,8 +973,7 @@
 
     def upward_second(levels_s, table_s, children_s, parents_s, guide_r, recv, back_r, up, cot_fb,
                       packets, cc):
-        planes = guide_r.get()
-        plan.upward(recv, 48, cc, children_s, parents_s, plan.native_at(planes), slab_put(up.ref), back_r)
+        plan.upward(recv, 48, cc, children_s, parents_s, plan.slab_at(guide_r), slab_put(up.ref), back_r)
         up.send()
         corrected_cot_of(plan.slab_at(up.ref), levels_s, cot_fb.ref)
         cot_fb.send()
@@ -971,7 +984,7 @@
         upward_second,
         "upward_second",
         [levels, table, children, parents],
-        [Late(native_guidance, native=True), received1, half_back],
+        [guide1, received1, half_back],
         [(plan.slab, "late"), (plan.fb, "late"), ((peers, 3, 4, COL), "late")],
         [vm((S + 1) * 32, COL)],
     )
@@ -995,14 +1008,13 @@
     received3 = exchange(packets)
 
     def middle_pack(send_s, parents_s, updated, recv, volume, layers, packets, fb):
-        volume.ref[...] = updated[...]
+        volume[...] = updated[...]
 
         def store(s, x, q, value):
-            volume.ref[q, plan.slab_rows(s, x), :] = value
+            volume[q, plan.slab_rows(s, x), :] = value
 
         plan.place_octants(recv, 0, parents_s, store)
-        volume.send()
-        layers_of(plan.slab_at(volume.ref), fb, layers.ref)
+        layers_of(plan.slab_at(volume), fb, layers.ref)
         layers.send()
         plan.pack_faces(fb, send_s, packets)
 
@@ -1011,7 +1023,7 @@
         "middle_pack",
         [send, parents],
         [updated1, received3],
-        [(plan.slab, "late"), (plan.ff, "late"), ((peers, 48, COL), "late")],
+        [(plan.slab, None), (plan.ff, "late"), ((peers, 48, COL), "late")],
         [fb_scratch],
     )
     received4 = exchange(packets)
@@ -1029,20 +1041,22 @@
         [kind_scratch] + quarter_sums,
     )
 
-    def interior_both(levels_s, volume, cot, partial, through):
+    def interior_both(levels_s, volume, cot, partial, through, done):
         plan.interior(
-            dyn_get(volume.get()), levels_s, dyn_put(partial.ref), dyn_get(cot.get()), dyn_put(through.ref)
+            dyn_get(volume), levels_s, dyn_put(partial.ref), dyn_get(cot.get()), dyn_put(through.ref)
         )
         partial.send()
         through.send()
-
-    partial2, through2 = run(
-        interior_both, "interior_both", [levels], [Late(volume2), Late(up2)],
-        [(plan.slab, "late"), (plan.slab, "late")], [],
-    )
-
-    def second_pull(levels_s, table_s, layers, recv, flux_cot, half_r, back_r, gb, layer_cot,
-                    packets, planes, near, kinds, gcot):
+        done[...] = jnp.zeros(done.shape, f32)
+
+    partial2, through2, done2 = run(
+        interior_both, "interior_both", [levels], [volume2, Late(up2)],
+        [(plan.slab, "late"), (plan.slab, "late"), ((8, COL), None)], [],
+    )
+
+    def second_pull(levels_s, table_s, layers, after, recv, flux_cot, half_r, back_r, gb, layer_cot,
+                    packets, planes, near, kinds, gcot, *parts):
+        del after
         plan.ghosts(recv, table_s, planes, near, kinds, gb.ref, half_r, back_r)
         gb.send()
         layer = plan.ff_at(layers)
@@ -1051,15 +1065,15 @@
             cot_emitter(layer_cot.ref, gcot),
         )
         layer_cot.send()
-        plan.pack_ghost_cot(gcot, table_s, planes, near, packets, half_r, back_r)
+        plan.pack_ghost_cot(gcot, table_s, planes, near, packets, parts, half_r, back_r)
 
     ghosts2, layercot2, packets = run(
         second_pull,
         "second_pull",
         [levels, table],
-        [layers2, received4, Late(fluxcot2), half, half_back],
+        [layers2, done2, received4, Late(fluxcot2), half, half_back],
         [(plan.fb, "late"), (plan.ff, "late"), ((peers, 48, COL), "late")],
-        ghost_scratch + [fb_scratch],
+        ghost_scratch + [fb_scratch] + cot_halves,
     )
     received5 = exchange(packets)
 
@@ -1156,7 +1170,8 @@
     )
 
     def first_pull(levels_s, send_s, table_s, children_s, layers, gb, cot_fb, recv, coarse, half_r,
-                   back_r, layer_cot, packets, planes, near, kinds, flux_cot, gcot, *sums):
+                   back_r, layer_cot, packets, planes, near, kinds, flux_cot, gcot, *late):
+        parts, sums = late[:2], late[2:]
         plan.pack_children(coarse, children_s, packets.ref, 48)
         packets.send(48, 16)
         flux_cot_of(recv, 0, cot_fb, table_s, send_s, sums, kinds, flux_cot, back_r)
@@ -1166,7 +1181,7 @@
             cot_emitter(layer_cot.ref, gcot),
         )
         layer_cot.send()
-        plan.pack_ghost_cot(gcot, table_s, planes, near, packets, half_r, back_r)
+        plan.pack_ghost_cot(gcot, table_s, planes, near, packets, parts, half_r, back_r)
 
     layercot1, packets = run(
         first_pull,
@@ -1174,7 +1189,7 @@
         [levels, send, table, children],
         [layers1, ghosts1, corrcot1, received7, coarse2, half, half_back],
         [(plan.ff, "late"), ((peers, 64, COL), "late")],
-        ghost_scratch + [vm(*plan.ff), fb_scratch] + quarter_sums,
+        ghost_scratch + [vm(*plan.ff), fb_scratch] + cot_halves + quarter_sums,
     )
     received8 = exchange(packets)
 

time: 206 us -> 206 us (level)
  transfers between devices with their start and end apart: 6 -> 6, of which waited for: 6 -> 6; matrix products, arithmetic and copies ran while one was open for 0% -> 0% of each run, Pallas kernels for 17% -> 16%
where the time goes in v5:
time: 206 us; the launch traced here: 205 us
  waiting for transfers between devices  75 us (36%)
  Pallas kernels  67.5 us (33%)
  blocking collectives  34.8 us (17%)
  starting transfers between devices  22.9 us (11%)
  local copies, waits for them, and re-layouts  3.81 us (2%)
    all_to_all x6, waiting for transfers between devices, exchange(): lax.all_to_all(packets, 'blk', split_axis=0, concat_axis=0, tiled=True)  75 us
    pallas_call x16, Pallas kernels, run(): pl.pallas_call(wrapped, name=name, in_specs=specs, out_specs=out_specs, o...  67.5 us
    all_to_all x2, blocking collectives, exchange(): lax.all_to_all(packets, 'blk', split_axis=0, concat_axis=0, tiled=True)  34.8 us
    all_to_all x6, starting transfers between devices, exchange(): lax.all_to_all(packets, 'blk', split_axis=0, concat_axis=0, tiled=True)  22.9 us
  transfers between devices with their start and end apart: 6, of which 6 were waited for; matrix products, arithmetic and copies ran while one was open for 0% of the time, Pallas kernels for 16%

profile of v5, /device:TPU:0, one launch (start us, length us, event | category | flops | bytes accessed | tf_op | source)
XLA Modules:
  0.0 205.2 jit_solution(2406574776883852086)
XLA Ops:
  0.6 0.8 copy.21
  1.4 0.0 copy-start.9
  1.4 0.7 copy-done.9
  2.1 4.1 %first_pack.1 = (f32[2,512,128]{2,1,0:T(8,128)S(1)}, f32[2,192,128]{2,1,0:T(8,128)}, f32[32,64,128]{2,1,0:T(8,128)}) custom-call(s32[32,6]{1,0:T(8,128)S(1)} %bitcast.22, s32[8,8]{1,0:T(8,128)S(1)} %copy-done.9, f32[512,256]{1,0:T(8,128)} %bitcast.36, f32[512,256]{1,0:T(8,128)} %bitcast.34), custom_call_target="tpu_custom_call" | custom-call | tf_op jit(solution)/shard_map/first_pack/pallas_call | solution.py:684
  6.2 0.0 copy-start.12
  6.2 7.5 %all-to-all-start = ((f32[32,64,128]{2,1,0:T(8,128)}), f32[32,64,128]{2,1,0:T(8,128)S(1)}, u32[]{:S(2)}, u32[]{:S(2)}) async-start(f32[32,64,128]{2,1,0:T(8,128)} %get-tuple-element.44), calls=%async_computation | async-start | bytes 2097152 | tf_op jit(solution)/shard_map/all_to_all | solution.py:783
  13.7 0.0 copy-done.12
  13.8 0.0 copy-start.13
  13.8 0.1 copy.22
  13.9 0.6 copy-done.13
  14.5 0.1 copy.23
  14.7 0.1 copy.29
  14.9 0.1 reshape.36.refs_2_.refs_1_
  14.9 0.0 copy-start.10
  15.0 0.6 copy-done.10
  15.6 0.0 copy-start
  15.6 0.0 copy-start.1
  15.6 0.0 copy-start.3
  15.6 6.0 %interior_first.1 = (f32[2,512,128]{2,1,0:T(8,128)}, f32[2,512,128]{2,1,0:T(8,128)}, f32[2,512,128]{2,1,0:T(8,128)}, f32[8,128]{1,0:T(8,128)S(1)}) custom-call(s32[8]{0:T(128)S(1)} %copy-done.10, f32[2,512,128]{2,1,0:T(8,128)S(1)} %get-tuple-element.39.refs_1_, f32[512,256]{1,0:T(8,128)} %bitcast.35), custom_call_target="tpu_custom_call" | custom-call | tf_op jit(solution)/shard_map/interior_first/pallas_call | solution.py:684
  21.6 18.3 %all-to-all-done.refs_5_ = f32[32,64,128]{2,1,0:T(8,128)S(1)} async-done(((f32[32,64,128]{2,1,0:T(8,128)}), f32[32,64,128]{2,1,0:T(8,128)S(1)}, u32[]{:S(2)}, u32[]{:S(2)}) %all-to-all-start) | async-done | bytes 1048608 | tf_op jit(solution)/shard_map/all_to_all | solution.py:783
  39.9 0.0 copy-done
  39.9 0.0 copy-done.1
  39.9 0.0 copy-done.3
  39.9 0.0 copy-start.5
  40.0 3.1 %first_flux.1 = (f32[2,192,128]{2,1,0:T(8,128)}, f32[2,192,128]{2,1,0:T(8,128)}, f32[32,3,4,128]{3,2,1,0:T(4,128)}) custom-call(s32[8]{0:T(128)S(1)} %copy-done.10, s32[32,6]{1,0:T(8,128)S(1)} %bitcast.23, s32[384]{0:T(512)S(1)} %reshape.36.refs_2_.refs_1_, f32[2,192,128]{2,1,0:T(8,128)S(1)} %copy-done.3, f32[8,128]{1,0:T(8,128)S(1)} %get-tuple-element.43.refs_4_, ...), custom_call_target="tpu_custom_call" | custom-call | tf_op jit(solution)/shard_map/first_flux/pallas_call | solution.py:684
  43.0 3.6 %all-to-all-start.1 = ((f32[32,3,4,128]{3,2,1,0:T(4,128)}), f32[32,3,4,128]{3,2,1,0:T(4,128)S(1)}, u32[]{:S(2)}, u32[]{:S(2)}) async-start(f32[32,3,4,128]{3,2,1,0:T(4,128)} %get-tuple-element.46), calls=%async_computation.1 | async-start | bytes 393216 | tf_op jit(solution)/shard_map/all_to_all | solution.py:783
  46.7 0.0 copy-start.11
  46.7 0.0 copy-done.5
  46.7 0.6 copy-done.11
  47.3 0.0 copy-start.4
  47.3 0.0 copy-start.8
  47.3 4.5 %upward_second.1 = (f32[2,512,128]{2,1,0:T(8,128)}, f32[2,192,128]{2,1,0:T(8,128)}, f32[32,3,4,128]{3,2,1,0:T(4,128)}) custom-call(s32[8]{0:T(128)S(1)} %copy-done.10, s32[384]{0:T(512)S(1)} %reshape.36.refs_2_.refs_1_, s32[32]{0:T(128)S(1)} %bitcast.30, s32[8,8]{1,0:T(8,128)S(1)} %copy-done.9, f32[2,512,128]{2,1,0:T(8,128)S(1)} %copy-done.5, ...), custom_call_target="tpu_custom_call" | custom-call | tf_op jit(solution)/shard_map/upward_second/pallas_call | solution.py:684
  51.8 3.8 %all-to-all-done.1.refs_5_ = f32[32,3,4,128]{3,2,1,0:T(4,128)S(1)} async-done(((f32[32,3,4,128]{3,2,1,0:T(4,128)}), f32[32,3,4,128]{3,2,1,0:T(4,128)S(1)}, u32[]{:S(2)}, u32[]{:S(2)}) %all-to-all-start.1) | async-done | bytes 196640 | tf_op jit(solution)/shard_map/all_to_all | solution.py:783
  55.6 0.0 copy-done.4
  55.6 0.0 copy-done.8
  55.6 3.3 %first_update.1 = (f32[2,512,128]{2,1,0:T(8,128)S(1)}, f32[32,7,4,128]{3,2,1,0:T(4,128)S(1)}) custom-call(s32[8]{0:T(128)S(1)} %copy-done.10, s32[384]{0:T(512)S(1)} %reshape.36.refs_2_.refs_1_, s32[32]{0:T(128)S(1)} %bitcast.31, f32[2,512,128]{2,1,0:T(8,128)S(1)} %copy-done.4, f32[2,192,128]{2,1,0:T(8,128)S(1)} %copy-done.8, ...), custom_call_target="tpu_custom_call" | custom-call | tf_op jit(solution)/shard_map/first_update/pallas_call | solution.py:684
  58.9 16.8 %all_to_all.40.refs_3_ = f32[32,7,4,128]{3,2,1,0:T(4,128)S(1)} all-to-all(f32[32,7,4,128]{3,2,1,0:T(4,128)S(1)} %get-tuple-element.50), channel_id=1, replica_groups=mesh['blk'=32] {'blk'}, dimensions={0} | all-to-all | bytes 917504 | tf_op jit(solution)/shard_map/all_to_all | solution.py:783
  75.7 2.9 %middle_pack.1 = (f32[2,512,128]{2,1,0:T(8,128)S(1)}, f32[2,192,128]{2,1,0:T(8,128)}, f32[32,48,128]{2,1,0:T(8,128)}) custom-call(s32[32,6]{1,0:T(8,128)S(1)} %bitcast.24, s32[8,8]{1,0:T(8,128)S(1)} %copy-done.9, f32[2,512,128]{2,1,0:T(8,128)S(1)} %get-tuple-element.49.refs_2_, f32[32,7,4,128]{3,2,1,0:T(4,128)S(1)} %all_to_all.40.refs_3_), custom_call_target="tpu_custom_call" | custom-call | tf_op jit(solution)/shard_map/middle_pack/pallas_call | solution.py:684
  78.6 2.9 %all-to-all-start.3 = ((f32[32,48,128]{2,1,0:T(8,128)}), f32[32,48,128]{2,1,0:T(8,128)S(1)}, u32[]{:S(2)}, u32[]{:S(2)}) async-start(f32[32,48,128]{2,1,0:T(8,128)} %get-tuple-element.56), calls=%async_computation.3 | async-start | bytes 1572864 | tf_op jit(solution)/shard_map/all_to_all | solution.py:783
  81.6 6.1 %interior_both.1 = (f32[2,512,128]{2,1,0:T(8,128)}, f32[2,512,128]{2,1,0:T(8,128)}, f32[8,128]{1,0:T(8,128)S(1)}) custom-call(s32[8]{0:T(128)S(1)} %copy-done.10, f32[2,512,128]{2,1,0:T(8,128)S(1)} %get-tuple-element.51.refs_1_, f32[2,512,128]{2,1,0:T(8,128)} %get-tuple-element.52.refs_2_), custom_call_target="tpu_custom_call" | custom-call | tf_op jit(solution)/shard_map/interior_both/pallas_call | solution.py:684
  87.7 0.0 copy-start.2
  87.7 3.1 %flux_cot_second.1.refs_5_ = f32[2,192,128]{2,1,0:T(8,128)} custom-call(s32[32,6]{1,0:T(8,128)S(1)} %bitcast.25, s32[384]{0:T(512)S(1)} %reshape.36.refs_2_.refs_1_, f32[2,192,128]{2,1,0:T(8,128)} %get-tuple-element.57.refs_2_, f32[32,7,4,128]{3,2,1,0:T(4,128)S(1)} %all_to_all.40.refs_3_, bf16[128,512]{1,0:T(8,128)(2,1)S(1)} %copy-done), custom_call_target="tpu_custom_call" | custom-call | tf_op jit(solution)/shard_map/flux_cot_second/pallas_call | solution.py:684
  90.8 11.4 %all-to-all-done.3.refs_4_ = f32[32,48,128]{2,1,0:T(8,128)S(1)} async-done(((f32[32,48,128]{2,1,0:T(8,128)}), f32[32,48,128]{2,1,0:T(8,128)S(1)}, u32[]{:S(2)}, u32[]{:S(2)}) %all-to-all-start.3) | async-done | bytes 786464 | tf_op jit(solution)/shard_map/all_to_all | solution.py:783
  102.2 0.0 copy-done.2
  102.2 5.1 %second_pull.1 = (f32[2,192,128]{2,1,0:T(8,128)}, f32[2,192,128]{2,1,0:T(8,128)}, f32[32,48,128]{2,1,0:T(8,128)}) custom-call(s32[8]{0:T(128)S(1)} %copy-done.10, s32[384]{0:T(512)S(1)} %reshape.36.refs_2_.refs_1_, f32[2,192,128]{2,1,0:T(8,128)S(1)} %copy-done.2, f32[8,128]{1,0:T(8,128)S(1)} %get-tuple-element.55.refs_3_, ...), custom_call_target="tpu_custom_call" | custom-call | tf_op jit(solution)/shard_map/second_pull/pallas_call | solution.py:684
  107.3 3.5 %all-to-all-start.4 = ((f32[32,48,128]{2,1,0:T(8,128)}), f32[32,48,128]{2,1,0:T(8,128)S(1)}, u32[]{:S(2)}, u32[]{:S(2)}) async-start(f32[32,48,128]{2,1,0:T(8,128)} %get-tuple-element.59), calls=%async_computation.4 | async-start | bytes 1572864 | tf_op jit(solution)/shard_map/all_to_all | solution.py:783
  110.8 3.3 %second_flux.1 = (f32[2,192,128]{2,1,0:T(8,128)}, f32[32,3,4,128]{3,2,1,0:T(4,128)}) custom-call(s32[8]{0:T(128)S(1)} %copy-done.10, s32[32,6]{1,0:T(8,128)S(1)} %bitcast.26, f32[2,192,128]{2,1,0:T(8,128)} %get-tuple-element.54.refs_2_, f32[2,192,128]{2,1,0:T(8,128)} %get-tuple-element.60.refs_3_, bf16[512,128]{1,0:T(8,128)(2,1)S(1)} %copy-done.1), custom_call_target="tpu_custom_call" | custom-call | tf_op jit(solution)/shard_map/second_flux/pallas_call | solution.py:684
  114.1 17.3 %all-to-all-done.4.refs_4_ = f32[32,48,128]{2,1,0:T(8,128)S(1)} async-done(((f32[32,48,128]{2,1,0:T(8,128)}), f32[32,48,128]{2,1,0:T(8,128)S(1)}, u32[]{:S(2)}, u32[]{:S(2)}) %all-to-all-start.4) | async-done | bytes 786464 | tf_op jit(solution)/shard_map/all_to_all | solution.py:783
  131.4 2.8 %middle_cot.1 = (f32[2,512,128]{2,1,0:T(8,128)S(1)}, f32[32,7,4,128]{3,2,1,0:T(4,128)S(1)}) custom-call(s32[32,6]{1,0:T(8,128)S(1)} %bitcast.27, s32[8,8]{1,0:T(8,128)S(1)} %copy-done.9, f32[2,512,128]{2,1,0:T(8,128)} %get-tuple-element.53.refs_2_, f32[2,192,128]{2,1,0:T(8,128)} %get-tuple-element.58.refs_3_, f32[32,48,128]{2,1,0:T(8,128)S(1)} %all-to-all-done.4.refs_4_, ...), custom_call_target="tpu_custom_call" | custom-call | tf_op jit(solution)/shard_map/middle_cot/pallas_call | solution.py:684
  134.1 18.0 %all_to_all.41.refs_5_.refs_4_ = f32[32,7,4,128]{3,2,1,0:T(4,128)S(1)} all-to-all(f32[32,7,4,128]{3,2,1,0:T(4,128)S(1)} %get-tuple-element.63), channel_id=1, replica_groups=mesh['blk'=32] {'blk'}, dimensions={0} | all-to-all | bytes 917504 | tf_op jit(solution)/shard_map/all_to_all | solution.py:783
  152.2 4.4 %upward_first.1 = (f32[2,512,128]{2,1,0:T(8,128)}, f32[2,192,128]{2,1,0:T(8,128)}, f32[32,3,4,128]{3,2,1,0:T(4,128)}) custom-call(s32[8]{0:T(128)S(1)} %copy-done.10, s32[384]{0:T(512)S(1)} %reshape.36.refs_2_.refs_1_, s32[32]{0:T(128)S(1)} %bitcast.32, s32[8,8]{1,0:T(8,128)S(1)} %copy-done.9, f32[2,512,128]{2,1,0:T(8,128)S(1)} %get-tuple-element.62.refs_4_, ...), custom_call_target="tpu_custom_call" | custom-call | tf_op jit(solution)/shard_map/upward_first/pallas_call | solution.py:684
  156.6 2.6 %all-to-all-start.6 = ((f32[32,3,4,128]{3,2,1,0:T(4,128)}), f32[32,3,4,128]{3,2,1,0:T(4,128)S(1)}, u32[]{:S(2)}, u32[]{:S(2)}) async-start(f32[32,3,4,128]{3,2,1,0:T(4,128)} %get-tuple-element.67), calls=%async_computation.6 | async-start | bytes 393216 | tf_op jit(solution)/shard_map/all_to_all | solution.py:783
  159.2 0.0 copy-start.6
  159.2 0.0 copy-start.7
  159.2 5.0 %second_update.1 = (f32[512,256]{1,0:T(8,128)}, f32[256,128]{1,0:T(8,128)S(1)}) custom-call(s32[8]{0:T(128)S(1)} %copy-done.10, s32[384]{0:T(512)S(1)} %reshape.36.refs_2_.refs_1_, f32[2,512,128]{2,1,0:T(8,128)} %get-tuple-element.68.refs_2_, f32[2,192,128]{2,1,0:T(8,128)} %get-tuple-element.69.refs_3_, f32[32,7,4,128]{3,2,1,0:T(4,128)S(1)} %all_to_all.41.refs_5_.refs_4_, ...), custom_call_target="tpu_custom_call" | custom-call | tf_op jit(solution)/shard_map/second_update/pallas_call | solution.py:684
  164.2 3.9 %all-to-all-done.6.refs_7_ = f32[32,3,4,128]{3,2,1,0:T(4,128)S(1)} async-done(((f32[32,3,4,128]{3,2,1,0:T(4,128)}), f32[32,3,4,128]{3,2,1,0:T(4,128)S(1)}, u32[]{:S(2)}, u32[]{:S(2)}) %all-to-all-start.6) | async-done | bytes 196640 | tf_op jit(solution)/shard_map/all_to_all | solution.py:783
  168.2 0.0 copy-done.6
  168.2 0.0 copy-done.7
  168.2 4.5 %first_pull.1 = (f32[2,192,128]{2,1,0:T(8,128)}, f32[32,64,128]{2,1,0:T(8,128)}) custom-call(s32[8]{0:T(128)S(1)} %copy-done.10, s32[32,6]{1,0:T(8,128)S(1)} %bitcast.28, s32[384]{0:T(512)S(1)} %reshape.36.refs_2_.refs_1_, s32[32]{0:T(128)S(1)} %bitcast.33, f32[2,192,128]{2,1,0:T(8,128)S(1)} %copy-done.3, f32[2,192,128]{2,1,0:T(8,128)S(1)} %copy-done.6, ...), custom_call_target="tpu_custom_call" | custom-call | tf_op jit(solution)/shard_map/first_pull/pallas_call | solution.py:684
  172.7 2.7 %all-to-all-start.7 = ((f32[32,64,128]{2,1,0:T(8,128)}), f32[32,64,128]{2,1,0:T(8,128)S(1)}, u32[]{:S(2)}, u32[]{:S(2)}) async-start(f32[32,64,128]{2,1,0:T(8,128)} %get-tuple-element.72), calls=%async_computation.7 | async-start | bytes 2097152 | tf_op jit(solution)/shard_map/all_to_all | solution.py:783
  175.4 5.9 %interior_back.1.refs_2_ = f32[2,512,128]{2,1,0:T(8,128)} custom-call(s32[8]{0:T(128)S(1)} %copy-done.10, f32[2,512,128]{2,1,0:T(8,128)} %get-tuple-element.40.refs_1_, f32[2,512,128]{2,1,0:T(8,128)} %get-tuple-element.64.refs_2_), custom_call_target="tpu_custom_call" | custom-call | tf_op jit(solution)/shard_map/interior_back/pallas_call | solution.py:684
  181.2 20.3 %all-to-all-done.7.refs_4_ = f32[32,64,128]{2,1,0:T(8,128)S(1)} async-done(((f32[32,64,128]{2,1,0:T(8,128)}), f32[32,64,128]{2,1,0:T(8,128)S(1)}, u32[]{:S(2)}, u32[]{:S(2)}) %all-to-all-start.7) | async-done | bytes 1048608 | tf_op jit(solution)/shard_map/all_to_all | solution.py:783
  201.6 3.5 %last_cot.1 = (f32[512,256]{1,0:T(8,128)}, f32[512,256]{1,0:T(8,128)}) custom-call(s32[32,6]{1,0:T(8,128)S(1)} %bitcast.29, s32[8,8]{1,0:T(8,128)S(1)} %copy-done.9, f32[2,512,128]{2,1,0:T(8,128)} %interior_back.1.refs_2_, f32[2,192,128]{2,1,0:T(8,128)} %get-tuple-element.71.refs_3_, ...), custom_call_target="tpu_custom_call", output_to_operand_aliasing={{1}: (5, {})} | custom-call | tf_op jit(solution)/shard_map/last_cot/pallas_call | solution.py:684
  (11 shorter events, 0.1 us)
Async XLA Ops:
  1.4 0.7 copy-start.9
  6.2 7.6 %copy-start.12 = (s32[8,6,4]{0,2,1:T(4,128)S(1)}, s32[8,6,4]{0,2,1:T(4,128)}, u32[]{:S(2)}) copy-start(s32[8,6,4]{0,2,1:T(4,128)} %param.14) | copy-start | bytes 2308
  6.2 33.7 %all-to-all-start = ((f32[32,64,128]{2,1,0:T(8,128)}), f32[32,64,128]{2,1,0:T(8,128)S(1)}, u32[]{:S(2)}, u32[]{:S(2)}) async-start(f32[32,64,128]{2,1,0:T(8,128)} %get-tuple-element.44), calls=%async_computation | async-start | bytes 2097152 | tf_op jit(solution)/shard_map/all_to_all | solution.py:783
  13.8 0.7 copy-start.13
  14.9 0.7 copy-start.10
  15.6 24.3 %copy-start = (bf16[128,512]{1,0:T(8,128)(2,1)S(1)}, bf16[128,512]{1,0:T(8,128)(2,1)}, u32[]{:S(2)}) copy-start(bf16[128,512]{1,0:T(8,128)(2,1)} %constant.45.clone.refs_7_.refs_6_.refs_4_.refs_10_) | copy-start | bytes 393220
  15.6 24.3 %copy-start.1 = (bf16[512,128]{1,0:T(8,128)(2,1)S(1)}, bf16[512,128]{1,0:T(8,128)(2,1)}, u32[]{:S(2)}) copy-start(bf16[512,128]{1,0:T(8,128)(2,1)} %constant.44.clone.refs_6_.refs_7_.refs_4_.refs_5_.refs_9_) | copy-start | bytes 393220
  15.6 24.3 %copy-start.3 = (f32[2,192,128]{2,1,0:T(8,128)S(1)}, f32[2,192,128]{2,1,0:T(8,128)}, u32[]{:S(2)}) copy-start(f32[2,192,128]{2,1,0:T(8,128)} %get-tuple-element.42.refs_3_.refs_4_) | copy-start | bytes 589828
  39.9 6.7 %copy-start.5 = (f32[2,512,128]{2,1,0:T(8,128)S(1)}, f32[2,512,128]{2,1,0:T(8,128)}, u32[]{:S(2)}) copy-start(f32[2,512,128]{2,1,0:T(8,128)} %get-tuple-element.47.refs_4_) | copy-start | bytes 1572868
  43.0 12.6 %all-to-all-start.1 = ((f32[32,3,4,128]{3,2,1,0:T(4,128)}), f32[32,3,4,128]{3,2,1,0:T(4,128)S(1)}, u32[]{:S(2)}, u32[]{:S(2)}) async-start(f32[32,3,4,128]{3,2,1,0:T(4,128)} %get-tuple-element.46), calls=%async_computation.1 | async-start | bytes 393216 | tf_op jit(solution)/shard_map/all_to_all | solution.py:783
  46.7 0.7 copy-start.11
  47.3 8.3 %copy-start.4 = (f32[2,512,128]{2,1,0:T(8,128)S(1)}, f32[2,512,128]{2,1,0:T(8,128)}, u32[]{:S(2)}) copy-start(f32[2,512,128]{2,1,0:T(8,128)} %get-tuple-element.41.refs_3_) | copy-start | bytes 1572868
  47.3 8.3 %copy-start.8 = (f32[2,192,128]{2,1,0:T(8,128)S(1)}, f32[2,192,128]{2,1,0:T(8,128)}, u32[]{:S(2)}) copy-start(f32[2,192,128]{2,1,0:T(8,128)} %get-tuple-element.45.refs_4_) | copy-start | bytes 589828
  78.6 23.5 %all-to-all-start.3 = ((f32[32,48,128]{2,1,0:T(8,128)}), f32[32,48,128]{2,1,0:T(8,128)S(1)}, u32[]{:S(2)}, u32[]{:S(2)}) async-start(f32[32,48,128]{2,1,0:T(8,128)} %get-tuple-element.56), calls=%async_computation.3 | async-start | bytes 1572864 | tf_op jit(solution)/shard_map/all_to_all | solution.py:783
  87.7 14.5 %copy-start.2 = (f32[2,192,128]{2,1,0:T(8,128)S(1)}, f32[2,192,128]{2,1,0:T(8,128)}, u32[]{:S(2)}) copy-start(f32[2,192,128]{2,1,0:T(8,128)} %get-tuple-element.54.refs_2_) | copy-start | bytes 589828
  107.3 24.1 %all-to-all-start.4 = ((f32[32,48,128]{2,1,0:T(8,128)}), f32[32,48,128]{2,1,0:T(8,128)S(1)}, u32[]{:S(2)}, u32[]{:S(2)}) async-start(f32[32,48,128]{2,1,0:T(8,128)} %get-tuple-element.59), calls=%async_computation.4 | async-start | bytes 1572864 | tf_op jit(solution)/shard_map/all_to_all | solution.py:783
  156.6 11.6 %all-to-all-start.6 = ((f32[32,3,4,128]{3,2,1,0:T(4,128)}), f32[32,3,4,128]{3,2,1,0:T(4,128)S(1)}, u32[]{:S(2)}, u32[]{:S(2)}) async-start(f32[32,3,4,128]{3,2,1,0:T(4,128)} %get-tuple-element.67), calls=%async_computation.6 | async-start | bytes 393216 | tf_op jit(solution)/shard_map/all_to_all | solution.py:783
  159.2 9.0 %copy-start.6 = (f32[2,192,128]{2,1,0:T(8,128)S(1)}, f32[2,192,128]{2,1,0:T(8,128)}, u32[]{:S(2)}) copy-start(f32[2,192,128]{2,1,0:T(8,128)} %get-tuple-element.65.refs_5_) | copy-start | bytes 589828
  159.2 8.9 %copy-start.7 = (f32[2,192,128]{2,1,0:T(8,128)S(1)}, f32[2,192,128]{2,1,0:T(8,128)}, u32[]{:S(2)}) copy-start(f32[2,192,128]{2,1,0:T(8,128)} %get-tuple-element.66.refs_6_) | copy-start | bytes 589828
  172.7 28.9 %all-to-all-start.7 = ((f32[32,64,128]{2,1,0:T(8,128)}), f32[32,64,128]{2,1,0:T(8,128)S(1)}, u32[]{:S(2)}, u32[]{:S(2)}) async-start(f32[32,64,128]{2,1,0:T(8,128)} %get-tuple-element.72), calls=%async_computation.7 | async-start | bytes 2097152 | tf_op jit(solution)/shard_map/all_to_all | solution.py:783

commit v6 on v5

--- a/solution.py
+++ b/solution.py
@@ -191,7 +191,7 @@
         for axis in range(3):
 
             def one(peer, carry, axis=axis):
-                slots = [jnp.maximum(send[peer, axis * 2 + side], 0) for side in range(2)]
+                slots = [jnp.maximum(send[axis * 2 + side, 0, peer], 0) for side in range(2)]
                 for q in range(2):
                     lo, hi = [
                         fb[q, pl.ds(pl.multiple_of((axis * self.S + slot) * 8, 8), 8), :]
@@ -207,7 +207,7 @@
     def take_faces(self, packets, send, sums):
         def one(peer, carry):
             for f in range(6):
-                slot = jnp.maximum(send[peer, f], 0)
+                slot = jnp.maximum(send[f, 0, peer], 0)
                 rows = pl.ds(pl.multiple_of(slot * 8, 8), 8)
                 for q in range(2):
                     at = (f // 2) * 16 + q * 8
@@ -237,7 +237,7 @@
             for axis in range(3):
                 lo, hi = [
                     rb[pl.ds(pl.multiple_of(slot * 24 + axis * 8, 8), 4), :]
-                    for slot in [jnp.maximum(send[peer, axis * 2 + side], 0) for side in range(2)]
+                    for slot in [jnp.maximum(send[axis * 2 + side, 0, peer], 0) for side in range(2)]
                 ]
                 tile(out, peer, row0 + axis * 4)[...] = jnp.where(low, lo, hi)
             return carry
@@ -279,7 +279,7 @@
             for axis in range(3):
                 block = tile(packets, peer, row0 + axis * 4)[...]
                 for f in (axis * 2, axis * 2 + 1):
-                    slot = jnp.maximum(send[peer, f], 0)
+                    slot = jnp.maximum(send[f, 0, peer], 0)
                     sums[f][pl.ds(pl.multiple_of(slot * 8, 8), 4), :] += block
             return carry
 
@@ -773,7 +773,7 @@
         jnp.zeros_like(kind),
     ]
     table = jnp.stack(columns, axis=-1).astype(jnp.int32).reshape(-1)
-    send = send_faces.reshape(peers, 6)
+    send = jnp.transpose(send_faces, (2, 0, 1))
     children = child_send.reshape(-1)
     parents = parent_peer
     native_fields = fields.reshape(plan.native)
@@ -890,7 +890,7 @@
 
         lax.fori_loop(0, peers, one, 0, unroll=4)
 
-    def add_layers(through, layer_cot, total, sums, put):
+    def add_layers(through, layer_cot, total, sums, put, finish=None):
         own = plan.ff_at(layer_cot)
         for f in range(6):
             for c in range(4):
@@ -899,10 +899,12 @@
                     total[q, (f * 4 + c) * S : (f * 4 + c + 1) * S, :] = own(q, f, c) + added
         get = plan.slab_at(through)
         summed = plan.ff_at(total)
-        for x in range(E):
-            for c in range(4):
-                for q in range(2):
+        for q in range(2):
+            for x in range(E):
+                for c in range(4):
                     put(q, x, c, get(q, x, c) + plan.spread(summed, q, x, c))
+            if finish is not None:
+                finish(q)
 
     def first_pack(send_s, parents_s, fields_r, guide_r, volume, layers, packets, fb):
         get = plan.native_at(fields_r.get())
@@ -1220,10 +1222,10 @@
         def put(q, x, c, value):
             planes[q][pl.ds(c * E + x, S, stride=4 * E), :] = value
 
-        add_layers(through.get(), layer_cot.get(), total, sums, put)
         copies = native_copies(planes, gradient, sems, False)
-        for copy in copies:
-            copy.start()
+        add_layers(
+            through.get(), layer_cot.get(), total, sums, put, lambda q: copies[q].start()
+        )
         for copy in copies:
             copy.wait()
         each_covered(lambda copy: copy.wait())

time: 206 us -> 204 us (level)
  transfers between devices with their start and end apart: 6 -> 6, of which waited for: 6 -> 6; matrix products, arithmetic and copies ran while one was open for 0% -> 0% of each run, Pallas kernels for 16% -> 17%
where the time goes in v6:
time: 204 us; the launch traced here: 202 us
  waiting for transfers between devices  75.1 us (37%)
  Pallas kernels  66.5 us (33%)
  blocking collectives  33.8 us (17%)
  starting transfers between devices  21.7 us (11%)
  local copies, waits for them, and re-layouts  3.72 us (2%)
    all_to_all x6, waiting for transfers between devices, exchange(): lax.all_to_all(packets, 'blk', split_axis=0, concat_axis=0, tiled=True)  75.1 us
    pallas_call x16, Pallas kernels, run(): pl.pallas_call(wrapped, name=name, in_specs=specs, out_specs=out_specs, o...  66.5 us
    all_to_all x2, blocking collectives, exchange(): lax.all_to_all(packets, 'blk', split_axis=0, concat_axis=0, tiled=True)  33.8 us
    all_to_all x6, starting transfers between devices, exchange(): lax.all_to_all(packets, 'blk', split_axis=0, concat_axis=0, tiled=True)  21.7 us
  transfers between devices with their start and end apart: 6, of which 6 were waited for; matrix products, arithmetic and copies ran while one was open for 0% of the time, Pallas kernels for 17%

profile of v6, /device:TPU:0, one launch (start us, length us, event | category | flops | bytes accessed | tf_op | source)
XLA Modules:
  0.0 202.2 jit_solution(3188061072910664636)
XLA Ops:
  0.6 0.0 copy-start.6
  0.6 0.7 copy-done.6
  1.3 0.0 copy-start.10
  1.3 0.7 copy-done.10
  2.0 4.1 %first_pack.1 = (f32[2,512,128]{2,1,0:T(8,128)S(1)}, f32[2,192,128]{2,1,0:T(8,128)}, f32[32,64,128]{2,1,0:T(8,128)}) custom-call(s32[6,1,32]{2,1,0:T(1,128)S(1)} %bitcast.22, s32[8,8]{1,0:T(8,128)S(1)} %copy-done.10, f32[512,256]{1,0:T(8,128)} %bitcast.37, f32[512,256]{1,0:T(8,128)} %bitcast.34), custom_call_target="tpu_custom_call" | custom-call | tf_op jit(solution)/shard_map/first_pack/pallas_call | solution.py:684
  6.1 0.0 copy-start.14
  6.1 7.1 %all-to-all-start = ((f32[32,64,128]{2,1,0:T(8,128)}), f32[32,64,128]{2,1,0:T(8,128)S(1)}, u32[]{:S(2)}, u32[]{:S(2)}) async-start(f32[32,64,128]{2,1,0:T(8,128)} %get-tuple-element.44), calls=%async_computation | async-start | bytes 2097152 | tf_op jit(solution)/shard_map/all_to_all | solution.py:783
  13.2 0.0 copy-done.14
  13.3 0.0 copy-start.15
  13.3 0.1 copy.20
  13.4 0.6 copy-done.15
  14.0 0.1 copy.21
  14.2 0.1 copy.27
  14.4 0.1 reshape.32.refs_2_.refs_1_
  14.5 0.0 copy-start.12
  14.5 0.6 copy-done.12
  15.1 0.0 copy-start
  15.1 0.0 copy-start.1
  15.1 0.0 copy-start.2
  15.1 6.0 %interior_first.1 = (f32[2,512,128]{2,1,0:T(8,128)}, f32[2,512,128]{2,1,0:T(8,128)}, f32[2,512,128]{2,1,0:T(8,128)}, f32[8,128]{1,0:T(8,128)S(1)}) custom-call(s32[8]{0:T(128)S(1)} %copy-done.12, f32[2,512,128]{2,1,0:T(8,128)S(1)} %get-tuple-element.39.refs_1_, f32[512,256]{1,0:T(8,128)} %bitcast.35), custom_call_target="tpu_custom_call" | custom-call | tf_op jit(solution)/shard_map/interior_first/pallas_call | solution.py:684
  21.1 18.3 %all-to-all-done.refs_5_ = f32[32,64,128]{2,1,0:T(8,128)S(1)} async-done(((f32[32,64,128]{2,1,0:T(8,128)}), f32[32,64,128]{2,1,0:T(8,128)S(1)}, u32[]{:S(2)}, u32[]{:S(2)}) %all-to-all-start) | async-done | bytes 1048608 | tf_op jit(solution)/shard_map/all_to_all | solution.py:783
  39.4 0.0 copy-done
  39.4 0.0 copy-done.1
  39.4 0.0 copy-done.2
  39.5 0.0 copy-start.5
  39.5 2.8 %first_flux.1 = (f32[2,192,128]{2,1,0:T(8,128)}, f32[2,192,128]{2,1,0:T(8,128)}, f32[32,3,4,128]{3,2,1,0:T(4,128)}) custom-call(s32[8]{0:T(128)S(1)} %copy-done.12, s32[6,1,32]{2,1,0:T(1,128)S(1)} %bitcast.23, s32[384]{0:T(512)S(1)} %reshape.32.refs_2_.refs_1_, f32[2,192,128]{2,1,0:T(8,128)S(1)} %copy-done.2, f32[8,128]{1,0:T(8,128)S(1)} %get-tuple-element.43.refs_4_, ...), custom_call_target="tpu_custom_call" | custom-call | tf_op jit(solution)/shard_map/first_flux/pallas_call | solution.py:684
  42.3 0.0 copy-start.11
  42.3 3.6 %all-to-all-start.1 = ((f32[32,3,4,128]{3,2,1,0:T(4,128)}), f32[32,3,4,128]{3,2,1,0:T(4,128)S(1)}, u32[]{:S(2)}, u32[]{:S(2)}) async-start(f32[32,3,4,128]{3,2,1,0:T(4,128)} %get-tuple-element.46), calls=%async_computation.1 | async-start | bytes 393216 | tf_op jit(solution)/shard_map/all_to_all | solution.py:783
  45.9 0.0 copy-start.13
  45.9 0.0 copy-done.5
  45.9 0.0 copy-done.11
  45.9 0.6 copy-done.13
  46.6 4.6 %upward_second.1 = (f32[2,512,128]{2,1,0:T(8,128)}, f32[2,192,128]{2,1,0:T(8,128)}, f32[32,3,4,128]{3,2,1,0:T(4,128)}) custom-call(s32[8]{0:T(128)S(1)} %copy-done.12, s32[384]{0:T(512)S(1)} %reshape.32.refs_2_.refs_1_, s32[32]{0:T(128)S(1)} %bitcast.30, s32[8,8]{1,0:T(8,128)S(1)} %copy-done.11, f32[2,512,128]{2,1,0:T(8,128)S(1)} %copy-done.5, ...), custom_call_target="tpu_custom_call" | custom-call | tf_op jit(solution)/shard_map/upward_second/pallas_call | solution.py:684
  51.2 3.7 %all-to-all-done.1.refs_5_ = f32[32,3,4,128]{3,2,1,0:T(4,128)S(1)} async-done(((f32[32,3,4,128]{3,2,1,0:T(4,128)}), f32[32,3,4,128]{3,2,1,0:T(4,128)S(1)}, u32[]{:S(2)}, u32[]{:S(2)}) %all-to-all-start.1) | async-done | bytes 196640 | tf_op jit(solution)/shard_map/all_to_all | solution.py:783
  54.9 0.0 copy-done.4
  54.9 0.0 copy-done.9
  54.9 3.4 %first_update.1 = (f32[2,512,128]{2,1,0:T(8,128)S(1)}, f32[32,7,4,128]{3,2,1,0:T(4,128)S(1)}) custom-call(s32[8]{0:T(128)S(1)} %copy-done.12, s32[384]{0:T(512)S(1)} %reshape.32.refs_2_.refs_1_, s32[32]{0:T(128)S(1)} %bitcast.31, f32[2,512,128]{2,1,0:T(8,128)S(1)} %copy-done.4, f32[2,192,128]{2,1,0:T(8,128)S(1)} %copy-done.9, ...), custom_call_target="tpu_custom_call" | custom-call | tf_op jit(solution)/shard_map/first_update/pallas_call | solution.py:684
  58.3 16.2 %all_to_all.40.refs_3_ = f32[32,7,4,128]{3,2,1,0:T(4,128)S(1)} all-to-all(f32[32,7,4,128]{3,2,1,0:T(4,128)S(1)} %get-tuple-element.50), channel_id=1, replica_groups=mesh['blk'=32] {'blk'}, dimensions={0} | all-to-all | bytes 917504 | tf_op jit(solution)/shard_map/all_to_all | solution.py:783
  74.4 2.9 %middle_pack.1 = (f32[2,512,128]{2,1,0:T(8,128)S(1)}, f32[2,192,128]{2,1,0:T(8,128)}, f32[32,48,128]{2,1,0:T(8,128)}) custom-call(s32[6,1,32]{2,1,0:T(1,128)S(1)} %bitcast.24, s32[8,8]{1,0:T(8,128)S(1)} %copy-done.11, f32[2,512,128]{2,1,0:T(8,128)S(1)} %get-tuple-element.49.refs_2_, f32[32,7,4,128]{3,2,1,0:T(4,128)S(1)} %all_to_all.40.refs_3_), custom_call_target="tpu_custom_call" | custom-call | tf_op jit(solution)/shard_map/middle_pack/pallas_call | solution.py:684
  77.3 2.6 %all-to-all-start.3 = ((f32[32,48,128]{2,1,0:T(8,128)}), f32[32,48,128]{2,1,0:T(8,128)S(1)}, u32[]{:S(2)}, u32[]{:S(2)}) async-start(f32[32,48,128]{2,1,0:T(8,128)} %get-tuple-element.56), calls=%async_computation.3 | async-start | bytes 1572864 | tf_op jit(solution)/shard_map/all_to_all | solution.py:783
  80.0 6.1 %interior_both.1 = (f32[2,512,128]{2,1,0:T(8,128)}, f32[2,512,128]{2,1,0:T(8,128)}, f32[8,128]{1,0:T(8,128)S(1)}) custom-call(s32[8]{0:T(128)S(1)} %copy-done.12, f32[2,512,128]{2,1,0:T(8,128)S(1)} %get-tuple-element.51.refs_1_, f32[2,512,128]{2,1,0:T(8,128)} %get-tuple-element.52.refs_2_), custom_call_target="tpu_custom_call" | custom-call | tf_op jit(solution)/shard_map/interior_both/pallas_call | solution.py:684
  86.1 0.0 copy-start.3
  86.1 3.0 %flux_cot_second.1.refs_5_ = f32[2,192,128]{2,1,0:T(8,128)} custom-call(s32[6,1,32]{2,1,0:T(1,128)S(1)} %bitcast.25, s32[384]{0:T(512)S(1)} %reshape.32.refs_2_.refs_1_, f32[2,192,128]{2,1,0:T(8,128)} %get-tuple-element.57.refs_2_, f32[32,7,4,128]{3,2,1,0:T(4,128)S(1)} %all_to_all.40.refs_3_, bf16[128,512]{1,0:T(8,128)(2,1)S(1)} %copy-done), custom_call_target="tpu_custom_call" | custom-call | tf_op jit(solution)/shard_map/flux_cot_second/pallas_call | solution.py:684
  89.1 11.5 %all-to-all-done.3.refs_4_ = f32[32,48,128]{2,1,0:T(8,128)S(1)} async-done(((f32[32,48,128]{2,1,0:T(8,128)}), f32[32,48,128]{2,1,0:T(8,128)S(1)}, u32[]{:S(2)}, u32[]{:S(2)}) %all-to-all-start.3) | async-done | bytes 786464 | tf_op jit(solution)/shard_map/all_to_all | solution.py:783
  100.6 0.0 copy-done.3
  100.6 5.0 %second_pull.1 = (f32[2,192,128]{2,1,0:T(8,128)}, f32[2,192,128]{2,1,0:T(8,128)}, f32[32,48,128]{2,1,0:T(8,128)}) custom-call(s32[8]{0:T(128)S(1)} %copy-done.12, s32[384]{0:T(512)S(1)} %reshape.32.refs_2_.refs_1_, f32[2,192,128]{2,1,0:T(8,128)S(1)} %copy-done.3, f32[8,128]{1,0:T(8,128)S(1)} %get-tuple-element.55.refs_3_, ...), custom_call_target="tpu_custom_call" | custom-call | tf_op jit(solution)/shard_map/second_pull/pallas_call | solution.py:684
  105.5 3.0 %all-to-all-start.4 = ((f32[32,48,128]{2,1,0:T(8,128)}), f32[32,48,128]{2,1,0:T(8,128)S(1)}, u32[]{:S(2)}, u32[]{:S(2)}) async-start(f32[32,48,128]{2,1,0:T(8,128)} %get-tuple-element.59), calls=%async_computation.4 | async-start | bytes 1572864 | tf_op jit(solution)/shard_map/all_to_all | solution.py:783
  108.6 3.1 %second_flux.1 = (f32[2,192,128]{2,1,0:T(8,128)}, f32[32,3,4,128]{3,2,1,0:T(4,128)}) custom-call(s32[8]{0:T(128)S(1)} %copy-done.12, s32[6,1,32]{2,1,0:T(1,128)S(1)} %bitcast.26, f32[2,192,128]{2,1,0:T(8,128)} %get-tuple-element.54.refs_2_, f32[2,192,128]{2,1,0:T(8,128)} %get-tuple-element.60.refs_3_, bf16[512,128]{1,0:T(8,128)(2,1)S(1)} %copy-done.1), custom_call_target="tpu_custom_call" | custom-call | tf_op jit(solution)/shard_map/second_flux/pallas_call | solution.py:684
  111.7 17.4 %all-to-all-done.4.refs_4_ = f32[32,48,128]{2,1,0:T(8,128)S(1)} async-done(((f32[32,48,128]{2,1,0:T(8,128)}), f32[32,48,128]{2,1,0:T(8,128)S(1)}, u32[]{:S(2)}, u32[]{:S(2)}) %all-to-all-start.4) | async-done | bytes 786464 | tf_op jit(solution)/shard_map/all_to_all | solution.py:783
  129.2 2.8 %middle_cot.1 = (f32[2,512,128]{2,1,0:T(8,128)S(1)}, f32[32,7,4,128]{3,2,1,0:T(4,128)S(1)}) custom-call(s32[6,1,32]{2,1,0:T(1,128)S(1)} %bitcast.27, s32[8,8]{1,0:T(8,128)S(1)} %copy-done.11, f32[2,512,128]{2,1,0:T(8,128)} %get-tuple-element.53.refs_2_, f32[2,192,128]{2,1,0:T(8,128)} %get-tuple-element.58.refs_3_, ...), custom_call_target="tpu_custom_call" | custom-call | tf_op jit(solution)/shard_map/middle_cot/pallas_call | solution.py:684
  132.0 17.7 %all_to_all.41.refs_5_.refs_4_ = f32[32,7,4,128]{3,2,1,0:T(4,128)S(1)} all-to-all(f32[32,7,4,128]{3,2,1,0:T(4,128)S(1)} %get-tuple-element.63), channel_id=1, replica_groups=mesh['blk'=32] {'blk'}, dimensions={0} | all-to-all | bytes 917504 | tf_op jit(solution)/shard_map/all_to_all | solution.py:783
  149.6 4.5 %upward_first.1 = (f32[2,512,128]{2,1,0:T(8,128)}, f32[2,192,128]{2,1,0:T(8,128)}, f32[32,3,4,128]{3,2,1,0:T(4,128)}) custom-call(s32[8]{0:T(128)S(1)} %copy-done.12, s32[384]{0:T(512)S(1)} %reshape.32.refs_2_.refs_1_, s32[32]{0:T(128)S(1)} %bitcast.32, s32[8,8]{1,0:T(8,128)S(1)} %copy-done.11, f32[2,512,128]{2,1,0:T(8,128)S(1)} %get-tuple-element.62.refs_4_, ...), custom_call_target="tpu_custom_call" | custom-call | tf_op jit(solution)/shard_map/upward_first/pallas_call | solution.py:684
  154.1 2.6 %all-to-all-start.6 = ((f32[32,3,4,128]{3,2,1,0:T(4,128)}), f32[32,3,4,128]{3,2,1,0:T(4,128)S(1)}, u32[]{:S(2)}, u32[]{:S(2)}) async-start(f32[32,3,4,128]{3,2,1,0:T(4,128)} %get-tuple-element.67), calls=%async_computation.6 | async-start | bytes 393216 | tf_op jit(solution)/shard_map/all_to_all | solution.py:783
  156.7 0.0 copy-start.7
  156.8 0.0 copy-start.8
  156.8 5.1 %second_update.1 = (f32[512,256]{1,0:T(8,128)}, f32[256,128]{1,0:T(8,128)S(1)}) custom-call(s32[8]{0:T(128)S(1)} %copy-done.12, s32[384]{0:T(512)S(1)} %reshape.32.refs_2_.refs_1_, f32[2,512,128]{2,1,0:T(8,128)} %get-tuple-element.68.refs_2_, f32[2,192,128]{2,1,0:T(8,128)} %get-tuple-element.69.refs_3_, f32[32,7,4,128]{3,2,1,0:T(4,128)S(1)} %all_to_all.41.refs_5_.refs_4_, ...), custom_call_target="tpu_custom_call" | custom-call | tf_op jit(solution)/shard_map/second_update/pallas_call | solution.py:684
  161.8 3.9 %all-to-all-done.6.refs_7_ = f32[32,3,4,128]{3,2,1,0:T(4,128)S(1)} async-done(((f32[32,3,4,128]{3,2,1,0:T(4,128)}), f32[32,3,4,128]{3,2,1,0:T(4,128)S(1)}, u32[]{:S(2)}, u32[]{:S(2)}) %all-to-all-start.6) | async-done | bytes 196640 | tf_op jit(solution)/shard_map/all_to_all | solution.py:783
  165.7 0.0 copy-done.7
  165.7 0.0 copy-done.8
  165.7 4.3 %first_pull.1 = (f32[2,192,128]{2,1,0:T(8,128)}, f32[32,64,128]{2,1,0:T(8,128)}) custom-call(s32[8]{0:T(128)S(1)} %copy-done.12, s32[6,1,32]{2,1,0:T(1,128)S(1)} %bitcast.28, s32[384]{0:T(512)S(1)} %reshape.32.refs_2_.refs_1_, s32[32]{0:T(128)S(1)} %bitcast.33, f32[2,192,128]{2,1,0:T(8,128)S(1)} %copy-done.2, f32[2,192,128]{2,1,0:T(8,128)S(1)} %copy-done.7, ...), custom_call_target="tpu_custom_call" | custom-call | tf_op jit(solution)/shard_map/first_pull/pallas_call | solution.py:684
  170.0 2.7 %all-to-all-start.7 = ((f32[32,64,128]{2,1,0:T(8,128)}), f32[32,64,128]{2,1,0:T(8,128)S(1)}, u32[]{:S(2)}, u32[]{:S(2)}) async-start(f32[32,64,128]{2,1,0:T(8,128)} %get-tuple-element.72), calls=%async_computation.7 | async-start | bytes 2097152 | tf_op jit(solution)/shard_map/all_to_all | solution.py:783
  172.7 5.8 %interior_back.1.refs_2_ = f32[2,512,128]{2,1,0:T(8,128)} custom-call(s32[8]{0:T(128)S(1)} %copy-done.12, f32[2,512,128]{2,1,0:T(8,128)} %get-tuple-element.40.refs_1_, f32[2,512,128]{2,1,0:T(8,128)} %get-tuple-element.64.refs_2_), custom_call_target="tpu_custom_call" | custom-call | tf_op jit(solution)/shard_map/interior_back/pallas_call | solution.py:684
  178.6 20.3 %all-to-all-done.7.refs_4_ = f32[32,64,128]{2,1,0:T(8,128)S(1)} async-done(((f32[32,64,128]{2,1,0:T(8,128)}), f32[32,64,128]{2,1,0:T(8,128)S(1)}, u32[]{:S(2)}, u32[]{:S(2)}) %all-to-all-start.7) | async-done | bytes 1048608 | tf_op jit(solution)/shard_map/all_to_all | solution.py:783
  198.9 3.1 %last_cot.1 = (f32[512,256]{1,0:T(8,128)}, f32[512,256]{1,0:T(8,128)}) custom-call(s32[6,1,32]{2,1,0:T(1,128)S(1)} %bitcast.29, s32[8,8]{1,0:T(8,128)S(1)} %copy-done.11, f32[2,512,128]{2,1,0:T(8,128)} %interior_back.1.refs_2_, f32[2,192,128]{2,1,0:T(8,128)} %get-tuple-element.71.refs_3_, ...), custom_call_target="tpu_custom_call", output_to_operand_aliasing={{1}: (5, {})} | custom-call | tf_op jit(solution)/shard_map/last_cot/pallas_call | solution.py:684
  (13 shorter events, 0.1 us)
Async XLA Ops:
  0.6 0.7 copy-start.6
  1.3 0.7 copy-start.10
  6.1 7.2 %copy-start.14 = (s32[8,6,4]{0,2,1:T(4,128)S(1)}, s32[8,6,4]{0,2,1:T(4,128)}, u32[]{:S(2)}) copy-start(s32[8,6,4]{0,2,1:T(4,128)} %param.14) | copy-start | bytes 2308
  6.1 33.4 %all-to-all-start = ((f32[32,64,128]{2,1,0:T(8,128)}), f32[32,64,128]{2,1,0:T(8,128)S(1)}, u32[]{:S(2)}, u32[]{:S(2)}) async-start(f32[32,64,128]{2,1,0:T(8,128)} %get-tuple-element.44), calls=%async_computation | async-start | bytes 2097152 | tf_op jit(solution)/shard_map/all_to_all | solution.py:783
  13.3 0.7 copy-start.15
  14.5 0.7 copy-start.12
  15.1 24.3 %copy-start = (bf16[128,512]{1,0:T(8,128)(2,1)S(1)}, bf16[128,512]{1,0:T(8,128)(2,1)}, u32[]{:S(2)}) copy-start(bf16[128,512]{1,0:T(8,128)(2,1)} %constant.45.clone.refs_7_.refs_6_.refs_4_.refs_10_) | copy-start | bytes 393220
  15.1 24.3 %copy-start.1 = (bf16[512,128]{1,0:T(8,128)(2,1)S(1)}, bf16[512,128]{1,0:T(8,128)(2,1)}, u32[]{:S(2)}) copy-start(bf16[512,128]{1,0:T(8,128)(2,1)} %constant.44.clone.refs_6_.refs_7_.refs_4_.refs_5_.refs_9_) | copy-start | bytes 393220
  15.1 24.3 %copy-start.2 = (f32[2,192,128]{2,1,0:T(8,128)S(1)}, f32[2,192,128]{2,1,0:T(8,128)}, u32[]{:S(2)}) copy-start(f32[2,192,128]{2,1,0:T(8,128)} %get-tuple-element.42.refs_3_.refs_4_) | copy-start | bytes 589828
  39.5 6.5 %copy-start.5 = (f32[2,512,128]{2,1,0:T(8,128)S(1)}, f32[2,512,128]{2,1,0:T(8,128)}, u32[]{:S(2)}) copy-start(f32[2,512,128]{2,1,0:T(8,128)} %get-tuple-element.47.refs_4_) | copy-start | bytes 1572868
  42.3 3.7 %copy-start.11 = (s32[8,8]{1,0:T(8,128)S(1)}, s32[8,8]{1,0:T(8,128)}, u32[]{:S(2)}) copy-start(s32[8,8]{1,0:T(8,128)} %refs_1_.7) | copy-start | bytes 772
  42.3 12.6 %all-to-all-start.1 = ((f32[32,3,4,128]{3,2,1,0:T(4,128)}), f32[32,3,4,128]{3,2,1,0:T(4,128)S(1)}, u32[]{:S(2)}, u32[]{:S(2)}) async-start(f32[32,3,4,128]{3,2,1,0:T(4,128)} %get-tuple-element.46), calls=%async_computation.1 | async-start | bytes 393216 | tf_op jit(solution)/shard_map/all_to_all | solution.py:783
  45.9 0.7 copy-start.13
  46.6 8.3 %copy-start.4 = (f32[2,512,128]{2,1,0:T(8,128)S(1)}, f32[2,512,128]{2,1,0:T(8,128)}, u32[]{:S(2)}) copy-start(f32[2,512,128]{2,1,0:T(8,128)} %get-tuple-element.41.refs_3_) | copy-start | bytes 1572868
  46.6 8.3 %copy-start.9 = (f32[2,192,128]{2,1,0:T(8,128)S(1)}, f32[2,192,128]{2,1,0:T(8,128)}, u32[]{:S(2)}) copy-start(f32[2,192,128]{2,1,0:T(8,128)} %get-tuple-element.45.refs_4_) | copy-start | bytes 589828
  77.3 23.2 %all-to-all-start.3 = ((f32[32,48,128]{2,1,0:T(8,128)}), f32[32,48,128]{2,1,0:T(8,128)S(1)}, u32[]{:S(2)}, u32[]{:S(2)}) async-start(f32[32,48,128]{2,1,0:T(8,128)} %get-tuple-element.56), calls=%async_computation.3 | async-start | bytes 1572864 | tf_op jit(solution)/shard_map/all_to_all | solution.py:783
  86.1 14.5 %copy-start.3 = (f32[2,192,128]{2,1,0:T(8,128)S(1)}, f32[2,192,128]{2,1,0:T(8,128)}, u32[]{:S(2)}) copy-start(f32[2,192,128]{2,1,0:T(8,128)} %get-tuple-element.54.refs_2_) | copy-start | bytes 589828
  105.5 23.6 %all-to-all-start.4 = ((f32[32,48,128]{2,1,0:T(8,128)}), f32[32,48,128]{2,1,0:T(8,128)S(1)}, u32[]{:S(2)}, u32[]{:S(2)}) async-start(f32[32,48,128]{2,1,0:T(8,128)} %get-tuple-element.59), calls=%async_computation.4 | async-start | bytes 1572864 | tf_op jit(solution)/shard_map/all_to_all | solution.py:783
  154.1 11.6 %all-to-all-start.6 = ((f32[32,3,4,128]{3,2,1,0:T(4,128)}), f32[32,3,4,128]{3,2,1,0:T(4,128)S(1)}, u32[]{:S(2)}, u32[]{:S(2)}) async-start(f32[32,3,4,128]{3,2,1,0:T(4,128)} %get-tuple-element.67), calls=%async_computation.6 | async-start | bytes 393216 | tf_op jit(solution)/shard_map/all_to_all | solution.py:783
  156.7 9.0 %copy-start.7 = (f32[2,192,128]{2,1,0:T(8,128)S(1)}, f32[2,192,128]{2,1,0:T(8,128)}, u32[]{:S(2)}) copy-start(f32[2,192,128]{2,1,0:T(8,128)} %get-tuple-element.65.refs_5_) | copy-start | bytes 589828
  156.8 8.9 %copy-start.8 = (f32[2,192,128]{2,1,0:T(8,128)S(1)}, f32[2,192,128]{2,1,0:T(8,128)}, u32[]{:S(2)}) copy-start(f32[2,192,128]{2,1,0:T(8,128)} %get-tuple-element.66.refs_6_) | copy-start | bytes 589828
  170.0 28.9 %all-to-all-start.7 = ((f32[32,64,128]{2,1,0:T(8,128)}), f32[32,64,128]{2,1,0:T(8,128)S(1)}, u32[]{:S(2)}, u32[]{:S(2)}) async-start(f32[32,64,128]{2,1,0:T(8,128)} %get-tuple-element.72), calls=%async_computation.7 | async-start | bytes 2097152 | tf_op jit(solution)/shard_map/all_to_all | solution.py:783
